TPU v7x, 128 devices: a whole 4x4x4 slice. The times are simulated.
128 devices in a mesh: neg: 16 (over x, y), qry: 8 (over z, core).
Axes of the slice: x: 4, y: 4, z: 4, core: 2. Of those that a mesh axis runs over, the one named last changes fastest.
Arguments:
- items_table: bfloat16 [131072, 512], P('neg'), may hold values from -6 to 6
- fetch_rows: int32 [2048, 640], P(('neg', 'qry')), may hold values from 0 to 8191, as said below
- neighbour_slots: int32 [65536, 40], P(('neg', 'qry')), may hold values from 0 to 10239, as said below
- neighbour_count: int32 [65536], P(('neg', 'qry')), may hold values from 20 to 40
- self_slot: int32 [65536], P(('neg', 'qry')), may hold values from 0 to 10239
- negative_count: int32 [65536], P('neg'), may hold values from 1 to 999
- message_weight: bfloat16 [512, 512], replicated, may hold values from -0.25 to 0.25
- message_bias: float32 [512], replicated, may hold values from -3 to 3
- self_weight: bfloat16 [512, 512], replicated, may hold values from -0.25 to 0.25
- neighbour_weight: bfloat16 [512, 512], replicated, may hold values from -0.25 to 0.25
- output_bias: float32 [512], replicated, may hold values from -3 to 3
- queries: bfloat16 [8192, 512], P('qry'), may hold values from -8 to 8
Outputs:
- negative_embed: bfloat16 [65536, 512], P(('neg', 'qry'))
- query_lse: float32 [8192], P('qry')
Inputs may be any that keep to these rules, and one draw needn't show every extreme that they name: Within one row of fetch_rows (one device's list for one partition) no item appears twice. `neighbour_slots`: every one of a device's 16 * 640 fetched rows is named by at least one live neighbour of that device's negatives.
All inputs are finite; a program needn't handle non-finite values.
Results may differ from a plain program's by a relative error of at most 0.0055.
Values may be sent and summed in bfloat16 or wider, within the bound.
No kernel may reach another device: no remote copies, remote signals or barrier semaphores. Data moves between devices by JAX's collectives and lax.ppermute only.
A program may use at most 128 MiB of HBM per device.

v0:
```python
import math

import jax
import jax.numpy as jnp
from jax import lax
from jax.experimental import pallas as pl
from jax.experimental.pallas import tpu as pltpu
from jax.sharding import PartitionSpec as P


LANES = 128
DEAD = 2**31 - 1
CHUNK = 128
STRIDE = 132
BLOCK = 10
STAGE = 1024
DEEP = 4
SIDE = 4
SCORED = 256
MESSAGES = 2 * SIDE


def compose_kernel(slots_ref, self_ref, count_ref, fetch_ref, keys_ref):
    neighbours, negatives = slots_ref.shape
    parts, per_part = fetch_ref.shape
    per_line = per_part // LANES
    half = parts // 2
    packed = fetch_ref[:half, :] | (fetch_ref[half:, :] << 13)
    lines = [
        jnp.broadcast_to(packed[p : p + 1, j * LANES : (j + 1) * LANES], (8, LANES))
        for p in range(half)
        for j in range(per_line)
    ]

    def located(slot):
        hi = slot >> 7
        lo = slot & 127
        upper = hi >= len(lines)
        folded = jnp.where(upper, hi - len(lines), hi)
        found = jnp.zeros_like(slot)
        for h, line in enumerate(lines):
            at = jnp.take_along_axis(line, lo, axis=1, mode="promise_in_bounds")
            found = jnp.where(folded == h, at, found)
        row = jnp.where(upper, found >> 13, found & 8191)
        return ((((hi * 205) >> 10) - 8) << 28) | row

    sublane = lax.broadcasted_iota(jnp.int32, (8, LANES), 0)
    lane = lax.broadcasted_iota(jnp.int32, (8, LANES), 1)
    for j in range(negatives // LANES):
        cols = slice(j * LANES, (j + 1) * LANES)
        count = jnp.broadcast_to(count_ref[:, cols], (8, LANES))
        for i in range(neighbours // 8):
            key = located(slots_ref[8 * i : 8 * (i + 1), cols]) | ((lane + j * LANES) << 19)
            first = (j * (neighbours // 8) + i) * 8
            keys_ref[first : first + 8, :] = jnp.where(sublane + 8 * i < count, key, DEAD)

    def tile_of(ref):
        tiles = [ref[:, j * LANES : (j + 1) * LANES] for j in range(negatives // LANES)]
        return jnp.concatenate(tiles + [jnp.zeros((8 - len(tiles), LANES), jnp.int32)], axis=0)

    own = located(tile_of(self_ref)) | ((sublane * LANES + lane) << 19)
    own = own | ((tile_of(count_ref) - 20) << 14) | (1 << 13)
    keys_ref[neighbours * negatives // LANES :, :] = own[: negatives // LANES]


def owner_kernel(part_ref, ends_ref, lists_ref, message_hbm, self_hbm, *refs):
    outs = refs[: 2 * MESSAGES]
    table, stage, pick, rows, acc, offsets, places, ready, sems, place_sem, out_sems = refs[2 * MESSAGES :]
    items = message_hbm.shape[0]
    width = message_hbm.shape[1]
    tiles = width // LANES
    per_table = items // STAGE
    step = pl.program_id(0)
    devices = pl.num_programs(0)
    part = part_ref[0] * SIDE + part_ref[1]
    negatives = pick.shape[0]
    quarter = negatives // 4

    def asker(i):
        x = (part_ref[0] + i // SIDE) % SIDE
        y = (part_ref[1] + i % SIDE) % SIDE
        return x * SIDE + y

    def range_of(r):
        return jnp.where(part == 0, 0, ends_ref[r, jnp.maximum(part - 1, 0)]), ends_ref[r, part]

    def place_copy():
        return pltpu.make_async_copy(offsets, places, place_sem)

    def place(r, base):
        for c in range(BLOCK):
            line = lists_ref[r, pl.ds(base + c, 1), :]
            offsets[c : c + 1, :] = (line & 16383) * tiles
        place_copy().start()

    def stage_copy(c):
        source = message_hbm if c < per_table else self_hbm
        return pltpu.make_async_copy(
            source.at[pl.ds((c % per_table) * STAGE, STAGE), :], stage.at[c % DEEP], sems.at[c % DEEP]
        )

    def out_copy(slot, q, array, at):
        return pltpu.make_async_copy(
            ready.at[slot, pl.ds(q * quarter, quarter), :], array.at[at], out_sems.at[slot, q]
        )

    def wait_out(slot):
        for q in range(4):
            out_copy(slot, q, outs[0], 0).wait()

    @pl.when(step == 0)
    def _():
        for c in range(DEEP):
            stage_copy(c).start()
        offsets[...] = jnp.zeros_like(offsets)
        place(asker(0), range_of(asker(0))[0] >> 7)
        rows[...] = jnp.zeros_like(rows)
        for c in range(2 * per_table):
            stage_copy(c).wait()

            def spread(i, _, c=c):
                for u in range(4):
                    at = pl.multiple_of(i * 64 + u * 16, 16)
                    block = stage[c % DEEP, pl.ds(at, 16), :].astype(jnp.float32)
                    for half in range(2):
                        for j in range(tiles):
                            first = (c * STAGE + at + half * 8) * tiles + j
                            table[pl.ds(first, 8, stride=tiles), :] = block[
                                half * 8 : half * 8 + 8, j * LANES : (j + 1) * LANES
                            ]
                return 0

            lax.fori_loop(0, STAGE // 64, spread, 0)
            if c + DEEP < 2 * per_table:
                stage_copy(c + DEEP).start()

    a = asker(step)
    start, end = range_of(a)
    row_first = start >> 7
    row_last = (end + 127) >> 7

    def picked(r):
        v = lax.broadcasted_iota(jnp.int32, (negatives, LANES), 0)
        line = lists_ref[a, pl.ds(r, 1), :]
        at = r * LANES + lax.broadcasted_iota(jnp.int32, (1, LANES), 1)
        who = jnp.where((at >= start) & (at < end), (line >> 19) & 511, -1)
        weight = jnp.where((line & 8192) != 0, ((line >> 14) & 31) + 20, 1).astype(jnp.float32)
        return jnp.where(v == who, weight, 0.0).astype(jnp.bfloat16)

    def gather(base):
        place_copy().wait()
        for c in range(BLOCK):
            r = base + c

            @pl.when(r < row_last)
            def _(c=c, r=r):
                pick[:, c * LANES : (c + 1) * LANES] = picked(r)
                for e in range(CHUNK):
                    at = pl.multiple_of(places[c, e], tiles)
                    rows[c, pl.ds(e, tiles, stride=STRIDE), :] = table[pl.ds(at, tiles), :]

            @pl.when(r >= row_last)
            def _(c=c):
                pick[:, c * LANES : (c + 1) * LANES] = jnp.zeros((negatives, LANES), jnp.bfloat16)

    def gather_more(base):
        place_copy().wait()

        def chunk(c, _):
            cols = pl.ds(pl.multiple_of(c * LANES, LANES), LANES)
            live = base + c < row_last
            pick[:, cols] = jnp.where(live, picked(base + c), 0).astype(jnp.bfloat16)

            def entry(e, _):
                at = pl.multiple_of(places[c, e], tiles)
                rows[c, pl.ds(e, tiles, stride=STRIDE), :] = table[pl.ds(at, tiles), :]
                return 0

            return lax.fori_loop(0, CHUNK, entry, 0)

        lax.fori_loop(0, BLOCK, chunk, 0)

    def summed():
        gathered = jnp.concatenate(
            [
                jnp.concatenate(
                    [rows[c, j * STRIDE : j * STRIDE + CHUNK, :].astype(jnp.bfloat16) for j in range(tiles)],
                    axis=1,
                )
                for c in range(BLOCK)
            ],
            axis=0,
        )
        return jnp.dot(pick[...], gathered, preferred_element_type=jnp.float32)

    gather(row_first)
    blocks = (row_last - row_first + BLOCK - 1) // BLOCK

    @pl.when((blocks <= 1) & (step + 1 < devices))
    def _():
        following = asker(step + 1)
        place(following, range_of(following)[0] >> 7)

    acc[...] = summed()

    @pl.when(blocks > 1)
    def _():
        def more(i, _):
            place(a, row_first + i * BLOCK)
            gather_more(row_first + i * BLOCK)
            acc[...] += summed()
            return 0

        lax.fori_loop(1, blocks, more, 0)

        @pl.when(step + 1 < devices)
        def _():
            following = asker(step + 1)
            place(following, range_of(following)[0] >> 7)

    slot = step % 2

    @pl.when(step >= 2)
    def _():
        wait_out(slot)

    ready[slot] = acc[...].astype(jnp.bfloat16)
    dx = step // SIDE
    dy = step % SIDE
    for d in range(SIDE):

        @pl.when(dx == d)
        def _(d=d):
            for h in range(2):
                out_copy(slot, h, outs[2 * d + h], dy).start()

        @pl.when(dy == d)
        def _(d=d):
            for h in range(2):
                out_copy(slot, 2 + h, outs[MESSAGES + 2 * d + h], dx).start()

    @pl.when(step + 1 == devices)
    def _():
        wait_out(slot)
        wait_out(1 - slot)


def from_everyone(x, axis):
    devices = lax.axis_size(axis)
    return lax.all_to_all(jnp.broadcast_to(x[None], (devices, *x.shape)), axis, 0, 0, tiled=True)


def composed_keys(neighbour_slots, self_slot, neighbour_count, fetch_rows):
    negatives, neighbours = neighbour_slots.shape
    folded = negatives // LANES
    return pl.pallas_call(
        compose_kernel,
        out_shape=jax.ShapeDtypeStruct(((neighbours + 1) * folded, LANES), jnp.int32),
        name="compose",
    )(
        neighbour_slots.T,
        self_slot[None, :],
        neighbour_count[None, :],
        fetch_rows,
    )


def owner_sums(part, ends, lists, message_part, self_part, negatives):
    devices, _, _ = lists.shape
    items, width = message_part.shape
    tiles = width // LANES
    quarter = [jax.ShapeDtypeStruct((SIDE, negatives // 4, width), jnp.bfloat16)]
    return pl.pallas_call(
        owner_kernel,
        grid=(devices,),
        in_specs=[
            pl.BlockSpec(memory_space=pltpu.SMEM),
            pl.BlockSpec(memory_space=pltpu.SMEM),
            pl.BlockSpec(memory_space=pltpu.VMEM),
            pl.BlockSpec(memory_space=pl.ANY),
            pl.BlockSpec(memory_space=pl.ANY),
        ],
        out_specs=[pl.BlockSpec(memory_space=pl.ANY)] * (2 * MESSAGES),
        out_shape=quarter * (2 * MESSAGES),
        scratch_shapes=[
            pltpu.VMEM((2 * items * tiles, LANES), jnp.float32),
            pltpu.VMEM((DEEP, STAGE, width), jnp.bfloat16),
            pltpu.VMEM((negatives, BLOCK * CHUNK), jnp.bfloat16),
            pltpu.VMEM((BLOCK, tiles * STRIDE, LANES), jnp.float32),
            pltpu.VMEM((negatives, width), jnp.float32),
            pltpu.VMEM((16, LANES), jnp.int32),
            pltpu.SMEM((16, LANES), jnp.int32),
            pltpu.VMEM((2, negatives, width), jnp.bfloat16),
            pltpu.SemaphoreType.DMA((DEEP,)),
            pltpu.SemaphoreType.DMA,
            pltpu.SemaphoreType.DMA((2, 4)),
        ],
        compiler_params=pltpu.CompilerParams(
            dimension_semantics=("arbitrary",), vmem_limit_bytes=60 * 2**20
        ),
        name="owner",
    )(part, ends, lists, message_part, self_part)


def moved(x, along, by):
    def place(i):
        x_at, y_at = divmod(i, SIDE)
        if along == "x":
            return (x_at + by) % SIDE * SIDE + y_at
        return x_at * SIDE + (y_at + by) % SIDE

    return lax.ppermute(x, "neg", [(i, place(i)) for i in range(SIDE * SIDE)])


def joined(*parts):
    return sum(p.astype(jnp.float32) for p in parts)


def ring_sums(parts, along):
    far_up = moved(parts[2][0], along, 1)
    far_down = moved(parts[2][1], along, -1)
    near_up = moved(parts[1][1], along, 1)
    near_down = moved(parts[3][0], along, -1)
    sent_up = moved(joined(parts[1][0], far_up).astype(jnp.bfloat16), along, 1)
    sent_down = moved(joined(parts[3][1], far_down).astype(jnp.bfloat16), along, -1)
    return joined(parts[0][0], sent_up, near_down), joined(parts[0][1], near_up, sent_down)


def joint_sums(own_first, own_second, up, down, next_up, next_down, along):
    half = up.shape[0] // 2
    came_up = moved(up, along, 1)
    came_down = moved(down, along, -1)
    sent_up = moved(joined(next_up, came_up[:half]).astype(jnp.bfloat16), along, 1)
    sent_down = moved(joined(next_down, came_down[:half]).astype(jnp.bfloat16), along, -1)
    return joined(own_first, sent_up, came_down[half:]), joined(own_second, came_up[half:], sent_down)


def scattered_sums(outs):
    result = []
    for at, order in ((0, "xy"), (MESSAGES, "yx")):
        parts = [outs[at + 2 * d : at + 2 * d + 2] for d in range(SIDE)]
        first, second = ring_sums(parts, order[0])
        low_first, low_second = first.astype(jnp.bfloat16), second.astype(jnp.bfloat16)
        up = jnp.concatenate([low_first[2:3], low_second[1:2]], axis=0)
        down = jnp.concatenate([low_second[2:3], low_first[3:4]], axis=0)
        result += joint_sums(first[0:1], second[0:1], up, down, low_first[1:2], low_second[3:4], order[1])
    return result


def turned(x, deep, other):
    def place(i):
        z, core = divmod(i, 2)
        return (z + deep) % SIDE * 2 + (1 - core if other else core)

    return lax.ppermute(x, "qry", [(i, place(i)) for i in range(2 * SIDE)])


def all_queries(queries):
    up = turned(queries, 1, False)
    down = turned(queries, -1, False)
    other = turned(queries, 0, True)
    far = turned(up, 1, False)
    other_up = turned(up, 0, True)
    other_down = turned(down, 0, True)
    other_far = turned(far, 0, True)
    return [queries, up, far, down, other, other_up, other_far, other_down]


def table_kernel(items_ref, message_ref, bias_ref, neighbour_ref, self_ref, message_out, self_out):
    f32 = jnp.float32
    items = items_ref[...]
    message = jnp.dot(items, message_ref[...], preferred_element_type=f32) + bias_ref[...]
    message = jnp.maximum(message, 0.0).astype(jnp.bfloat16)
    message_out[...] = jnp.dot(message, neighbour_ref[...], preferred_element_type=f32).astype(jnp.bfloat16)
    self_out[...] = jnp.dot(items, self_ref[...], preferred_element_type=f32).astype(jnp.bfloat16)


def tables(items_table, message_weight, message_bias, neighbour_weight, self_weight):
    items, width = items_table.shape
    weight = pl.BlockSpec((width, width), lambda i: (0, 0))
    block = pl.BlockSpec((STAGE, width), lambda i: (i, 0))
    return pl.pallas_call(
        table_kernel,
        grid=(items // STAGE,),
        in_specs=[block, weight, pl.BlockSpec((1, width), lambda i: (0, 0)), weight, weight],
        out_specs=[block, block],
        out_shape=[jax.ShapeDtypeStruct((items, width), jnp.bfloat16)] * 2,
        compiler_params=pltpu.CompilerParams(dimension_semantics=("arbitrary",)),
        name="tables",
    )(items_table, message_weight, message_bias[None, :], neighbour_weight, self_weight)


def score_kernel(*refs):
    sums = refs[:4]
    count_ref, bias_ref, log_ref = refs[4:7]
    queries = refs[7 : 7 + 2 * SIDE]
    embed_ref, lse_ref, held, sems = refs[7 + 2 * SIDE :]
    f32 = jnp.float32
    rows = queries[0].shape[0]

    def copy(j, source):
        return pltpu.make_async_copy(source, held.at[pl.ds(j * rows, rows), :], sems.at[j])

    for j, source in enumerate(queries):
        copy(j, source).start()
    quarter = embed_ref.shape[0] // 4
    for q in range(4):
        at = slice(q * quarter, (q + 1) * quarter)
        hidden = jnp.maximum(sums[q][...] / count_ref[at, :] + bias_ref[...], 0.0)
        scale_inv = lax.rsqrt(jnp.mean(hidden * hidden, axis=-1, keepdims=True) + 0.25)
        embed_ref[at, :] = (hidden * scale_inv).astype(jnp.bfloat16)

    def block(j, _):
        copy(j, queries[0]).wait()

        def pair(i, _):
            first = j * rows + i * 2 * SCORED
            for u in range(2):
                at = pl.multiple_of(first + u * SCORED, SCORED)
                scores = lax.dot_general(
                    embed_ref[...], held[pl.ds(at, SCORED), :], (((1,), (1,)), ((), ())), preferred_element_type=f32
                )
                scores = 0.25 * scores - log_ref[...]
                peak = jnp.max(scores, axis=0, keepdims=True)
                total = jnp.sum(jnp.exp(scores - peak), axis=0, keepdims=True)
                lse_ref[pl.ds(at // SCORED, 1), :] = peak + jnp.log(total)
            return 0

        return lax.fori_loop(0, rows // (2 * SCORED), pair, 0)

    lax.fori_loop(0, len(queries), block, 0)


def scored(sums, count, bias, log_count, queries):
    negatives = count.shape[0]
    rows, width = queries[0].shape
    total = rows * len(queries)
    in_vmem = pl.BlockSpec(memory_space=pltpu.VMEM)
    return pl.pallas_call(
        score_kernel,
        in_specs=[in_vmem] * 7 + [pl.BlockSpec(memory_space=pl.ANY)] * len(queries),
        out_specs=[in_vmem] * 2,
        out_shape=[
            jax.ShapeDtypeStruct((negatives, width), jnp.bfloat16),
            jax.ShapeDtypeStruct((total // SCORED, SCORED), jnp.float32),
        ],
        scratch_shapes=[
            pltpu.VMEM((total, width), jnp.bfloat16),
            pltpu.SemaphoreType.DMA((len(queries),)),
        ],
        name="score",
    )(*sums, count[:, None], bias[None, :], log_count[:, None], *queries)


def per_device(
    items_table,
    fetch_rows,
    neighbour_slots,
    neighbour_count,
    self_slot,
    negative_count,
    message_weight,
    message_bias,
    self_weight,
    neighbour_weight,
    output_bias,
    queries,
):
    f32 = jnp.float32
    negatives = neighbour_count.shape[0]
    parts = lax.axis_size("neg")
    groups = lax.axis_size("qry")
    query_blocks = all_queries(queries)

    keys = composed_keys(neighbour_slots, self_slot, neighbour_count, fetch_rows).reshape(-1)
    bounds = jnp.array([min((p + 1 - 8) << 28, DEAD) for p in range(parts)], jnp.int32)
    ends = jnp.sum((keys[None, :] < bounds[:, None]).astype(jnp.int32), axis=1)
    lines = jnp.concatenate([lax.sort(keys, is_stable=False), ends, jnp.zeros((184 * LANES - keys.size - parts,), jnp.int32)])
    lists = from_everyone(lines.reshape(184, LANES), "neg")

    message_part, self_part = tables(items_table, message_weight, message_bias, neighbour_weight, self_weight)

    place = lax.axis_index("neg")
    part = jnp.stack([place // SIDE, place % SIDE]).astype(jnp.int32)
    outs = owner_sums(part, lists[:, keys.size // LANES, :parts], lists, message_part, self_part, negatives)
    sums = [q[0] for q in scattered_sums(outs)]

    own_count = lax.dynamic_slice(negative_count, (lax.axis_index("qry") * negatives,), (negatives,))
    log_count = jnp.log(own_count.astype(f32))
    negative_embed, part_lse = scored(sums, neighbour_count.astype(f32), output_bias, log_count, query_blocks)
    here = lax.axis_index("qry")
    z, core = here // 2, here % 2
    group = jnp.arange(groups)
    source = ((z - group // 2) % SIDE) + SIDE * ((group % 2) ^ core)
    picked = source[:, None] == group[None, :]
    blocks = part_lse.reshape(groups, -1)
    blocks = jnp.sum(jnp.where(picked[:, :, None], blocks[None], 0.0), axis=1)
    shared = jnp.broadcast_to(blocks[None], (parts, groups, queries.shape[0]))
    parts_lse = lax.all_to_all(
        shared.reshape(parts * groups, -1), ("neg", "qry"), split_axis=0, concat_axis=0, tiled=True
    )
    top = jnp.max(parts_lse, axis=0)
    query_lse = top + jnp.log(jnp.sum(jnp.exp(parts_lse - top[None, :]), axis=0))
    return (negative_embed, query_lse - math.log(negatives * parts * groups))


def solution(mesh):
    in_specs = (
        P("neg", None),
        P(("neg", "qry"), None),
        P(("neg", "qry"), None),
        P(("neg", "qry")),
        P(("neg", "qry")),
        P("neg"),
        P(),
        P(),
        P(),
        P(),
        P(),
        P("qry", None),
    )
    out_specs = (P(("neg", "qry"), None), P("qry"))

    return jax.shard_map(per_device, mesh=mesh, in_specs=in_specs, out_specs=out_specs, check_vma=False)
```

profile of v0, /device:TPU:1, one launch (start us, length us, event | category | flops | bytes accessed | tf_op | source)
XLA Modules:
  0.0 227.6 jit_solution(2927374092974879668)
XLA Ops:
  0.6 2.6 %compose.1 = s32[164,128]{1,0:T(8,128)} custom-call(s32[40,512]{1,0:T(8,128)} %bitcast.29, s32[1,512]{1,0:T(1,128)} %bitcast.34, s32[1,512]{1,0:T(1,128)} %bitcast.33, s32[16,640]{1,0:T(8,128)} %fetch_ref.1), custom_call_target="tpu_custom_call" | custom-call | tf_op jit(solution)/shard_map/compose/pallas_call | solution.py:256
  3.2 9.3 %sort.7 = s32[20992]{0:T(1024)S(1)} sort(s32[20992]{0:T(1024)} %bitcast.26), dimensions={0}, to_apply=%region_0.0 | sort | flops 314880 | bytes 167936 | tf_op jit(solution)/shard_map/sort | solution.py:478
  12.5 1.2 convert_reduce_fusion
  13.8 1.3 broadcast_in_dim.65
  15.1 7.6 %all-to-all-start = ((s32[16,184,128]{2,1,0:T(8,128)}), s32[16,184,128]{2,1,0:T(8,128)S(1)}, u32[]{:S(2)}, u32[]{:S(2)}) async-start(s32[16,184,128]{2,1,0:T(8,128)} %broadcast_in_dim.65), calls=%async_computation | async-start | bytes 3014656 | tf_op jit(solution)/shard_map/all_to_all | solution.py:250
  22.7 17.2 %tables.1 = (bf16[8192,512]{1,0:T(8,128)(2,1)}, bf16[8192,512]{1,0:T(8,128)(2,1)}) custom-call(bf16[8192,512]{1,0:T(8,128)(2,1)} %items_ref.1, bf16[512,512]{1,0:T(8,128)(2,1)} %message_ref.1, f32[1,512]{1,0:T(1,128)} %bitcast.35, bf16[512,512]{1,0:T(8,128)(2,1)} %neighbour_ref.1, bf16[512,512]{1,0:T(8,128)(2,1)} %self_ref.1), custom_call_target="tpu_custom_call" | custom-call | tf_op jit(solution)/shard_map/tables/pallas_call | solution.py:382
  39.9 0.6 pad_add_fusion.part_ref
  40.5 2.2 all-to-all-done.lists_ref
  42.7 0.6 slice.100
  43.3 0.5 copy-done
  43.9 42.8 %owner.1 = (bf16[4,128,512]{2,1,0:T(8,128)(2,1)}, bf16[4,128,512]{2,1,0:T(8,128)(2,1)}, bf16[4,128,512]{2,1,0:T(8,128)(2,1)}, bf16[4,128,512]{2,1,0:T(8,128)(2,1...) custom-call(s32[2]{0:T(128)} %pad_add_fusion.part_ref, ...), custom_call_target="tpu_custom_call" | custom-call | tf_op jit(solution)/shard_map/owner/pallas_call | solution.py:273
  86.7 2.6 %collective-permute-start.14 = (bf16[4,128,512]{2,1,0:T(8,128)(2,1)}, bf16[4,128,512]{2,1,0:T(8,128)(2,1)S(1)}, u32[]{:S(2)}, u32[]{:S(2)}) collective-permute-start(bf16[4,128,512]{2,1,0:T(8,128)(2,1)} %get-tuple-element.39), channel_id=1, source_target_pairs={{0,24},{8,0},{16,8},{24,16},{32,56},{40,32},{48,40},{56,48},{64,88... | collective-permute-start | bytes 1572872 | tf_op jit(solution)/shard_map/ppermute | solution.py:312
  89.3 1.7 collective-permute-start.20
  91.1 0.5 collective-permute-start.13
  91.7 2.2 collective-permute-start.12
  93.9 5.1 %collective-permute-done.14 = bf16[4,128,512]{2,1,0:T(8,128)(2,1)S(1)} collective-permute-done((bf16[4,128,512]{2,1,0:T(8,128)(2,1)}, bf16[4,128,512]{2,1,0:T(8,128)(2,1)S(1)}, u32[]{:S(2)}, u32[]{:S(2)}) %collective-permute-start.14) | collective-permute-done | bytes 524320 | tf_op jit(solution)/shard_map/ppermute | solution.py:312
  99.0 1.7 collective-permute-start.4
  100.7 1.2 add_convert_fusion
  101.9 1.2 collective-permute-done.10
  103.2 2.1 collective-permute-start
  105.4 2.2 collective-permute-done.4
  107.6 3.6 %collective-permute-start.15 = (bf16[4,128,512]{2,1,0:T(8,128)(2,1)S(1)}, bf16[4,128,512]{2,1,0:T(8,128)(2,1)S(1)}, u32[]{:S(2)}, u32[]{:S(2)}) collective-permute-start(bf16[4,128,512]{2,1,0:T(8,128)(2,1)S(1)} %add_convert_fusion), channel_id=1, source_target_pairs={{0,24},{8,0},{16,8},{24,16},{32,56},{40,32},{48,40},{56,48},{64,88... | collective-permute-start | bytes 1572872 | tf_op jit(solution)/shard_map/ppermute | solution.py:312
  111.4 1.4 collective-permute-done
  112.9 1.4 collective-permute-done.13
  114.4 2.1 collective-permute-start.3
  116.5 1.8 collective-permute-done.15
  118.3 2.4 %collective-permute-start.2 = (bf16[4,128,512]{2,1,0:T(8,128)(2,1)S(1)}, bf16[4,128,512]{2,1,0:T(8,128)(2,1)S(1)}, u32[]{:S(2)}, u32[]{:S(2)}) collective-permute-start(bf16[4,128,512]{2,1,0:T(8,128)(2,1)S(1)} %copy-done.13), channel_id=1, source_target_pairs={{0,96},{8,104},{16,112},{24,120},{32,0},{40,8},{48,16},{56,24},{64... | collective-permute-start | bytes 1572872 | tf_op jit(solution)/shard_map/ppermute | solution.py:312
  121.4 1.6 collective-permute-done.11
  123.0 1.8 collective-permute-start.1
  125.1 0.8 pad_maximum_fusion.2
  125.9 1.9 collective-permute-start.22
  127.8 9.3 %collective-permute-done.5 = bf16[4,128,512]{2,1,0:T(8,128)(2,1)S(1)} collective-permute-done((bf16[4,128,512]{2,1,0:T(8,128)(2,1)S(1)}, bf16[4,128,512]{2,1,0:T(8,128)(2,1)S(1)}, u32[]{:S(2)}, u32[]{:S(2)}) %collective-permute-start.5) | collective-permute-done | bytes 524320 | tf_op jit(solution)/shard_map/ppermute | solution.py:312
  137.0 1.7 collective-permute-start.16
  138.8 1.2 fusion.18
  140.0 1.4 collective-permute-start.18
  141.7 0.8 copy-done.3
  142.5 0.7 pad_maximum_fusion
  143.2 1.6 collective-permute-start.6
  144.8 0.7 pad_maximum_fusion.1
  145.6 1.0 collective-permute-done.18
  146.5 3.3 %collective-permute-start.8 = (bf16[2,128,512]{2,1,0:T(8,128)(2,1)}, bf16[2,128,512]{2,1,0:T(8,128)(2,1)}, u32[]{:S(2)}, u32[]{:S(2)}) collective-permute-start(bf16[2,128,512]{2,1,0:T(8,128)(2,1)} %pad_maximum_fusion.1), channel_id=1, source_target_pairs={{0,24},{8,0},{16,8},{24,16},{32,56},{40,32},{48,40},{56,48},{64,88... | collective-permute-start | bytes 786440 | tf_op jit(solution)/shard_map/ppermute | solution.py:312
  149.9 0.8 convert_log_fusion
  150.6 0.9 copy.20.refs_6_
  151.5 0.9 copy.19.refs_4_
  152.3 0.9 add_convert_fusion.4
  153.3 8.2 %collective-permute-start.23 = (bf16[1024,512]{1,0:T(8,128)(2,1)}, bf16[1024,512]{1,0:T(8,128)(2,1)}, u32[]{:S(2)}, u32[]{:S(2)}) collective-permute-start(bf16[1024,512]{1,0:T(8,128)(2,1)} %refs_7_.1), channel_id=1, source_target_pairs={{0,1},{1,0},{2,3},{3,2},{4,5},{5,4},{6,7},{7,6},{8,9},{9,8},{10,11... | collective-permute-start | bytes 3145736 | tf_op jit(solution)/shard_map/ppermute | solution.py:355
  161.6 0.4 collective-permute-start.26
  162.1 3.4 %collective-permute-start.19 = (bf16[1,128,512]{2,1,0:T(8,128)(2,1)S(1)}, bf16[1,128,512]{2,1,0:T(8,128)(2,1)S(1)}, u32[]{:S(2)}, u32[]{:S(2)}) collective-permute-start(bf16[1,128,512]{2,1,0:T(8,128)(2,1)S(1)} %add_convert_fusion.4), channel_id=1, source_target_pairs={{0,96},{8,104},{16,112},{24,120},{32,0},{40,8},{48,16},{56,24},{64... | collective-permute-start | bytes 393224 | tf_op jit(solution)/shard_map/ppermute | solution.py:312
  165.5 1.0 add_convert_fusion.6
  166.6 1.4 collective-permute-done.19
  168.0 1.8 fusion.3
  169.8 2.0 collective-permute-done.9
  171.8 0.9 collective-permute-start.17
  172.8 1.9 fusion.7
  174.6 2.9 %collective-permute-done.17 = bf16[1,128,512]{2,1,0:T(8,128)(2,1)S(1)} collective-permute-done((bf16[1,128,512]{2,1,0:T(8,128)(2,1)S(1)}, bf16[1,128,512]{2,1,0:T(8,128)(2,1)S(1)}, u32[]{:S(2)}, u32[]{:S(2)}) %collective-permute-start.17) | collective-permute-done | bytes 131104 | tf_op jit(solution)/shard_map/ppermute | solution.py:312
  177.6 0.8 fusion.5.refs_2_
  178.4 4.3 %collective-permute-done.7 = bf16[1,128,512]{2,1,0:T(8,128)(2,1)S(1)} collective-permute-done((bf16[1,128,512]{2,1,0:T(8,128)(2,1)S(1)}, bf16[1,128,512]{2,1,0:T(8,128)(2,1)S(1)}, u32[]{:S(2)}, u32[]{:S(2)}) %collective-permute-start.7) | collective-permute-done | bytes 131104 | tf_op jit(solution)/shard_map/ppermute | solution.py:312
  182.6 1.7 fusion.9.refs_0_
  184.3 14.4 %score.1 = (bf16[512,512]{1,0:T(8,128)(2,1)}, f32[32,256]{1,0:T(8,128)}) custom-call(f32[128,512]{1,0:T(8,128)} %fusion.9.refs_0_, f32[128,512]{1,0:T(8,128)} %get-tuple-element.60.refs_1_, f32[128,512]{1,0:T(8,128)} %fusion.5.refs_2_, f32[128,512]{1,0:T(8,128)} %get-tuple-element.58.refs_3_, f32[512,1]{1,0:T(8,128)} %copy.19.refs_4_, f32[1,512]{1,0:T(1,128)} %bitcast.36, ...), custom_call_target="tpu_custom_call" | custom-call | tf_op jit(solution)/shard_map/score/pallas_call | solution.py:439
  198.7 0.8 broadcast_in_dim.71
  199.7 0.6 all_to_all.12
  200.3 26.2 %all_to_all.17 = f32[128,1,1024]{2,1,0:T(1,128)S(1)} all-to-all(f32[128,1,1024]{2,1,0:T(1,128)S(1)} %all_to_all.12), channel_id=1, replica_groups=mesh['neg'=16,'qry'=8] {'neg','qry'}, dimensions={0} | all-to-all | bytes 1048576 | tf_op jit(solution)/shard_map/all_to_all | solution.py:499
  226.5 0.3 reduce_max.9
  227.0 0.6 add_add_fusion
  (69 shorter events, 2.4 us)
Async XLA Ops:
  15.1 27.6 %all-to-all-start = ((s32[16,184,128]{2,1,0:T(8,128)}), s32[16,184,128]{2,1,0:T(8,128)S(1)}, u32[]{:S(2)}, u32[]{:S(2)}) async-start(s32[16,184,128]{2,1,0:T(8,128)} %broadcast_in_dim.65), calls=%async_computation | async-start | bytes 3014656 | tf_op jit(solution)/shard_map/all_to_all | solution.py:250
  42.7 1.2 copy-start
  86.7 16.5 %copy-start.15 = (bf16[4,128,512]{2,1,0:T(8,128)(2,1)S(1)}, bf16[4,128,512]{2,1,0:T(8,128)(2,1)}, u32[]{:S(2)}) copy-start(bf16[4,128,512]{2,1,0:T(8,128)(2,1)} %get-tuple-element.26) | copy-start | bytes 1572868
  86.7 18.6 %copy-start.7 = (bf16[4,128,512]{2,1,0:T(8,128)(2,1)S(1)}, bf16[4,128,512]{2,1,0:T(8,128)(2,1)}, u32[]{:S(2)}) copy-start(bf16[4,128,512]{2,1,0:T(8,128)(2,1)} %get-tuple-element.33) | copy-start | bytes 1572868
  86.7 12.3 %collective-permute-start.14 = (bf16[4,128,512]{2,1,0:T(8,128)(2,1)}, bf16[4,128,512]{2,1,0:T(8,128)(2,1)S(1)}, u32[]{:S(2)}, u32[]{:S(2)}) collective-permute-start(bf16[4,128,512]{2,1,0:T(8,128)(2,1)} %get-tuple-element.39), channel_id=1, source_target_pairs={{0,24},{8,0},{16,8},{24,16},{32,56},{40,32},{48,40},{56,48},{64,88... | collective-permute-start | bytes 1572872 | tf_op jit(solution)/shard_map/ppermute | solution.py:312
  89.3 36.5 %collective-permute-start.20 = (bf16[1024,512]{1,0:T(8,128)(2,1)}, bf16[1024,512]{1,0:T(8,128)(2,1)}, u32[]{:S(2)}, u32[]{:S(2)}) collective-permute-start(bf16[1024,512]{1,0:T(8,128)(2,1)} %refs_7_.1), channel_id=1, source_target_pairs={{0,2},{1,3},{2,4},{3,5},{4,6},{5,7},{6,0},{7,1},{8,10},{9,11},{10,... | collective-permute-start | bytes 3145736 | tf_op jit(solution)/shard_map/ppermute | solution.py:355
  91.1 12.1 %collective-permute-start.10 = (bf16[4,128,512]{2,1,0:T(8,128)(2,1)}, bf16[4,128,512]{2,1,0:T(8,128)(2,1)S(1)}, u32[]{:S(2)}, u32[]{:S(2)}) collective-permute-start(bf16[4,128,512]{2,1,0:T(8,128)(2,1)} %get-tuple-element.34), channel_id=1, source_target_pairs={{0,8},{8,16},{16,24},{24,0},{32,40},{40,48},{48,56},{56,32},{64,72... | collective-permute-start | bytes 1572872 | tf_op jit(solution)/shard_map/ppermute | solution.py:312
  91.1 23.2 %collective-permute-start.13 = (bf16[4,128,512]{2,1,0:T(8,128)(2,1)}, bf16[4,128,512]{2,1,0:T(8,128)(2,1)S(1)}, u32[]{:S(2)}, u32[]{:S(2)}) collective-permute-start(bf16[4,128,512]{2,1,0:T(8,128)(2,1)} %get-tuple-element.37), channel_id=1, source_target_pairs={{0,8},{8,16},{16,24},{24,0},{32,40},{40,48},{48,56},{56,32},{64,72... | collective-permute-start | bytes 1572872 | tf_op jit(solution)/shard_map/ppermute | solution.py:312
  91.7 29.3 %collective-permute-start.12 = (bf16[4,128,512]{2,1,0:T(8,128)(2,1)}, bf16[4,128,512]{2,1,0:T(8,128)(2,1)S(1)}, u32[]{:S(2)}, u32[]{:S(2)}) collective-permute-start(bf16[4,128,512]{2,1,0:T(8,128)(2,1)} %get-tuple-element.35), channel_id=1, source_target_pairs={{0,24},{8,0},{16,8},{24,16},{32,56},{40,32},{48,40},{56,48},{64,88... | collective-permute-start | bytes 1572872 | tf_op jit(solution)/shard_map/ppermute | solution.py:312
  99.0 8.6 %collective-permute-start.4 = (bf16[4,128,512]{2,1,0:T(8,128)(2,1)}, bf16[4,128,512]{2,1,0:T(8,128)(2,1)S(1)}, u32[]{:S(2)}, u32[]{:S(2)}) collective-permute-start(bf16[4,128,512]{2,1,0:T(8,128)(2,1)} %get-tuple-element.31), channel_id=1, source_target_pairs={{0,96},{8,104},{16,112},{24,120},{32,0},{40,8},{48,16},{56,24},{64... | collective-permute-start | bytes 1572872 | tf_op jit(solution)/shard_map/ppermute | solution.py:312
  100.7 10.5 %copy-start.6 = (bf16[4,128,512]{2,1,0:T(8,128)(2,1)S(1)}, bf16[4,128,512]{2,1,0:T(8,128)(2,1)}, u32[]{:S(2)}) copy-start(bf16[4,128,512]{2,1,0:T(8,128)(2,1)} %get-tuple-element.30) | copy-start | bytes 1572868
  103.2 9.6 %collective-permute-start = (bf16[4,128,512]{2,1,0:T(8,128)(2,1)S(1)}, bf16[4,128,512]{2,1,0:T(8,128)(2,1)S(1)}, u32[]{:S(2)}, u32[]{:S(2)}) collective-permute-start(bf16[4,128,512]{2,1,0:T(8,128)(2,1)S(1)} %copy-done.15), channel_id=1, source_target_pairs={{0,32},{8,40},{16,48},{24,56},{32,64},{40,72},{48,80},{56,88},{64,... | collective-permute-start | bytes 1572872 | tf_op jit(solution)/shard_map/ppermute | solution.py:312
  105.3 7.5 %copy-start.5 = (bf16[4,128,512]{2,1,0:T(8,128)(2,1)S(1)}, bf16[4,128,512]{2,1,0:T(8,128)(2,1)}, u32[]{:S(2)}) copy-start(bf16[4,128,512]{2,1,0:T(8,128)(2,1)} %get-tuple-element.25) | copy-start | bytes 1572868
  107.6 10.7 %collective-permute-start.15 = (bf16[4,128,512]{2,1,0:T(8,128)(2,1)S(1)}, bf16[4,128,512]{2,1,0:T(8,128)(2,1)S(1)}, u32[]{:S(2)}, u32[]{:S(2)}) collective-permute-start(bf16[4,128,512]{2,1,0:T(8,128)(2,1)S(1)} %add_convert_fusion), channel_id=1, source_target_pairs={{0,24},{8,0},{16,8},{24,16},{32,56},{40,32},{48,40},{56,48},{64,88... | collective-permute-start | bytes 1572872 | tf_op jit(solution)/shard_map/ppermute | solution.py:312
  111.2 3.2 %copy-start.14 = (bf16[4,128,512]{2,1,0:T(8,128)(2,1)S(1)}, bf16[4,128,512]{2,1,0:T(8,128)(2,1)}, u32[]{:S(2)}) copy-start(bf16[4,128,512]{2,1,0:T(8,128)(2,1)} %get-tuple-element.29) | copy-start | bytes 1572868
  111.2 7.1 %copy-start.13 = (bf16[4,128,512]{2,1,0:T(8,128)(2,1)S(1)}, bf16[4,128,512]{2,1,0:T(8,128)(2,1)}, u32[]{:S(2)}) copy-start(bf16[4,128,512]{2,1,0:T(8,128)(2,1)} %get-tuple-element.27) | copy-start | bytes 1572868
  111.2 9.5 %copy-start.11 = (bf16[4,128,512]{2,1,0:T(8,128)(2,1)S(1)}, bf16[4,128,512]{2,1,0:T(8,128)(2,1)}, u32[]{:S(2)}) copy-start(bf16[4,128,512]{2,1,0:T(8,128)(2,1)} %get-tuple-element.36) | copy-start | bytes 1572868
  112.8 10.2 %collective-permute-start.11 = (bf16[4,128,512]{2,1,0:T(8,128)(2,1)S(1)}, bf16[4,128,512]{2,1,0:T(8,128)(2,1)S(1)}, u32[]{:S(2)}, u32[]{:S(2)}) collective-permute-start(bf16[4,128,512]{2,1,0:T(8,128)(2,1)S(1)} %add_convert_fusion.1), channel_id=1, source_target_pairs={{0,8},{8,16},{16,24},{24,0},{32,40},{40,48},{48,56},{56,32},{64,72... | collective-permute-start | bytes 1572872 | tf_op jit(solution)/shard_map/ppermute | solution.py:312
  114.4 13.4 %collective-permute-start.3 = (bf16[4,128,512]{2,1,0:T(8,128)(2,1)S(1)}, bf16[4,128,512]{2,1,0:T(8,128)(2,1)S(1)}, u32[]{:S(2)}, u32[]{:S(2)}) collective-permute-start(bf16[4,128,512]{2,1,0:T(8,128)(2,1)S(1)} %copy-done.14), channel_id=1, source_target_pairs={{0,32},{8,40},{16,48},{24,56},{32,64},{40,72},{48,80},{56,88},{64,... | collective-permute-start | bytes 1572872 | tf_op jit(solution)/shard_map/ppermute | solution.py:312
  118.3 21.7 %collective-permute-start.2 = (bf16[4,128,512]{2,1,0:T(8,128)(2,1)S(1)}, bf16[4,128,512]{2,1,0:T(8,128)(2,1)S(1)}, u32[]{:S(2)}, u32[]{:S(2)}) collective-permute-start(bf16[4,128,512]{2,1,0:T(8,128)(2,1)S(1)} %copy-done.13), channel_id=1, source_target_pairs={{0,96},{8,104},{16,112},{24,120},{32,0},{40,8},{48,16},{56,24},{64... | collective-permute-start | bytes 1572872 | tf_op jit(solution)/shard_map/ppermute | solution.py:312
  120.8 4.0 %copy-start.10 = (bf16[4,128,512]{2,1,0:T(8,128)(2,1)S(1)}, bf16[4,128,512]{2,1,0:T(8,128)(2,1)}, u32[]{:S(2)}) copy-start(bf16[4,128,512]{2,1,0:T(8,128)(2,1)} %get-tuple-element.32) | copy-start | bytes 1572868
  121.0 4.0 %copy-start.2 = (bf16[4,128,512]{2,1,0:T(8,128)(2,1)}, bf16[4,128,512]{2,1,0:T(8,128)(2,1)S(1)}, u32[]{:S(2)}) copy-start(bf16[4,128,512]{2,1,0:T(8,128)(2,1)S(1)} %get-tuple-element.44) | copy-start | bytes 1572868
  121.0 16.0 %collective-permute-start.5 = (bf16[4,128,512]{2,1,0:T(8,128)(2,1)S(1)}, bf16[4,128,512]{2,1,0:T(8,128)(2,1)S(1)}, u32[]{:S(2)}, u32[]{:S(2)}) collective-permute-start(bf16[4,128,512]{2,1,0:T(8,128)(2,1)S(1)} %add_convert_fusion.2), channel_id=1, source_target_pairs={{0,96},{8,104},{16,112},{24,120},{32,0},{40,8},{48,16},{56,24},{64... | collective-permute-start | bytes 1572872 | tf_op jit(solution)/shard_map/ppermute | solution.py:312
  123.0 18.4 %collective-permute-start.1 = (bf16[4,128,512]{2,1,0:T(8,128)(2,1)S(1)}, bf16[4,128,512]{2,1,0:T(8,128)(2,1)S(1)}, u32[]{:S(2)}, u32[]{:S(2)}) collective-permute-start(bf16[4,128,512]{2,1,0:T(8,128)(2,1)S(1)} %add_convert_fusion.3), channel_id=1, source_target_pairs={{0,32},{8,40},{16,48},{24,56},{32,64},{40,72},{48,80},{56,88},{64,... | collective-permute-start | bytes 1572872 | tf_op jit(solution)/shard_map/ppermute | solution.py:312
  125.0 15.0 %copy-start.1 = (bf16[4,128,512]{2,1,0:T(8,128)(2,1)}, bf16[4,128,512]{2,1,0:T(8,128)(2,1)S(1)}, u32[]{:S(2)}) copy-start(bf16[4,128,512]{2,1,0:T(8,128)(2,1)S(1)} %get-tuple-element.42) | copy-start | bytes 1572868
  125.0 13.8 %copy-start.9 = (bf16[4,128,512]{2,1,0:T(8,128)(2,1)S(1)}, bf16[4,128,512]{2,1,0:T(8,128)(2,1)}, u32[]{:S(2)}) copy-start(bf16[4,128,512]{2,1,0:T(8,128)(2,1)} %get-tuple-element.28) | copy-start | bytes 1572868
  125.9 27.4 %collective-permute-start.22 = (bf16[1024,512]{1,0:T(8,128)(2,1)}, bf16[1024,512]{1,0:T(8,128)(2,1)}, u32[]{:S(2)}, u32[]{:S(2)}) collective-permute-start(bf16[1024,512]{1,0:T(8,128)(2,1)} %refs_7_.1), channel_id=1, source_target_pairs={{0,6},{1,7},{2,0},{3,1},{4,2},{5,3},{6,4},{7,5},{8,14},{9,15},{10,... | collective-permute-start | bytes 3145736 | tf_op jit(solution)/shard_map/ppermute | solution.py:355
  127.8 33.8 %collective-permute-start.21 = (bf16[1024,512]{1,0:T(8,128)(2,1)}, bf16[1024,512]{1,0:T(8,128)(2,1)}, u32[]{:S(2)}, u32[]{:S(2)}) collective-permute-start(bf16[1024,512]{1,0:T(8,128)(2,1)} %collective-permute-done.20.refs_8_), channel_id=1, source_target_pairs={{0,2},{1,3},{2,4},{3,5},{4,6},{5,7},{6,0},{7,1},{8,10},{9,11},{10,... | collective-permute-start | bytes 3145736 | tf_op jit(solution)/shard_map/ppermute | solution.py:355
  137.0 24.6 %collective-permute-start.16 = (bf16[2,128,512]{2,1,0:T(8,128)(2,1)}, bf16[2,128,512]{2,1,0:T(8,128)(2,1)}, u32[]{:S(2)}, u32[]{:S(2)}) collective-permute-start(bf16[2,128,512]{2,1,0:T(8,128)(2,1)} %pad_maximum_fusion.2), channel_id=1, source_target_pairs={{0,32},{8,40},{16,48},{24,56},{32,64},{40,72},{48,80},{56,88},{64,... | collective-permute-start | bytes 786440 | tf_op jit(solution)/shard_map/ppermute | solution.py:312
  138.8 2.6 %copy-start.8 = (bf16[4,128,512]{2,1,0:T(8,128)(2,1)S(1)}, bf16[4,128,512]{2,1,0:T(8,128)(2,1)}, u32[]{:S(2)}) copy-start(bf16[4,128,512]{2,1,0:T(8,128)(2,1)} %get-tuple-element.24) | copy-start | bytes 1572868
  140.0 1.7 copy-start.4
  140.0 6.5 %collective-permute-start.18 = (bf16[2,128,512]{2,1,0:T(8,128)(2,1)S(1)}, bf16[2,128,512]{2,1,0:T(8,128)(2,1)S(1)}, u32[]{:S(2)}, u32[]{:S(2)}) collective-permute-start(bf16[2,128,512]{2,1,0:T(8,128)(2,1)S(1)} %pad_maximum_fusion.3), channel_id=1, source_target_pairs={{0,96},{8,104},{16,112},{24,120},{32,0},{40,8},{48,16},{56,24},{64... | collective-permute-start | bytes 786440 | tf_op jit(solution)/shard_map/ppermute | solution.py:312
  141.6 0.8 copy-start.3
  141.7 9.0 %copy-start.12 = (s32[512]{0:T(512)S(1)}, s32[512]{0:T(512)}, u32[]{:S(2)}) copy-start(s32[512]{0:T(512)} %param.16) | copy-start | bytes 6148
  143.2 18.8 %collective-permute-start.6 = (bf16[2,128,512]{2,1,0:T(8,128)(2,1)}, bf16[2,128,512]{2,1,0:T(8,128)(2,1)}, u32[]{:S(2)}, u32[]{:S(2)}) collective-permute-start(bf16[2,128,512]{2,1,0:T(8,128)(2,1)} %pad_maximum_fusion), channel_id=1, source_target_pairs={{0,8},{8,16},{16,24},{24,0},{32,40},{40,48},{48,56},{56,32},{64,72... | collective-permute-start | bytes 786440 | tf_op jit(solution)/shard_map/ppermute | solution.py:312
  146.5 15.6 %collective-permute-start.8 = (bf16[2,128,512]{2,1,0:T(8,128)(2,1)}, bf16[2,128,512]{2,1,0:T(8,128)(2,1)}, u32[]{:S(2)}, u32[]{:S(2)}) collective-permute-start(bf16[2,128,512]{2,1,0:T(8,128)(2,1)} %pad_maximum_fusion.1), channel_id=1, source_target_pairs={{0,24},{8,0},{16,8},{24,16},{32,56},{40,32},{48,40},{56,48},{64,88... | collective-permute-start | bytes 786440 | tf_op jit(solution)/shard_map/ppermute | solution.py:312
  153.3 31.0 %collective-permute-start.23 = (bf16[1024,512]{1,0:T(8,128)(2,1)}, bf16[1024,512]{1,0:T(8,128)(2,1)}, u32[]{:S(2)}, u32[]{:S(2)}) collective-permute-start(bf16[1024,512]{1,0:T(8,128)(2,1)} %refs_7_.1), channel_id=1, source_target_pairs={{0,1},{1,0},{2,3},{3,2},{4,5},{5,4},{6,7},{7,6},{8,9},{9,8},{10,11... | collective-permute-start | bytes 3145736 | tf_op jit(solution)/shard_map/ppermute | solution.py:355
  161.5 22.8 %collective-permute-start.24 = (bf16[1024,512]{1,0:T(8,128)(2,1)}, bf16[1024,512]{1,0:T(8,128)(2,1)}, u32[]{:S(2)}, u32[]{:S(2)}) collective-permute-start(bf16[1024,512]{1,0:T(8,128)(2,1)} %collective-permute-done.20.refs_8_), channel_id=1, source_target_pairs={{0,1},{1,0},{2,3},{3,2},{4,5},{5,4},{6,7},{7,6},{8,9},{9,8},{10,11... | collective-permute-start | bytes 3145736 | tf_op jit(solution)/shard_map/ppermute | solution.py:355
  161.6 22.7 %collective-permute-start.26 = (bf16[1024,512]{1,0:T(8,128)(2,1)}, bf16[1024,512]{1,0:T(8,128)(2,1)}, u32[]{:S(2)}, u32[]{:S(2)}) collective-permute-start(bf16[1024,512]{1,0:T(8,128)(2,1)} %collective-permute-done.22.refs_10_), channel_id=1, source_target_pairs={{0,1},{1,0},{2,3},{3,2},{4,5},{5,4},{6,7},{7,6},{8,9},{9,8},{10,11... | collective-permute-start | bytes 3145736 | tf_op jit(solution)/shard_map/ppermute | solution.py:355
  162.0 22.2 %collective-permute-start.25 = (bf16[1024,512]{1,0:T(8,128)(2,1)}, bf16[1024,512]{1,0:T(8,128)(2,1)}, u32[]{:S(2)}, u32[]{:S(2)}) collective-permute-start(bf16[1024,512]{1,0:T(8,128)(2,1)} %collective-permute-done.21.refs_9_), channel_id=1, source_target_pairs={{0,1},{1,0},{2,3},{3,2},{4,5},{5,4},{6,7},{7,6},{8,9},{9,8},{10,11... | collective-permute-start | bytes 3145736 | tf_op jit(solution)/shard_map/ppermute | solution.py:355
  162.1 5.9 %collective-permute-start.19 = (bf16[1,128,512]{2,1,0:T(8,128)(2,1)S(1)}, bf16[1,128,512]{2,1,0:T(8,128)(2,1)S(1)}, u32[]{:S(2)}, u32[]{:S(2)}) collective-permute-start(bf16[1,128,512]{2,1,0:T(8,128)(2,1)S(1)} %add_convert_fusion.4), channel_id=1, source_target_pairs={{0,96},{8,104},{16,112},{24,120},{32,0},{40,8},{48,16},{56,24},{64... | collective-permute-start | bytes 393224 | tf_op jit(solution)/shard_map/ppermute | solution.py:312
  168.0 3.8 %collective-permute-start.9 = (bf16[1,128,512]{2,1,0:T(8,128)(2,1)S(1)}, bf16[1,128,512]{2,1,0:T(8,128)(2,1)S(1)}, u32[]{:S(2)}, u32[]{:S(2)}) collective-permute-start(bf16[1,128,512]{2,1,0:T(8,128)(2,1)S(1)} %add_convert_fusion.6), channel_id=1, source_target_pairs={{0,24},{8,0},{16,8},{24,16},{32,56},{40,32},{48,40},{56,48},{64,88... | collective-permute-start | bytes 393224 | tf_op jit(solution)/shard_map/ppermute | solution.py:312
  171.8 5.8 %collective-permute-start.17 = (bf16[1,128,512]{2,1,0:T(8,128)(2,1)S(1)}, bf16[1,128,512]{2,1,0:T(8,128)(2,1)S(1)}, u32[]{:S(2)}, u32[]{:S(2)}) collective-permute-start(bf16[1,128,512]{2,1,0:T(8,128)(2,1)S(1)} %get-tuple-element.59), channel_id=1, source_target_pairs={{0,32},{8,40},{16,48},{24,56},{32,64},{40,72},{48,80},{56,88},{64,... | collective-permute-start | bytes 393224 | tf_op jit(solution)/shard_map/ppermute | solution.py:312
  177.6 5.0 %collective-permute-start.7 = (bf16[1,128,512]{2,1,0:T(8,128)(2,1)S(1)}, bf16[1,128,512]{2,1,0:T(8,128)(2,1)S(1)}, u32[]{:S(2)}, u32[]{:S(2)}) collective-permute-start(bf16[1,128,512]{2,1,0:T(8,128)(2,1)S(1)} %get-tuple-element.61), channel_id=1, source_target_pairs={{0,8},{8,16},{16,24},{24,0},{32,40},{40,48},{48,56},{56,32},{64,72... | collective-permute-start | bytes 393224 | tf_op jit(solution)/shard_map/ppermute | solution.py:312
where the time goes:
time: 228 us
  Pallas kernels  77 us (34%)
  starting transfers between devices  51.9 us (23%)
  waiting for transfers between devices  37.9 us (17%)
  other arithmetic  27.1 us (12%)
  blocking collectives  26.2 us (11%)
  local copies, waits for them, and re-layouts  6.56 us (3%)
    pallas_call x1, Pallas kernels, owner_sums(): pl.pallas_call(owner_kernel, grid=(devices,), in_specs=[pl.BlockSpec(memo...  42.8 us
    ppermute x20, waiting for transfers between devices, moved(): return lax.ppermute(x, 'neg', [(i, place(i)) for i in range(SIDE * SIDE)])  35.7 us
    ppermute x20, starting transfers between devices, moved(): return lax.ppermute(x, 'neg', [(i, place(i)) for i in range(SIDE * SIDE)])  31.9 us
    all_to_all x1, blocking collectives, per_device(): lax.all_to_all(shared.reshape(parts * groups, -1), ('neg', 'qry'), split_...  26.2 us
    pallas_call x1, Pallas kernels, tables(): pl.pallas_call(table_kernel, grid=(items // STAGE,), in_specs=[block, wei...  17.2 us
    pallas_call x1, Pallas kernels, scored(): pl.pallas_call(score_kernel, in_specs=[in_vmem] * 7 + [pl.BlockSpec(memor...  14.4 us
    ppermute x7, starting transfers between devices, turned(): return lax.ppermute(x, 'qry', [(i, place(i)) for i in range(2 * SIDE)])  12.4 us
    sort x1, other arithmetic, per_device(): lax.sort(keys, is_stable=False)  9.26 us
  transfers between devices with their start and end apart: 28, of which 14 were waited for; matrix products, arithmetic and copies ran while one was open for 8% of the time, Pallas kernels for 8%

commit v1 on v0

--- a/solution.py
+++ b/solution.py
@@ -15,8 +15,11 @@
 BLOCK = 10
 STAGE = 1024
 DEEP = 4
+LINES = 176
+COUNTS = 165
 SIDE = 4
 SCORED = 256
+LOG2E = 1.4426950408889634
 MESSAGES = 2 * SIDE
 
 
@@ -65,7 +68,7 @@
 
 def owner_kernel(part_ref, ends_ref, lists_ref, message_hbm, self_hbm, *refs):
     outs = refs[: 2 * MESSAGES]
-    table, stage, pick, rows, acc, offsets, places, ready, sems, place_sem, out_sems = refs[2 * MESSAGES :]
+    table, stage, pick, rows, acc, raw, weights, offsets, places, ready, sems, place_sem, out_sems = refs[2 * MESSAGES :]
     items = message_hbm.shape[0]
     width = message_hbm.shape[1]
     tiles = width // LANES
@@ -89,8 +92,18 @@
 
     def place(r, base):
         for c in range(BLOCK):
-            line = lists_ref[r, pl.ds(base + c, 1), :]
-            offsets[c : c + 1, :] = (line & 16383) * tiles
+            raw[c : c + 1, :] = lists_ref[r, pl.ds(base + c, 1), :]
+        for half in range(2):
+            at = slice(8 * half, 8 * half + 8)
+            lines = raw[at, :]
+            offsets[at, :] = (lines & 16383) * tiles
+            v = (lines >> 16) & (negatives - 1)
+            count = jnp.zeros_like(v)
+            for q in range(negatives // LANES):
+                counts = jnp.broadcast_to(lists_ref[r, COUNTS + q : COUNTS + q + 1, :], v.shape)
+                found = jnp.take_along_axis(counts, v & (LANES - 1), axis=1, mode="promise_in_bounds")
+                count = jnp.where(v >> 7 == q, found, count)
+            weights[at, :] = jnp.where((lines & 8192) != 0, count, 1).astype(jnp.float32)
         place_copy().start()
 
     def stage_copy(c):
@@ -112,7 +125,7 @@
     def _():
         for c in range(DEEP):
             stage_copy(c).start()
-        offsets[...] = jnp.zeros_like(offsets)
+        raw[...] = jnp.zeros_like(raw)
         place(asker(0), range_of(asker(0))[0] >> 7)
         rows[...] = jnp.zeros_like(rows)
         for c in range(2 * per_table):
@@ -139,12 +152,10 @@
     row_first = start >> 7
     row_last = (end + 127) >> 7
 
-    def picked(r):
+    def picked(r, line, weight):
         v = lax.broadcasted_iota(jnp.int32, (negatives, LANES), 0)
-        line = lists_ref[a, pl.ds(r, 1), :]
         at = r * LANES + lax.broadcasted_iota(jnp.int32, (1, LANES), 1)
-        who = jnp.where((at >= start) & (at < end), (line >> 19) & 511, -1)
-        weight = jnp.where((line & 8192) != 0, ((line >> 14) & 31) + 20, 1).astype(jnp.float32)
+        who = jnp.where((at >= start) & (at < end), line >> 16, -1)
         return jnp.where(v == who, weight, 0.0).astype(jnp.bfloat16)
 
     def gather(base):
@@ -154,7 +165,7 @@
 
             @pl.when(r < row_last)
             def _(c=c, r=r):
-                pick[:, c * LANES : (c + 1) * LANES] = picked(r)
+                pick[:, c * LANES : (c + 1) * LANES] = picked(r, raw[c : c + 1, :], weights[c : c + 1, :])
                 for e in range(CHUNK):
                     at = pl.multiple_of(places[c, e], tiles)
                     rows[c, pl.ds(e, tiles, stride=STRIDE), :] = table[pl.ds(at, tiles), :]
@@ -169,7 +180,8 @@
         def chunk(c, _):
             cols = pl.ds(pl.multiple_of(c * LANES, LANES), LANES)
             live = base + c < row_last
-            pick[:, cols] = jnp.where(live, picked(base + c), 0).astype(jnp.bfloat16)
+            one = pl.ds(c, 1)
+            pick[:, cols] = jnp.where(live, picked(base + c, raw[one, :], weights[one, :]), 0).astype(jnp.bfloat16)
 
             def entry(e, _):
                 at = pl.multiple_of(places[c, e], tiles)
@@ -289,6 +301,8 @@
             pltpu.VMEM((BLOCK, tiles * STRIDE, LANES), jnp.float32),
             pltpu.VMEM((negatives, width), jnp.float32),
             pltpu.VMEM((16, LANES), jnp.int32),
+            pltpu.VMEM((16, LANES), jnp.float32),
+            pltpu.VMEM((16, LANES), jnp.int32),
             pltpu.SMEM((16, LANES), jnp.int32),
             pltpu.VMEM((2, negatives, width), jnp.bfloat16),
             pltpu.SemaphoreType.DMA((DEEP,)),
@@ -394,44 +408,66 @@
     sums = refs[:4]
     count_ref, bias_ref, log_ref = refs[4:7]
     queries = refs[7 : 7 + 2 * SIDE]
-    embed_ref, lse_ref, held, sems = refs[7 + 2 * SIDE :]
+    embed_ref, lse_ref, held, even, odd, logs, sems = refs[7 + 2 * SIDE :]
     f32 = jnp.float32
     rows = queries[0].shape[0]
+    blocks = len(queries) * rows // SCORED
+    per_query = rows // SCORED
 
     def copy(j, source):
         return pltpu.make_async_copy(source, held.at[pl.ds(j * rows, rows), :], sems.at[j])
 
     for j, source in enumerate(queries):
         copy(j, source).start()
-    quarter = embed_ref.shape[0] // 4
+    negatives, width = embed_ref.shape
+
+    def columns(row):
+        return jnp.broadcast_to(row, (LANES, negatives)).T
+
+    logs[...] = columns(jnp.log(log_ref[...].astype(f32)) * LOG2E)
+    counts = columns(count_ref[...].astype(f32))
+    quarter = negatives // 4
     for q in range(4):
         at = slice(q * quarter, (q + 1) * quarter)
-        hidden = jnp.maximum(sums[q][...] / count_ref[at, :] + bias_ref[...], 0.0)
+        count = jnp.concatenate([counts[at, :]] * (width // LANES), axis=1)
+        hidden = jnp.maximum(sums[q][...] / count + bias_ref[...], 0.0)
         scale_inv = lax.rsqrt(jnp.mean(hidden * hidden, axis=-1, keepdims=True) + 0.25)
         embed_ref[at, :] = (hidden * scale_inv).astype(jnp.bfloat16)
 
-    def block(j, _):
-        copy(j, queries[0]).wait()
-
-        def pair(i, _):
-            first = j * rows + i * 2 * SCORED
-            for u in range(2):
-                at = pl.multiple_of(first + u * SCORED, SCORED)
-                scores = lax.dot_general(
-                    embed_ref[...], held[pl.ds(at, SCORED), :], (((1,), (1,)), ((), ())), preferred_element_type=f32
-                )
-                scores = 0.25 * scores - log_ref[...]
-                peak = jnp.max(scores, axis=0, keepdims=True)
-                total = jnp.sum(jnp.exp(scores - peak), axis=0, keepdims=True)
-                lse_ref[pl.ds(at // SCORED, 1), :] = peak + jnp.log(total)
-            return 0
-
-        return lax.fori_loop(0, rows // (2 * SCORED), pair, 0)
-
-    lax.fori_loop(0, len(queries), block, 0)
-
-
-def scored(sums, count, bias, log_count, queries):
+    def products(i):
+        block = held[pl.ds(pl.multiple_of(i * SCORED, SCORED), SCORED), :]
+        return lax.dot_general(embed_ref[...], block, (((1,), (1,)), ((), ())), preferred_element_type=f32)
+
+    def reduced(ref, i):
+        found = []
+        for j in range(SCORED // LANES):
+            lane = slice(j * LANES, (j + 1) * LANES)
+            scores = ref[:, lane] * (0.25 * LOG2E) - logs[...]
+            peak = jnp.max(scores, axis=0, keepdims=True)
+            total = jnp.sum(jnp.exp2(scores - peak), axis=0, keepdims=True)
+            found.append((peak + jnp.log2(total)) * (1.0 / LOG2E))
+        lse_ref[pl.ds(i, 1), :] = jnp.concatenate(found, axis=1)
+
+    copy(0, queries[0]).wait()
+    even[...] = products(0)
+
+    def pair(i, _):
+        following = jnp.minimum(2 * i + 2, blocks - 1)
+
+        @pl.when((following % per_query == 0) & (2 * i + 2 < blocks))
+        def _():
+            copy(following // per_query, queries[0]).wait()
+
+        odd[...] = products(2 * i + 1)
+        reduced(even, 2 * i)
+        even[...] = products(following)
+        reduced(odd, 2 * i + 1)
+        return 0
+
+    lax.fori_loop(0, blocks // 2, pair, 0)
+
+
+def scored(sums, count, bias, own_count, queries):
     negatives = count.shape[0]
     rows, width = queries[0].shape
     total = rows * len(queries)
@@ -446,10 +482,13 @@
         ],
         scratch_shapes=[
             pltpu.VMEM((total, width), jnp.bfloat16),
+            pltpu.VMEM((negatives, SCORED), jnp.float32),
+            pltpu.VMEM((negatives, SCORED), jnp.float32),
+            pltpu.VMEM((negatives, LANES), jnp.float32),
             pltpu.SemaphoreType.DMA((len(queries),)),
         ],
         name="score",
-    )(*sums, count[:, None], bias[None, :], log_count[:, None], *queries)
+    )(*sums, count[None, :], bias[None, :], own_count[None, :], *queries)
 
 
 def per_device(
@@ -466,7 +505,6 @@
     output_bias,
     queries,
 ):
-    f32 = jnp.float32
     negatives = neighbour_count.shape[0]
     parts = lax.axis_size("neg")
     groups = lax.axis_size("qry")
@@ -475,19 +513,21 @@
     keys = composed_keys(neighbour_slots, self_slot, neighbour_count, fetch_rows).reshape(-1)
     bounds = jnp.array([min((p + 1 - 8) << 28, DEAD) for p in range(parts)], jnp.int32)
     ends = jnp.sum((keys[None, :] < bounds[:, None]).astype(jnp.int32), axis=1)
-    lines = jnp.concatenate([lax.sort(keys, is_stable=False), ends, jnp.zeros((184 * LANES - keys.size - parts,), jnp.int32)])
-    lists = from_everyone(lines.reshape(184, LANES), "neg")
+    ordered = lax.sort(keys, is_stable=False)
+    ordered = (((ordered >> 19) & (negatives - 1)) << 16) | (ordered & 16383)
+    tail = jnp.zeros((LINES * LANES - keys.size - LANES - negatives,), jnp.int32)
+    lines = jnp.concatenate([ordered, jnp.pad(ends, (0, LANES - parts)), neighbour_count, tail])
+    lists = from_everyone(lines.reshape(LINES, LANES), "neg")
 
     message_part, self_part = tables(items_table, message_weight, message_bias, neighbour_weight, self_weight)
 
+    own_count = lax.dynamic_slice(negative_count, (lax.axis_index("qry") * negatives,), (negatives,))
     place = lax.axis_index("neg")
     part = jnp.stack([place // SIDE, place % SIDE]).astype(jnp.int32)
     outs = owner_sums(part, lists[:, keys.size // LANES, :parts], lists, message_part, self_part, negatives)
     sums = [q[0] for q in scattered_sums(outs)]
 
-    own_count = lax.dynamic_slice(negative_count, (lax.axis_index("qry") * negatives,), (negatives,))
-    log_count = jnp.log(own_count.astype(f32))
-    negative_embed, part_lse = scored(sums, neighbour_count.astype(f32), output_bias, log_count, query_blocks)
+    negative_embed, part_lse = scored(sums, neighbour_count, output_bias, own_count, query_blocks)
     here = lax.axis_index("qry")
     z, core = here // 2, here % 2
     group = jnp.arange(groups)

time: 228 us -> 231 us (1.013)
  starting transfers between devices: 51.9 us -> 49.3 us
  waiting for transfers between devices: 37.9 us -> 40.5 us
    ppermute x20, starting transfers between devices: 31.9 us -> 28.6 us  [moved(): return lax.ppermute(x, 'neg', [(i, place(i)) for i in range(SIDE * SIDE)])]
    ppermute x20, waiting for transfers between devices: 35.7 us -> 38.9 us  [moved(): return lax.ppermute(x, 'neg', [(i, place(i)) for i in range(SIDE * SIDE)])]
  transfers between devices with their start and end apart: 28 -> 28, of which waited for: 14 -> 11; matrix products, arithmetic and copies ran while one was open for 8% -> 7% of each run, Pallas kernels for 8% -> 7%
where the time goes in v1:
time: 231 us; the launch traced here: 230 us
  Pallas kernels  77.6 us (34%)
  starting transfers between devices  49.3 us (21%)
  waiting for transfers between devices  40.5 us (18%)
  blocking collectives  28 us (12%)
  other arithmetic  27 us (12%)
  local copies, waits for them, and re-layouts  6.69 us (3%)
    pallas_call x1, Pallas kernels, owner_sums(): pl.pallas_call(owner_kernel, grid=(devices,), in_specs=[pl.BlockSpec(memo...  43.8 us
    ppermute x20, waiting for transfers between devices, moved(): return lax.ppermute(x, 'neg', [(i, place(i)) for i in range(SIDE * SIDE)])  38.9 us
    ppermute x20, starting transfers between devices, moved(): return lax.ppermute(x, 'neg', [(i, place(i)) for i in range(SIDE * SIDE)])  28.6 us
    all_to_all x1, blocking collectives, per_device(): lax.all_to_all(shared.reshape(parts * groups, -1), ('neg', 'qry'), split_...  28 us
    pallas_call x1, Pallas kernels, tables(): pl.pallas_call(table_kernel, grid=(items // STAGE,), in_specs=[block, wei...  17.2 us
    pallas_call x1, Pallas kernels, scored(): pl.pallas_call(score_kernel, in_specs=[in_vmem] * 7 + [pl.BlockSpec(memor...  14 us
    ppermute x7, starting transfers between devices, turned(): return lax.ppermute(x, 'qry', [(i, place(i)) for i in range(2 * SIDE)])  13.1 us
    sort x1, other arithmetic, per_device(): ordered = lax.sort(keys, is_stable=False)  9.26 us
  transfers between devices with their start and end apart: 28, of which 11 were waited for; matrix products, arithmetic and copies ran while one was open for 7% of the time, Pallas kernels for 7%

profile of v1, /device:TPU:1, one launch (start us, length us, event | category | flops | bytes accessed | tf_op | source)
XLA Modules:
  0.0 230.2 jit_solution(4307127626701604158)
XLA Ops:
  0.6 2.6 %compose.1 = s32[164,128]{1,0:T(8,128)} custom-call(s32[40,512]{1,0:T(8,128)} %bitcast.28, s32[1,512]{1,0:T(1,128)} %bitcast.34, s32[1,512]{1,0:T(1,128)} %bitcast.30, s32[16,640]{1,0:T(8,128)} %fetch_ref.1), custom_call_target="tpu_custom_call" | custom-call | tf_op jit(solution)/shard_map/compose/pallas_call | solution.py:268
  3.2 9.3 %sort.7 = s32[20992]{0:T(1024)S(1)} sort(s32[20992]{0:T(1024)} %bitcast.26), dimensions={0}, to_apply=%region_0.0 | sort | flops 314880 | bytes 167936 | tf_op jit(solution)/shard_map/sort | solution.py:516
  12.5 1.2 convert_reduce_fusion
  13.7 0.7 fusion.12
  14.4 1.2 broadcast_in_dim.63
  15.7 7.6 %all-to-all-start = ((s32[16,176,128]{2,1,0:T(8,128)}), s32[16,176,128]{2,1,0:T(8,128)S(1)}, u32[]{:S(2)}, u32[]{:S(2)}) async-start(s32[16,176,128]{2,1,0:T(8,128)} %broadcast_in_dim.63), calls=%async_computation | async-start | bytes 2883584 | tf_op jit(solution)/shard_map/all_to_all | solution.py:262
  23.3 17.2 %tables.1 = (bf16[8192,512]{1,0:T(8,128)(2,1)}, bf16[8192,512]{1,0:T(8,128)(2,1)}) custom-call(bf16[8192,512]{1,0:T(8,128)(2,1)} %items_ref.1, bf16[512,512]{1,0:T(8,128)(2,1)} %message_ref.1, f32[1,512]{1,0:T(1,128)} %bitcast.35, bf16[512,512]{1,0:T(8,128)(2,1)} %neighbour_ref.1, bf16[512,512]{1,0:T(8,128)(2,1)} %self_ref.1), custom_call_target="tpu_custom_call" | custom-call | tf_op jit(solution)/shard_map/tables/pallas_call | solution.py:396
  40.5 0.6 pad_add_fusion.1.part_ref
  41.1 1.6 all-to-all-done.lists_ref
  42.7 0.6 slice.100
  43.4 0.5 copy-done
  43.9 43.8 %owner.1 = (bf16[4,128,512]{2,1,0:T(8,128)(2,1)}, bf16[4,128,512]{2,1,0:T(8,128)(2,1)}, bf16[4,128,512]{2,1,0:T(8,128)(2,1)}, bf16[4,128,512]{2,1,0:T(8,128)(2,1...) custom-call(s32[2]{0:T(128)} %pad_add_fusion.1.part_ref, ...), custom_call_target="tpu_custom_call" | custom-call | tf_op jit(solution)/shard_map/owner/pallas_call | solution.py:285
  87.7 2.4 %collective-permute-start.14 = (bf16[4,128,512]{2,1,0:T(8,128)(2,1)}, bf16[4,128,512]{2,1,0:T(8,128)(2,1)S(1)}, u32[]{:S(2)}, u32[]{:S(2)}) collective-permute-start(bf16[4,128,512]{2,1,0:T(8,128)(2,1)} %get-tuple-element.39), channel_id=1, source_target_pairs={{0,24},{8,0},{16,8},{24,16},{32,56},{40,32},{48,40},{56,48},{64,88... | collective-permute-start | bytes 1572872 | tf_op jit(solution)/shard_map/ppermute | solution.py:326
  90.2 1.7 collective-permute-start.20
  91.9 0.7 collective-permute-start.13
  92.6 2.2 collective-permute-start.12
  94.7 5.1 %collective-permute-done.14 = bf16[4,128,512]{2,1,0:T(8,128)(2,1)S(1)} collective-permute-done((bf16[4,128,512]{2,1,0:T(8,128)(2,1)}, bf16[4,128,512]{2,1,0:T(8,128)(2,1)S(1)}, u32[]{:S(2)}, u32[]{:S(2)}) %collective-permute-start.14) | collective-permute-done | bytes 524320 | tf_op jit(solution)/shard_map/ppermute | solution.py:326
  99.8 2.9 %collective-permute-start.4 = (bf16[4,128,512]{2,1,0:T(8,128)(2,1)}, bf16[4,128,512]{2,1,0:T(8,128)(2,1)S(1)}, u32[]{:S(2)}, u32[]{:S(2)}) collective-permute-start(bf16[4,128,512]{2,1,0:T(8,128)(2,1)} %get-tuple-element.31), channel_id=1, source_target_pairs={{0,96},{8,104},{16,112},{24,120},{32,0},{40,8},{48,16},{56,24},{64... | collective-permute-start | bytes 1572872 | tf_op jit(solution)/shard_map/ppermute | solution.py:326
  102.8 1.2 add_convert_fusion
  104.1 0.1 add_convert_fusion.1
  104.3 4.9 %collective-permute-done.4 = bf16[4,128,512]{2,1,0:T(8,128)(2,1)S(1)} collective-permute-done((bf16[4,128,512]{2,1,0:T(8,128)(2,1)}, bf16[4,128,512]{2,1,0:T(8,128)(2,1)S(1)}, u32[]{:S(2)}, u32[]{:S(2)}) %collective-permute-start.4) | collective-permute-done | bytes 524320 | tf_op jit(solution)/shard_map/ppermute | solution.py:326
  109.2 5.1 %collective-permute-start.15 = (bf16[4,128,512]{2,1,0:T(8,128)(2,1)S(1)}, bf16[4,128,512]{2,1,0:T(8,128)(2,1)S(1)}, u32[]{:S(2)}, u32[]{:S(2)}) collective-permute-start(bf16[4,128,512]{2,1,0:T(8,128)(2,1)S(1)} %add_convert_fusion), channel_id=1, source_target_pairs={{0,24},{8,0},{16,8},{24,16},{32,56},{40,32},{48,40},{56,48},{64,88... | collective-permute-start | bytes 1572872 | tf_op jit(solution)/shard_map/ppermute | solution.py:326
  114.3 0.1 add_convert_fusion.2
  114.6 0.1 add_convert_fusion.3
  114.7 0.6 copy-done.13
  115.3 5.9 %collective-permute-done.15 = bf16[4,128,512]{2,1,0:T(8,128)(2,1)S(1)} collective-permute-done((bf16[4,128,512]{2,1,0:T(8,128)(2,1)S(1)}, bf16[4,128,512]{2,1,0:T(8,128)(2,1)S(1)}, u32[]{:S(2)}, u32[]{:S(2)}) %collective-permute-start.15) | collective-permute-done | bytes 524320 | tf_op jit(solution)/shard_map/ppermute | solution.py:326
  121.2 3.5 %collective-permute-start.2 = (bf16[4,128,512]{2,1,0:T(8,128)(2,1)S(1)}, bf16[4,128,512]{2,1,0:T(8,128)(2,1)S(1)}, u32[]{:S(2)}, u32[]{:S(2)}) collective-permute-start(bf16[4,128,512]{2,1,0:T(8,128)(2,1)S(1)} %copy-done.12), channel_id=1, source_target_pairs={{0,96},{8,104},{16,112},{24,120},{32,0},{40,8},{48,16},{56,24},{64... | collective-permute-start | bytes 1572872 | tf_op jit(solution)/shard_map/ppermute | solution.py:326
  124.8 0.2 fusion.19
  125.1 1.0 collective-permute-done.11
  126.1 0.5 collective-permute-start.1
  126.6 0.2 fusion.18
  126.9 0.7 pad_maximum_fusion.2
  127.7 3.7 %collective-permute-start.22 = (bf16[1024,512]{1,0:T(8,128)(2,1)}, bf16[1024,512]{1,0:T(8,128)(2,1)}, u32[]{:S(2)}, u32[]{:S(2)}) collective-permute-start(bf16[1024,512]{1,0:T(8,128)(2,1)} %refs_7_.1), channel_id=1, source_target_pairs={{0,6},{1,7},{2,0},{3,1},{4,2},{5,3},{6,4},{7,5},{8,14},{9,15},{10,... | collective-permute-start | bytes 3145736 | tf_op jit(solution)/shard_map/ppermute | solution.py:369
  131.4 10.8 %collective-permute-done.5 = bf16[4,128,512]{2,1,0:T(8,128)(2,1)S(1)} collective-permute-done((bf16[4,128,512]{2,1,0:T(8,128)(2,1)S(1)}, bf16[4,128,512]{2,1,0:T(8,128)(2,1)S(1)}, u32[]{:S(2)}, u32[]{:S(2)}) %collective-permute-start.5) | collective-permute-done | bytes 524320 | tf_op jit(solution)/shard_map/ppermute | solution.py:326
  142.2 1.2 fusion.21
  143.4 3.6 %collective-permute-start.18 = (bf16[2,128,512]{2,1,0:T(8,128)(2,1)S(1)}, bf16[2,128,512]{2,1,0:T(8,128)(2,1)S(1)}, u32[]{:S(2)}, u32[]{:S(2)}) collective-permute-start(bf16[2,128,512]{2,1,0:T(8,128)(2,1)S(1)} %pad_maximum_fusion.3), channel_id=1, source_target_pairs={{0,96},{8,104},{16,112},{24,120},{32,0},{40,8},{48,16},{56,24},{64... | collective-permute-start | bytes 786440 | tf_op jit(solution)/shard_map/ppermute | solution.py:326
  147.0 0.2 fusion.20
  147.3 0.8 copy-done.3
  148.1 0.7 pad_maximum_fusion
  148.9 0.7 pad_maximum_fusion.1
  149.6 1.0 collective-permute-done.18
  150.5 3.4 %collective-permute-start.8 = (bf16[2,128,512]{2,1,0:T(8,128)(2,1)}, bf16[2,128,512]{2,1,0:T(8,128)(2,1)}, u32[]{:S(2)}, u32[]{:S(2)}) collective-permute-start(bf16[2,128,512]{2,1,0:T(8,128)(2,1)} %pad_maximum_fusion.1), channel_id=1, source_target_pairs={{0,24},{8,0},{16,8},{24,16},{32,56},{40,32},{48,40},{56,48},{64,88... | collective-permute-start | bytes 786440 | tf_op jit(solution)/shard_map/ppermute | solution.py:326
  154.0 1.3 dynamic_slice.3
  155.4 0.9 add_convert_fusion.4
  156.3 7.0 %collective-permute-start.23 = (bf16[1024,512]{1,0:T(8,128)(2,1)}, bf16[1024,512]{1,0:T(8,128)(2,1)}, u32[]{:S(2)}, u32[]{:S(2)}) collective-permute-start(bf16[1024,512]{1,0:T(8,128)(2,1)} %refs_7_.1), channel_id=1, source_target_pairs={{0,1},{1,0},{2,3},{3,2},{4,5},{5,4},{6,7},{7,6},{8,9},{9,8},{10,11... | collective-permute-start | bytes 3145736 | tf_op jit(solution)/shard_map/ppermute | solution.py:369
  163.5 0.4 collective-permute-start.26
  164.0 3.4 %collective-permute-start.19 = (bf16[1,128,512]{2,1,0:T(8,128)(2,1)S(1)}, bf16[1,128,512]{2,1,0:T(8,128)(2,1)S(1)}, u32[]{:S(2)}, u32[]{:S(2)}) collective-permute-start(bf16[1,128,512]{2,1,0:T(8,128)(2,1)S(1)} %add_convert_fusion.4), channel_id=1, source_target_pairs={{0,96},{8,104},{16,112},{24,120},{32,0},{40,8},{48,16},{56,24},{64... | collective-permute-start | bytes 393224 | tf_op jit(solution)/shard_map/ppermute | solution.py:326
  167.4 1.0 add_convert_fusion.6
  168.4 0.9 collective-permute-done.19
  169.4 1.8 fusion.3
  171.2 2.0 collective-permute-done.9
  173.2 0.7 collective-permute-start.17
  173.9 1.9 fusion.7
  175.8 2.8 %collective-permute-done.17 = bf16[1,128,512]{2,1,0:T(8,128)(2,1)S(1)} collective-permute-done((bf16[1,128,512]{2,1,0:T(8,128)(2,1)S(1)}, bf16[1,128,512]{2,1,0:T(8,128)(2,1)S(1)}, u32[]{:S(2)}, u32[]{:S(2)}) %collective-permute-start.17) | collective-permute-done | bytes 131104 | tf_op jit(solution)/shard_map/ppermute | solution.py:326
  178.6 0.8 fusion.5.refs_2_
  179.4 4.4 %collective-permute-done.7 = bf16[1,128,512]{2,1,0:T(8,128)(2,1)S(1)} collective-permute-done((bf16[1,128,512]{2,1,0:T(8,128)(2,1)S(1)}, bf16[1,128,512]{2,1,0:T(8,128)(2,1)S(1)}, u32[]{:S(2)}, u32[]{:S(2)}) %collective-permute-start.7) | collective-permute-done | bytes 131104 | tf_op jit(solution)/shard_map/ppermute | solution.py:326
  183.8 1.7 fusion.9.refs_0_
  185.4 14.0 %score.1 = (bf16[512,512]{1,0:T(8,128)(2,1)}, f32[32,256]{1,0:T(8,128)}) custom-call(f32[128,512]{1,0:T(8,128)} %fusion.9.refs_0_, f32[128,512]{1,0:T(8,128)} %get-tuple-element.60.refs_1_, f32[128,512]{1,0:T(8,128)} %fusion.5.refs_2_, f32[128,512]{1,0:T(8,128)} %get-tuple-element.58.refs_3_, s32[1,512]{1,0:T(1,128)} %bitcast.31, f32[1,512]{1,0:T(1,128)} %bitcast.33, ...), custom_call_target="tpu_custom_call" | custom-call | tf_op jit(solution)/shard_map/score/pallas_call | solution.py:475
  199.4 0.8 broadcast_in_dim.68
  200.2 0.1 select_reduce_fusion
  200.4 0.6 all_to_all.12
  201.0 28.0 %all_to_all.17 = f32[128,1,1024]{2,1,0:T(1,128)S(1)} all-to-all(f32[128,1,1024]{2,1,0:T(1,128)S(1)} %all_to_all.12), channel_id=1, replica_groups=mesh['neg'=16,'qry'=8] {'neg','qry'}, dimensions={0} | all-to-all | bytes 1048576 | tf_op jit(solution)/shard_map/all_to_all | solution.py:539
  229.1 0.3 reduce_max.9
  229.5 0.6 add_add_fusion
  (65 shorter events, 0.9 us)
Async XLA Ops:
  15.7 27.1 %all-to-all-start = ((s32[16,176,128]{2,1,0:T(8,128)}), s32[16,176,128]{2,1,0:T(8,128)S(1)}, u32[]{:S(2)}, u32[]{:S(2)}) async-start(s32[16,176,128]{2,1,0:T(8,128)} %broadcast_in_dim.63), calls=%async_computation | async-start | bytes 2883584 | tf_op jit(solution)/shard_map/all_to_all | solution.py:262
  42.7 1.2 copy-start
  87.7 16.3 %copy-start.14 = (bf16[4,128,512]{2,1,0:T(8,128)(2,1)S(1)}, bf16[4,128,512]{2,1,0:T(8,128)(2,1)}, u32[]{:S(2)}) copy-start(bf16[4,128,512]{2,1,0:T(8,128)(2,1)} %get-tuple-element.26) | copy-start | bytes 1572868
  87.7 16.4 %copy-start.7 = (bf16[4,128,512]{2,1,0:T(8,128)(2,1)S(1)}, bf16[4,128,512]{2,1,0:T(8,128)(2,1)}, u32[]{:S(2)}) copy-start(bf16[4,128,512]{2,1,0:T(8,128)(2,1)} %get-tuple-element.33) | copy-start | bytes 1572868
  87.7 12.1 %collective-permute-start.14 = (bf16[4,128,512]{2,1,0:T(8,128)(2,1)}, bf16[4,128,512]{2,1,0:T(8,128)(2,1)S(1)}, u32[]{:S(2)}, u32[]{:S(2)}) collective-permute-start(bf16[4,128,512]{2,1,0:T(8,128)(2,1)} %get-tuple-element.39), channel_id=1, source_target_pairs={{0,24},{8,0},{16,8},{24,16},{32,56},{40,32},{48,40},{56,48},{64,88... | collective-permute-start | bytes 1572872 | tf_op jit(solution)/shard_map/ppermute | solution.py:326
  90.2 13.8 %collective-permute-start.10 = (bf16[4,128,512]{2,1,0:T(8,128)(2,1)}, bf16[4,128,512]{2,1,0:T(8,128)(2,1)S(1)}, u32[]{:S(2)}, u32[]{:S(2)}) collective-permute-start(bf16[4,128,512]{2,1,0:T(8,128)(2,1)} %get-tuple-element.34), channel_id=1, source_target_pairs={{0,8},{8,16},{16,24},{24,0},{32,40},{40,48},{48,56},{56,32},{64,72... | collective-permute-start | bytes 1572872 | tf_op jit(solution)/shard_map/ppermute | solution.py:326
  90.2 37.5 %collective-permute-start.20 = (bf16[1024,512]{1,0:T(8,128)(2,1)}, bf16[1024,512]{1,0:T(8,128)(2,1)}, u32[]{:S(2)}, u32[]{:S(2)}) collective-permute-start(bf16[1024,512]{1,0:T(8,128)(2,1)} %refs_7_.1), channel_id=1, source_target_pairs={{0,2},{1,3},{2,4},{3,5},{4,6},{5,7},{6,0},{7,1},{8,10},{9,11},{10,... | collective-permute-start | bytes 3145736 | tf_op jit(solution)/shard_map/ppermute | solution.py:369
  91.9 22.8 %collective-permute-start.13 = (bf16[4,128,512]{2,1,0:T(8,128)(2,1)}, bf16[4,128,512]{2,1,0:T(8,128)(2,1)S(1)}, u32[]{:S(2)}, u32[]{:S(2)}) collective-permute-start(bf16[4,128,512]{2,1,0:T(8,128)(2,1)} %get-tuple-element.37), channel_id=1, source_target_pairs={{0,8},{8,16},{16,24},{24,0},{32,40},{40,48},{48,56},{56,32},{64,72... | collective-permute-start | bytes 1572872 | tf_op jit(solution)/shard_map/ppermute | solution.py:326
  92.6 32.5 %collective-permute-start.12 = (bf16[4,128,512]{2,1,0:T(8,128)(2,1)}, bf16[4,128,512]{2,1,0:T(8,128)(2,1)S(1)}, u32[]{:S(2)}, u32[]{:S(2)}) collective-permute-start(bf16[4,128,512]{2,1,0:T(8,128)(2,1)} %get-tuple-element.35), channel_id=1, source_target_pairs={{0,24},{8,0},{16,8},{24,16},{32,56},{40,32},{48,40},{56,48},{64,88... | collective-permute-start | bytes 1572872 | tf_op jit(solution)/shard_map/ppermute | solution.py:326
  99.8 9.4 %collective-permute-start.4 = (bf16[4,128,512]{2,1,0:T(8,128)(2,1)}, bf16[4,128,512]{2,1,0:T(8,128)(2,1)S(1)}, u32[]{:S(2)}, u32[]{:S(2)}) collective-permute-start(bf16[4,128,512]{2,1,0:T(8,128)(2,1)} %get-tuple-element.31), channel_id=1, source_target_pairs={{0,96},{8,104},{16,112},{24,120},{32,0},{40,8},{48,16},{56,24},{64... | collective-permute-start | bytes 1572872 | tf_op jit(solution)/shard_map/ppermute | solution.py:326
  102.8 11.5 %copy-start.6 = (bf16[4,128,512]{2,1,0:T(8,128)(2,1)S(1)}, bf16[4,128,512]{2,1,0:T(8,128)(2,1)}, u32[]{:S(2)}) copy-start(bf16[4,128,512]{2,1,0:T(8,128)(2,1)} %get-tuple-element.30) | copy-start | bytes 1572868
  104.0 10.4 %collective-permute-start = (bf16[4,128,512]{2,1,0:T(8,128)(2,1)S(1)}, bf16[4,128,512]{2,1,0:T(8,128)(2,1)S(1)}, u32[]{:S(2)}, u32[]{:S(2)}) collective-permute-start(bf16[4,128,512]{2,1,0:T(8,128)(2,1)S(1)} %copy-done.14), channel_id=1, source_target_pairs={{0,32},{8,40},{16,48},{24,56},{32,64},{40,72},{48,80},{56,88},{64,... | collective-permute-start | bytes 1572872 | tf_op jit(solution)/shard_map/ppermute | solution.py:326
  104.1 10.4 %copy-start.5 = (bf16[4,128,512]{2,1,0:T(8,128)(2,1)S(1)}, bf16[4,128,512]{2,1,0:T(8,128)(2,1)}, u32[]{:S(2)}) copy-start(bf16[4,128,512]{2,1,0:T(8,128)(2,1)} %get-tuple-element.25) | copy-start | bytes 1572868
  109.2 12.0 %collective-permute-start.15 = (bf16[4,128,512]{2,1,0:T(8,128)(2,1)S(1)}, bf16[4,128,512]{2,1,0:T(8,128)(2,1)S(1)}, u32[]{:S(2)}, u32[]{:S(2)}) collective-permute-start(bf16[4,128,512]{2,1,0:T(8,128)(2,1)S(1)} %add_convert_fusion), channel_id=1, source_target_pairs={{0,24},{8,0},{16,8},{24,16},{32,56},{40,32},{48,40},{56,48},{64,88... | collective-permute-start | bytes 1572872 | tf_op jit(solution)/shard_map/ppermute | solution.py:326
  114.3 1.0 copy-start.13
  114.3 6.9 %copy-start.12 = (bf16[4,128,512]{2,1,0:T(8,128)(2,1)S(1)}, bf16[4,128,512]{2,1,0:T(8,128)(2,1)}, u32[]{:S(2)}) copy-start(bf16[4,128,512]{2,1,0:T(8,128)(2,1)} %get-tuple-element.27) | copy-start | bytes 1572868
  114.3 10.5 %copy-start.11 = (bf16[4,128,512]{2,1,0:T(8,128)(2,1)S(1)}, bf16[4,128,512]{2,1,0:T(8,128)(2,1)}, u32[]{:S(2)}) copy-start(bf16[4,128,512]{2,1,0:T(8,128)(2,1)} %get-tuple-element.36) | copy-start | bytes 1572868
  114.5 11.6 %collective-permute-start.11 = (bf16[4,128,512]{2,1,0:T(8,128)(2,1)S(1)}, bf16[4,128,512]{2,1,0:T(8,128)(2,1)S(1)}, u32[]{:S(2)}, u32[]{:S(2)}) collective-permute-start(bf16[4,128,512]{2,1,0:T(8,128)(2,1)S(1)} %add_convert_fusion.1), channel_id=1, source_target_pairs={{0,8},{8,16},{16,24},{24,0},{32,40},{40,48},{48,56},{56,32},{64,72... | collective-permute-start | bytes 1572872 | tf_op jit(solution)/shard_map/ppermute | solution.py:326
  115.3 16.0 %collective-permute-start.3 = (bf16[4,128,512]{2,1,0:T(8,128)(2,1)S(1)}, bf16[4,128,512]{2,1,0:T(8,128)(2,1)S(1)}, u32[]{:S(2)}, u32[]{:S(2)}) collective-permute-start(bf16[4,128,512]{2,1,0:T(8,128)(2,1)S(1)} %copy-done.13), channel_id=1, source_target_pairs={{0,32},{8,40},{16,48},{24,56},{32,64},{40,72},{48,80},{56,88},{64,... | collective-permute-start | bytes 1572872 | tf_op jit(solution)/shard_map/ppermute | solution.py:326
  121.2 22.2 %collective-permute-start.2 = (bf16[4,128,512]{2,1,0:T(8,128)(2,1)S(1)}, bf16[4,128,512]{2,1,0:T(8,128)(2,1)S(1)}, u32[]{:S(2)}, u32[]{:S(2)}) collective-permute-start(bf16[4,128,512]{2,1,0:T(8,128)(2,1)S(1)} %copy-done.12), channel_id=1, source_target_pairs={{0,96},{8,104},{16,112},{24,120},{32,0},{40,8},{48,16},{56,24},{64... | collective-permute-start | bytes 1572872 | tf_op jit(solution)/shard_map/ppermute | solution.py:326
  124.8 1.8 copy-start.10
  125.0 1.8 copy-start.2
  125.0 17.2 %collective-permute-start.5 = (bf16[4,128,512]{2,1,0:T(8,128)(2,1)S(1)}, bf16[4,128,512]{2,1,0:T(8,128)(2,1)S(1)}, u32[]{:S(2)}, u32[]{:S(2)}) collective-permute-start(bf16[4,128,512]{2,1,0:T(8,128)(2,1)S(1)} %add_convert_fusion.2), channel_id=1, source_target_pairs={{0,96},{8,104},{16,112},{24,120},{32,0},{40,8},{48,16},{56,24},{64... | collective-permute-start | bytes 1572872 | tf_op jit(solution)/shard_map/ppermute | solution.py:326
  126.1 20.9 %collective-permute-start.1 = (bf16[4,128,512]{2,1,0:T(8,128)(2,1)S(1)}, bf16[4,128,512]{2,1,0:T(8,128)(2,1)S(1)}, u32[]{:S(2)}, u32[]{:S(2)}) collective-permute-start(bf16[4,128,512]{2,1,0:T(8,128)(2,1)S(1)} %add_convert_fusion.3), channel_id=1, source_target_pairs={{0,32},{8,40},{16,48},{24,56},{32,64},{40,72},{48,80},{56,88},{64,... | collective-permute-start | bytes 1572872 | tf_op jit(solution)/shard_map/ppermute | solution.py:326
  126.8 16.6 %copy-start.1 = (bf16[4,128,512]{2,1,0:T(8,128)(2,1)}, bf16[4,128,512]{2,1,0:T(8,128)(2,1)S(1)}, u32[]{:S(2)}) copy-start(bf16[4,128,512]{2,1,0:T(8,128)(2,1)S(1)} %get-tuple-element.42) | copy-start | bytes 1572868
  126.8 15.4 %copy-start.9 = (bf16[4,128,512]{2,1,0:T(8,128)(2,1)S(1)}, bf16[4,128,512]{2,1,0:T(8,128)(2,1)}, u32[]{:S(2)}) copy-start(bf16[4,128,512]{2,1,0:T(8,128)(2,1)} %get-tuple-element.28) | copy-start | bytes 1572868
  127.7 28.6 %collective-permute-start.22 = (bf16[1024,512]{1,0:T(8,128)(2,1)}, bf16[1024,512]{1,0:T(8,128)(2,1)}, u32[]{:S(2)}, u32[]{:S(2)}) collective-permute-start(bf16[1024,512]{1,0:T(8,128)(2,1)} %refs_7_.1), channel_id=1, source_target_pairs={{0,6},{1,7},{2,0},{3,1},{4,2},{5,3},{6,4},{7,5},{8,14},{9,15},{10,... | collective-permute-start | bytes 3145736 | tf_op jit(solution)/shard_map/ppermute | solution.py:369
  131.4 32.0 %collective-permute-start.21 = (bf16[1024,512]{1,0:T(8,128)(2,1)}, bf16[1024,512]{1,0:T(8,128)(2,1)}, u32[]{:S(2)}, u32[]{:S(2)}) collective-permute-start(bf16[1024,512]{1,0:T(8,128)(2,1)} %collective-permute-done.20.refs_8_), channel_id=1, source_target_pairs={{0,2},{1,3},{2,4},{3,5},{4,6},{5,7},{6,0},{7,1},{8,10},{9,11},{10,... | collective-permute-start | bytes 3145736 | tf_op jit(solution)/shard_map/ppermute | solution.py:369
  142.2 21.3 %collective-permute-start.16 = (bf16[2,128,512]{2,1,0:T(8,128)(2,1)}, bf16[2,128,512]{2,1,0:T(8,128)(2,1)}, u32[]{:S(2)}, u32[]{:S(2)}) collective-permute-start(bf16[2,128,512]{2,1,0:T(8,128)(2,1)} %pad_maximum_fusion.2), channel_id=1, source_target_pairs={{0,32},{8,40},{16,48},{24,56},{32,64},{40,72},{48,80},{56,88},{64,... | collective-permute-start | bytes 786440 | tf_op jit(solution)/shard_map/ppermute | solution.py:326
  142.2 4.8 %copy-start.8 = (bf16[4,128,512]{2,1,0:T(8,128)(2,1)S(1)}, bf16[4,128,512]{2,1,0:T(8,128)(2,1)}, u32[]{:S(2)}) copy-start(bf16[4,128,512]{2,1,0:T(8,128)(2,1)} %get-tuple-element.24) | copy-start | bytes 1572868
  143.4 3.9 %copy-start.4 = (bf16[4,128,512]{2,1,0:T(8,128)(2,1)}, bf16[4,128,512]{2,1,0:T(8,128)(2,1)S(1)}, u32[]{:S(2)}) copy-start(bf16[4,128,512]{2,1,0:T(8,128)(2,1)S(1)} %get-tuple-element.48) | copy-start | bytes 1572868
  143.4 7.1 %collective-permute-start.18 = (bf16[2,128,512]{2,1,0:T(8,128)(2,1)S(1)}, bf16[2,128,512]{2,1,0:T(8,128)(2,1)S(1)}, u32[]{:S(2)}, u32[]{:S(2)}) collective-permute-start(bf16[2,128,512]{2,1,0:T(8,128)(2,1)S(1)} %pad_maximum_fusion.3), channel_id=1, source_target_pairs={{0,96},{8,104},{16,112},{24,120},{32,0},{40,8},{48,16},{56,24},{64... | collective-permute-start | bytes 786440 | tf_op jit(solution)/shard_map/ppermute | solution.py:326
  147.3 0.8 copy-start.3
  148.8 15.0 %collective-permute-start.6 = (bf16[2,128,512]{2,1,0:T(8,128)(2,1)}, bf16[2,128,512]{2,1,0:T(8,128)(2,1)}, u32[]{:S(2)}, u32[]{:S(2)}) collective-permute-start(bf16[2,128,512]{2,1,0:T(8,128)(2,1)} %pad_maximum_fusion), channel_id=1, source_target_pairs={{0,8},{8,16},{16,24},{24,0},{32,40},{40,48},{48,56},{56,32},{64,72... | collective-permute-start | bytes 786440 | tf_op jit(solution)/shard_map/ppermute | solution.py:326
  150.5 13.4 %collective-permute-start.8 = (bf16[2,128,512]{2,1,0:T(8,128)(2,1)}, bf16[2,128,512]{2,1,0:T(8,128)(2,1)}, u32[]{:S(2)}, u32[]{:S(2)}) collective-permute-start(bf16[2,128,512]{2,1,0:T(8,128)(2,1)} %pad_maximum_fusion.1), channel_id=1, source_target_pairs={{0,24},{8,0},{16,8},{24,16},{32,56},{40,32},{48,40},{56,48},{64,88... | collective-permute-start | bytes 786440 | tf_op jit(solution)/shard_map/ppermute | solution.py:326
  156.3 29.1 %collective-permute-start.23 = (bf16[1024,512]{1,0:T(8,128)(2,1)}, bf16[1024,512]{1,0:T(8,128)(2,1)}, u32[]{:S(2)}, u32[]{:S(2)}) collective-permute-start(bf16[1024,512]{1,0:T(8,128)(2,1)} %refs_7_.1), channel_id=1, source_target_pairs={{0,1},{1,0},{2,3},{3,2},{4,5},{5,4},{6,7},{7,6},{8,9},{9,8},{10,11... | collective-permute-start | bytes 3145736 | tf_op jit(solution)/shard_map/ppermute | solution.py:369
  163.4 22.1 %collective-permute-start.24 = (bf16[1024,512]{1,0:T(8,128)(2,1)}, bf16[1024,512]{1,0:T(8,128)(2,1)}, u32[]{:S(2)}, u32[]{:S(2)}) collective-permute-start(bf16[1024,512]{1,0:T(8,128)(2,1)} %collective-permute-done.20.refs_8_), channel_id=1, source_target_pairs={{0,1},{1,0},{2,3},{3,2},{4,5},{5,4},{6,7},{7,6},{8,9},{9,8},{10,11... | collective-permute-start | bytes 3145736 | tf_op jit(solution)/shard_map/ppermute | solution.py:369
  163.5 22.0 %collective-permute-start.26 = (bf16[1024,512]{1,0:T(8,128)(2,1)}, bf16[1024,512]{1,0:T(8,128)(2,1)}, u32[]{:S(2)}, u32[]{:S(2)}) collective-permute-start(bf16[1024,512]{1,0:T(8,128)(2,1)} %collective-permute-done.22.refs_10_), channel_id=1, source_target_pairs={{0,1},{1,0},{2,3},{3,2},{4,5},{5,4},{6,7},{7,6},{8,9},{9,8},{10,11... | collective-permute-start | bytes 3145736 | tf_op jit(solution)/shard_map/ppermute | solution.py:369
  163.9 21.5 %collective-permute-start.25 = (bf16[1024,512]{1,0:T(8,128)(2,1)}, bf16[1024,512]{1,0:T(8,128)(2,1)}, u32[]{:S(2)}, u32[]{:S(2)}) collective-permute-start(bf16[1024,512]{1,0:T(8,128)(2,1)} %collective-permute-done.21.refs_9_), channel_id=1, source_target_pairs={{0,1},{1,0},{2,3},{3,2},{4,5},{5,4},{6,7},{7,6},{8,9},{9,8},{10,11... | collective-permute-start | bytes 3145736 | tf_op jit(solution)/shard_map/ppermute | solution.py:369
  164.0 5.4 %collective-permute-start.19 = (bf16[1,128,512]{2,1,0:T(8,128)(2,1)S(1)}, bf16[1,128,512]{2,1,0:T(8,128)(2,1)S(1)}, u32[]{:S(2)}, u32[]{:S(2)}) collective-permute-start(bf16[1,128,512]{2,1,0:T(8,128)(2,1)S(1)} %add_convert_fusion.4), channel_id=1, source_target_pairs={{0,96},{8,104},{16,112},{24,120},{32,0},{40,8},{48,16},{56,24},{64... | collective-permute-start | bytes 393224 | tf_op jit(solution)/shard_map/ppermute | solution.py:326
  169.4 3.8 %collective-permute-start.9 = (bf16[1,128,512]{2,1,0:T(8,128)(2,1)S(1)}, bf16[1,128,512]{2,1,0:T(8,128)(2,1)S(1)}, u32[]{:S(2)}, u32[]{:S(2)}) collective-permute-start(bf16[1,128,512]{2,1,0:T(8,128)(2,1)S(1)} %add_convert_fusion.6), channel_id=1, source_target_pairs={{0,24},{8,0},{16,8},{24,16},{32,56},{40,32},{48,40},{56,48},{64,88... | collective-permute-start | bytes 393224 | tf_op jit(solution)/shard_map/ppermute | solution.py:326
  173.2 5.4 %collective-permute-start.17 = (bf16[1,128,512]{2,1,0:T(8,128)(2,1)S(1)}, bf16[1,128,512]{2,1,0:T(8,128)(2,1)S(1)}, u32[]{:S(2)}, u32[]{:S(2)}) collective-permute-start(bf16[1,128,512]{2,1,0:T(8,128)(2,1)S(1)} %get-tuple-element.59), channel_id=1, source_target_pairs={{0,32},{8,40},{16,48},{24,56},{32,64},{40,72},{48,80},{56,88},{64,... | collective-permute-start | bytes 393224 | tf_op jit(solution)/shard_map/ppermute | solution.py:326
  178.6 5.2 %collective-permute-start.7 = (bf16[1,128,512]{2,1,0:T(8,128)(2,1)S(1)}, bf16[1,128,512]{2,1,0:T(8,128)(2,1)S(1)}, u32[]{:S(2)}, u32[]{:S(2)}) collective-permute-start(bf16[1,128,512]{2,1,0:T(8,128)(2,1)S(1)} %get-tuple-element.61), channel_id=1, source_target_pairs={{0,8},{8,16},{16,24},{24,0},{32,40},{40,48},{48,56},{56,32},{64,72... | collective-permute-start | bytes 393224 | tf_op jit(solution)/shard_map/ppermute | solution.py:326

commit v2 on v1

--- a/solution.py
+++ b/solution.py
@@ -1,3 +1,4 @@
+import functools
 import math
 
 import jax
@@ -404,31 +405,33 @@
     )(items_table, message_weight, message_bias[None, :], neighbour_weight, self_weight)
 
 
-def score_kernel(*refs):
-    sums = refs[:4]
-    count_ref, bias_ref, log_ref = refs[4:7]
-    queries = refs[7 : 7 + 2 * SIDE]
-    embed_ref, lse_ref, held, even, odd, logs, sems = refs[7 + 2 * SIDE :]
+def score_kernel(*refs, first, many):
+    sums = refs[:2]
+    place_ref, count_ref, bias_ref, log_ref, earlier_ref = refs[2:7]
+    queries = refs[7 : 7 + many]
+    embed_ref, lse_ref, held, even, odd, logs, sems = refs[7 + many :]
     f32 = jnp.float32
     rows = queries[0].shape[0]
-    blocks = len(queries) * rows // SCORED
+    blocks = many * rows // SCORED
     per_query = rows // SCORED
+    negatives, width = embed_ref.shape
+    here = slice(first, first + negatives)
 
     def copy(j, source):
         return pltpu.make_async_copy(source, held.at[pl.ds(j * rows, rows), :], sems.at[j])
 
     for j, source in enumerate(queries):
         copy(j, source).start()
-    negatives, width = embed_ref.shape
 
     def columns(row):
         return jnp.broadcast_to(row, (LANES, negatives)).T
 
-    logs[...] = columns(jnp.log(log_ref[...].astype(f32)) * LOG2E)
-    counts = columns(count_ref[...].astype(f32))
-    quarter = negatives // 4
-    for q in range(4):
-        at = slice(q * quarter, (q + 1) * quarter)
+    own = log_ref[pl.ds(place_ref[0], 1), :][:, here]
+    logs[...] = columns(jnp.log(own.astype(f32)) * LOG2E)
+    counts = columns(count_ref[:, here].astype(f32))
+    half = negatives // 2
+    for q in range(2):
+        at = slice(q * half, (q + 1) * half)
         count = jnp.concatenate([counts[at, :]] * (width // LANES), axis=1)
         hidden = jnp.maximum(sums[q][...] / count + bias_ref[...], 0.0)
         scale_inv = lax.rsqrt(jnp.mean(hidden * hidden, axis=-1, keepdims=True) + 0.25)
@@ -446,7 +449,12 @@
             peak = jnp.max(scores, axis=0, keepdims=True)
             total = jnp.sum(jnp.exp2(scores - peak), axis=0, keepdims=True)
             found.append((peak + jnp.log2(total)) * (1.0 / LOG2E))
-        lse_ref[pl.ds(i, 1), :] = jnp.concatenate(found, axis=1)
+        found = jnp.concatenate(found, axis=1)
+        if earlier_ref is not None:
+            other = earlier_ref[pl.ds(i, 1), :]
+            peak = jnp.maximum(found, other)
+            found = peak + jnp.log(jnp.exp(found - peak) + jnp.exp(other - peak))
+        lse_ref[pl.ds(i, 1), :] = found
 
     copy(0, queries[0]).wait()
     even[...] = products(0)
@@ -467,14 +475,26 @@
     lax.fori_loop(0, blocks // 2, pair, 0)
 
 
-def scored(sums, count, bias, own_count, queries):
-    negatives = count.shape[0]
+def scored(sums, first, place, count, bias, counts_all, earlier, queries):
+    negatives = 2 * sums[0].shape[0]
     rows, width = queries[0].shape
-    total = rows * len(queries)
+    many = len(queries)
+    total = rows * many
     in_vmem = pl.BlockSpec(memory_space=pltpu.VMEM)
+    kernel = functools.partial(score_kernel, first=first, many=many)
+    if earlier is None:
+        body = kernel
+
+        def kernel(*refs):
+            return body(*refs[:6], None, *refs[6:])
+
+    extra = [] if earlier is None else [earlier]
     return pl.pallas_call(
-        score_kernel,
-        in_specs=[in_vmem] * 7 + [pl.BlockSpec(memory_space=pl.ANY)] * len(queries),
+        kernel,
+        in_specs=[in_vmem] * 2
+        + [pl.BlockSpec(memory_space=pltpu.SMEM)]
+        + [in_vmem] * (3 + len(extra))
+        + [pl.BlockSpec(memory_space=pl.ANY)] * many,
         out_specs=[in_vmem] * 2,
         out_shape=[
             jax.ShapeDtypeStruct((negatives, width), jnp.bfloat16),
@@ -485,10 +505,10 @@
             pltpu.VMEM((negatives, SCORED), jnp.float32),
             pltpu.VMEM((negatives, SCORED), jnp.float32),
             pltpu.VMEM((negatives, LANES), jnp.float32),
-            pltpu.SemaphoreType.DMA((len(queries),)),
+            pltpu.SemaphoreType.DMA((many,)),
         ],
         name="score",
-    )(*sums, count[None, :], bias[None, :], own_count[None, :], *queries)
+    )(*sums, place, count, bias[None, :], counts_all, *extra, *queries)
 
 
 def per_device(
@@ -521,14 +541,16 @@
 
     message_part, self_part = tables(items_table, message_weight, message_bias, neighbour_weight, self_weight)
 
-    own_count = lax.dynamic_slice(negative_count, (lax.axis_index("qry") * negatives,), (negatives,))
     place = lax.axis_index("neg")
     part = jnp.stack([place // SIDE, place % SIDE]).astype(jnp.int32)
     outs = owner_sums(part, lists[:, keys.size // LANES, :parts], lists, message_part, self_part, negatives)
     sums = [q[0] for q in scattered_sums(outs)]
 
-    negative_embed, part_lse = scored(sums, neighbour_count, output_bias, own_count, query_blocks)
     here = lax.axis_index("qry")
+    whole = (here.reshape(1), neighbour_count[None, :], output_bias, negative_count.reshape(groups, negatives))
+    early_embed, early_lse = scored(sums[:2], 0, *whole, None, query_blocks)
+    late_embed, part_lse = scored(sums[2:], negatives // 2, *whole, early_lse, query_blocks)
+    negative_embed = jnp.concatenate([early_embed, late_embed], axis=0)
     z, core = here // 2, here % 2
     group = jnp.arange(groups)
     source = ((z - group // 2) % SIDE) + SIDE * ((group % 2) ^ core)

time: 231 us -> 241 us (1.043)
  blocking collectives: 28 us -> 0 us
  starting transfers between devices: 49.3 us -> 66.9 us
  waiting for transfers between devices: 40.5 us -> 47.2 us
  Pallas kernels: 77.6 us -> 84.1 us
  other arithmetic: 27 us -> 32.1 us
  local copies, waits for them, and re-layouts: 6.69 us -> 9.11 us
    all_to_all x1 -> x0, blocking collectives: 28 us -> none  [per_device(): lax.all_to_all(shared.reshape(parts * groups, -1), ('neg', 'qry'), split_...]
    all_to_all x0 -> x1, starting transfers between devices: none -> 15.7 us  [per_device(): lax.all_to_all(shared.reshape(parts * groups, -1), ('neg', 'qry'), split_...]
    all_to_all x0 -> x1, waiting for transfers between devices: none -> 12.7 us  [per_device(): lax.all_to_all(shared.reshape(parts * groups, -1), ('neg', 'qry'), split_...]
    pallas_call x1 -> x2, Pallas kernels: 14 us -> 20.4 us  [scored(): pl.pallas_call(kernel, in_specs=[in_vmem] * 2 + [pl.BlockSpec(memory_spac...]
    ppermute x20, waiting for transfers between devices: 38.9 us -> 32.9 us  [moved(): return lax.ppermute(x, 'neg', [(i, place(i)) for i in range(SIDE * SIDE)])]
  transfers between devices with their start and end apart: 28 -> 29, of which waited for: 11 -> 12; matrix products, arithmetic and copies ran while one was open for 7% -> 8% of each run, Pallas kernels for 7% -> 7%
where the time goes in v2:
time: 241 us; the launch traced here: 240 us
  Pallas kernels  84.1 us (35%)
  starting transfers between devices  66.9 us (28%)
  waiting for transfers between devices  47.2 us (20%)
  other arithmetic  32.1 us (13%)
  local copies, waits for them, and re-layouts  9.11 us (4%)
    pallas_call x1, Pallas kernels, owner_sums(): pl.pallas_call(owner_kernel, grid=(devices,), in_specs=[pl.BlockSpec(memo...  43.9 us
    ppermute x20, waiting for transfers between devices, moved(): return lax.ppermute(x, 'neg', [(i, place(i)) for i in range(SIDE * SIDE)])  32.9 us
    ppermute x20, starting transfers between devices, moved(): return lax.ppermute(x, 'neg', [(i, place(i)) for i in range(SIDE * SIDE)])  28.5 us
    pallas_call x2, Pallas kernels, scored(): pl.pallas_call(kernel, in_specs=[in_vmem] * 2 + [pl.BlockSpec(memory_spac...  20.4 us
    pallas_call x1, Pallas kernels, tables(): pl.pallas_call(table_kernel, grid=(items // STAGE,), in_specs=[block, wei...  17.2 us
    all_to_all x1, starting transfers between devices, per_device(): lax.all_to_all(shared.reshape(parts * groups, -1), ('neg', 'qry'), split_...  15.7 us
    ppermute x7, starting transfers between devices, turned(): return lax.ppermute(x, 'qry', [(i, place(i)) for i in range(2 * SIDE)])  15.1 us
    all_to_all x1, waiting for transfers between devices, per_device(): lax.all_to_all(shared.reshape(parts * groups, -1), ('neg', 'qry'), split_...  12.7 us
  transfers between devices with their start and end apart: 29, of which 12 were waited for; matrix products, arithmetic and copies ran while one was open for 8% of the time, Pallas kernels for 7%

profile of v2, /device:TPU:1, one launch (start us, length us, event | category | flops | bytes accessed | tf_op | source)
XLA Modules:
  0.0 240.4 jit_solution(8910318930191846482)
XLA Ops:
  0.6 2.6 %compose.1 = s32[164,128]{1,0:T(8,128)} custom-call(s32[40,512]{1,0:T(8,128)} %bitcast.28, s32[1,512]{1,0:T(1,128)} %bitcast.35, s32[1,512]{1,0:T(1,128)} %bitcast.30, s32[16,640]{1,0:T(8,128)} %fetch_ref.1), custom_call_target="tpu_custom_call" | custom-call | tf_op jit(solution)/shard_map/compose/pallas_call | solution.py:269
  3.2 9.3 %sort.7 = s32[20992]{0:T(1024)S(1)} sort(s32[20992]{0:T(1024)} %bitcast.26), dimensions={0}, to_apply=%region_0.0 | sort | flops 314880 | bytes 167936 | tf_op jit(solution)/shard_map/sort | solution.py:536
  12.5 1.2 convert_reduce_fusion
  13.7 0.7 fusion.12
  14.4 1.2 broadcast_in_dim.61
  15.7 7.6 %all-to-all-start = ((s32[16,176,128]{2,1,0:T(8,128)}), s32[16,176,128]{2,1,0:T(8,128)S(1)}, u32[]{:S(2)}, u32[]{:S(2)}) async-start(s32[16,176,128]{2,1,0:T(8,128)} %broadcast_in_dim.61), calls=%async_computation | async-start | bytes 2883584 | tf_op jit(solution)/shard_map/all_to_all | solution.py:263
  23.3 17.2 %tables.1 = (bf16[8192,512]{1,0:T(8,128)(2,1)}, bf16[8192,512]{1,0:T(8,128)(2,1)}) custom-call(bf16[8192,512]{1,0:T(8,128)(2,1)} %items_ref.1, bf16[512,512]{1,0:T(8,128)(2,1)} %message_ref.1, f32[1,512]{1,0:T(1,128)} %bitcast.36, bf16[512,512]{1,0:T(8,128)(2,1)} %neighbour_ref.1, bf16[512,512]{1,0:T(8,128)(2,1)} %self_ref.1), custom_call_target="tpu_custom_call" | custom-call | tf_op jit(solution)/shard_map/tables/pallas_call | solution.py:397
  40.5 0.7 pad_add_fusion.1.part_ref
  41.1 1.6 all-to-all-done.lists_ref
  42.7 0.6 slice.100
  43.4 0.5 copy-done
  43.8 43.9 %owner.1 = (bf16[4,128,512]{2,1,0:T(8,128)(2,1)}, bf16[4,128,512]{2,1,0:T(8,128)(2,1)}, bf16[4,128,512]{2,1,0:T(8,128)(2,1)}, bf16[4,128,512]{2,1,0:T(8,128)(2,1...) custom-call(s32[2]{0:T(128)} %pad_add_fusion.1.part_ref, ...), custom_call_target="tpu_custom_call" | custom-call | tf_op jit(solution)/shard_map/owner/pallas_call | solution.py:286
  87.8 2.7 %collective-permute-start.4 = (bf16[4,128,512]{2,1,0:T(8,128)(2,1)}, bf16[4,128,512]{2,1,0:T(8,128)(2,1)}, u32[]{:S(2)}, u32[]{:S(2)}) collective-permute-start(bf16[4,128,512]{2,1,0:T(8,128)(2,1)} %get-tuple-element.33), channel_id=1, source_target_pairs={{0,96},{8,104},{16,112},{24,120},{32,0},{40,8},{48,16},{56,24},{64... | collective-permute-start | bytes 1572872 | tf_op jit(solution)/shard_map/ppermute | solution.py:327
  90.5 1.7 collective-permute-start.10
  92.3 2.7 %collective-permute-start.2 = (bf16[4,128,512]{2,1,0:T(8,128)(2,1)}, bf16[4,128,512]{2,1,0:T(8,128)(2,1)S(1)}, u32[]{:S(2)}, u32[]{:S(2)}) collective-permute-start(bf16[4,128,512]{2,1,0:T(8,128)(2,1)} %get-tuple-element.29), channel_id=1, source_target_pairs={{0,96},{8,104},{16,112},{24,120},{32,0},{40,8},{48,16},{56,24},{64... | collective-permute-start | bytes 1572872 | tf_op jit(solution)/shard_map/ppermute | solution.py:327
  95.1 4.1 %collective-permute-done.4 = bf16[4,128,512]{2,1,0:T(8,128)(2,1)} collective-permute-done((bf16[4,128,512]{2,1,0:T(8,128)(2,1)}, bf16[4,128,512]{2,1,0:T(8,128)(2,1)}, u32[]{:S(2)}, u32[]{:S(2)}) %collective-permute-start.4) | collective-permute-done | bytes 524320 | tf_op jit(solution)/shard_map/ppermute | solution.py:327
  99.2 3.7 %collective-permute-start.21 = (bf16[4,128,512]{2,1,0:T(8,128)(2,1)}, bf16[4,128,512]{2,1,0:T(8,128)(2,1)S(1)}, u32[]{:S(2)}, u32[]{:S(2)}) collective-permute-start(bf16[4,128,512]{2,1,0:T(8,128)(2,1)} %get-tuple-element.42), channel_id=1, source_target_pairs={{0,24},{8,0},{16,8},{24,16},{32,56},{40,32},{48,40},{56,48},{64,88... | collective-permute-start | bytes 1572872 | tf_op jit(solution)/shard_map/ppermute | solution.py:327
  102.9 1.4 add_convert_fusion.2
  104.5 5.6 %collective-permute-done.21 = bf16[4,128,512]{2,1,0:T(8,128)(2,1)S(1)} collective-permute-done((bf16[4,128,512]{2,1,0:T(8,128)(2,1)}, bf16[4,128,512]{2,1,0:T(8,128)(2,1)S(1)}, u32[]{:S(2)}, u32[]{:S(2)}) %collective-permute-start.21) | collective-permute-done | bytes 524320 | tf_op jit(solution)/shard_map/ppermute | solution.py:327
  110.1 4.2 %collective-permute-start.5 = (bf16[4,128,512]{2,1,0:T(8,128)(2,1)S(1)}, bf16[4,128,512]{2,1,0:T(8,128)(2,1)S(1)}, u32[]{:S(2)}, u32[]{:S(2)}) collective-permute-start(bf16[4,128,512]{2,1,0:T(8,128)(2,1)S(1)} %add_convert_fusion.2), channel_id=1, source_target_pairs={{0,96},{8,104},{16,112},{24,120},{32,0},{40,8},{48,16},{56,24},{64... | collective-permute-start | bytes 1572872 | tf_op jit(solution)/shard_map/ppermute | solution.py:327
  114.7 0.6 copy-done.23
  115.3 5.4 %collective-permute-done.5 = bf16[4,128,512]{2,1,0:T(8,128)(2,1)S(1)} collective-permute-done((bf16[4,128,512]{2,1,0:T(8,128)(2,1)S(1)}, bf16[4,128,512]{2,1,0:T(8,128)(2,1)S(1)}, u32[]{:S(2)}, u32[]{:S(2)}) %collective-permute-start.5) | collective-permute-done | bytes 524320 | tf_op jit(solution)/shard_map/ppermute | solution.py:327
  120.8 3.7 %collective-permute-start.19 = (bf16[4,128,512]{2,1,0:T(8,128)(2,1)S(1)}, bf16[4,128,512]{2,1,0:T(8,128)(2,1)S(1)}, u32[]{:S(2)}, u32[]{:S(2)}) collective-permute-start(bf16[4,128,512]{2,1,0:T(8,128)(2,1)S(1)} %copy-done.22), channel_id=1, source_target_pairs={{0,24},{8,0},{16,8},{24,16},{32,56},{40,32},{48,40},{56,48},{64,88... | collective-permute-start | bytes 1572872 | tf_op jit(solution)/shard_map/ppermute | solution.py:327
  124.4 1.2 fusion.19
  126.0 1.2 collective-permute-start.18
  127.2 1.2 fusion.18
  128.4 0.7 pad_maximum_fusion.1
  129.2 4.2 %collective-permute-start.12 = (bf16[1024,512]{1,0:T(8,128)(2,1)S(1)}, bf16[1024,512]{1,0:T(8,128)(2,1)S(1)}, u32[]{:S(2)}, u32[]{:S(2)}) collective-permute-start(bf16[1024,512]{1,0:T(8,128)(2,1)S(1)} %copy-done.1), channel_id=1, source_target_pairs={{0,6},{1,7},{2,0},{3,1},{4,2},{5,3},{6,4},{7,5},{8,14},{9,15},{10,... | collective-permute-start | bytes 3145736 | tf_op jit(solution)/shard_map/ppermute | solution.py:370
  133.4 8.2 %collective-permute-done.22 = bf16[4,128,512]{2,1,0:T(8,128)(2,1)S(1)} collective-permute-done((bf16[4,128,512]{2,1,0:T(8,128)(2,1)S(1)}, bf16[4,128,512]{2,1,0:T(8,128)(2,1)S(1)}, u32[]{:S(2)}, u32[]{:S(2)}) %collective-permute-start.22) | collective-permute-done | bytes 524320 | tf_op jit(solution)/shard_map/ppermute | solution.py:327
  141.6 1.2 fusion.21
  142.9 3.5 %collective-permute-start.8 = (bf16[2,128,512]{2,1,0:T(8,128)(2,1)S(1)}, bf16[2,128,512]{2,1,0:T(8,128)(2,1)S(1)}, u32[]{:S(2)}, u32[]{:S(2)}) collective-permute-start(bf16[2,128,512]{2,1,0:T(8,128)(2,1)S(1)} %pad_maximum_fusion.2), channel_id=1, source_target_pairs={{0,24},{8,0},{16,8},{24,16},{32,56},{40,32},{48,40},{56,48},{64,88... | collective-permute-start | bytes 786440 | tf_op jit(solution)/shard_map/ppermute | solution.py:327
  146.4 1.2 fusion.20
  147.6 0.8 copy-done.10
  148.5 0.7 pad_maximum_fusion.3
  149.2 0.7 pad_maximum_fusion.4
  150.2 3.4 %collective-permute-start.25 = (bf16[2,128,512]{2,1,0:T(8,128)(2,1)}, bf16[2,128,512]{2,1,0:T(8,128)(2,1)}, u32[]{:S(2)}, u32[]{:S(2)}) collective-permute-start(bf16[2,128,512]{2,1,0:T(8,128)(2,1)} %pad_maximum_fusion.4), channel_id=1, source_target_pairs={{0,96},{8,104},{16,112},{24,120},{32,0},{40,8},{48,16},{56,24},{64... | collective-permute-start | bytes 786440 | tf_op jit(solution)/shard_map/ppermute | solution.py:327
  153.7 0.6 reshape.80.refs_5_
  154.3 0.9 add_convert_fusion.6
  155.3 7.3 %collective-permute-start.13 = (bf16[1024,512]{1,0:T(8,128)(2,1)S(1)}, bf16[1024,512]{1,0:T(8,128)(2,1)S(1)}, u32[]{:S(2)}, u32[]{:S(2)}) collective-permute-start(bf16[1024,512]{1,0:T(8,128)(2,1)S(1)} %copy-done.1), channel_id=1, source_target_pairs={{0,1},{1,0},{2,3},{3,2},{4,5},{5,4},{6,7},{7,6},{8,9},{9,8},{10,11... | collective-permute-start | bytes 3145736 | tf_op jit(solution)/shard_map/ppermute | solution.py:370
  162.6 0.4 collective-permute-start.16
  163.1 1.4 collective-permute-start.15
  164.4 2.1 collective-permute-start.9
  166.6 1.0 add_convert_fusion.4
  167.6 1.3 collective-permute-done.9
  168.9 1.1 collective-permute-start.26
  170.0 1.9 fusion.7
  171.9 0.8 collective-permute-done.26
  172.7 1.9 fusion.3
  174.6 3.2 %collective-permute-done.7 = bf16[1,128,512]{2,1,0:T(8,128)(2,1)S(1)} collective-permute-done((bf16[1,128,512]{2,1,0:T(8,128)(2,1)S(1)}, bf16[1,128,512]{2,1,0:T(8,128)(2,1)S(1)}, u32[]{:S(2)}, u32[]{:S(2)}) %collective-permute-start.7) | collective-permute-done | bytes 131104 | tf_op jit(solution)/shard_map/ppermute | solution.py:327
  177.8 1.7 fusion.9.refs_0_
  179.5 3.6 %collective-permute-done.24 = bf16[1,128,512]{2,1,0:T(8,128)(2,1)S(1)} collective-permute-done((bf16[1,128,512]{2,1,0:T(8,128)(2,1)S(1)}, bf16[1,128,512]{2,1,0:T(8,128)(2,1)S(1)}, u32[]{:S(2)}, u32[]{:S(2)}) %collective-permute-start.24) | collective-permute-done | bytes 131104 | tf_op jit(solution)/shard_map/ppermute | solution.py:327
  183.1 1.8 fusion.5.refs_0_
  184.9 0.9 copy-done.4
  186.2 0.6 copy-done.6
  186.8 0.4 copy-done.7
  187.2 9.9 %score.2 = (bf16[256,512]{1,0:T(8,128)(2,1)}, f32[32,256]{1,0:T(8,128)}) custom-call(f32[128,512]{1,0:T(8,128)} %fusion.9.refs_0_, f32[128,512]{1,0:T(8,128)} %get-tuple-element.62.refs_1_, s32[1]{0:T(128)} %bitcast.11.refs_2_, s32[1,512]{1,0:T(1,128)} %bitcast.31, f32[1,512]{1,0:T(1,128)} %bitcast.33, s32[8,512]{1,0:T(8,128)} %reshape.80.refs_5_, ...), custom_call_target="tpu_custom_call" | custom-call | tf_op jit(solution)/shard_map/score/pallas_call | solution.py:492
  197.1 10.5 %score.3 = (bf16[256,512]{1,0:T(8,128)(2,1)}, f32[32,256]{1,0:T(8,128)}) custom-call(f32[128,512]{1,0:T(8,128)} %fusion.5.refs_0_, f32[128,512]{1,0:T(8,128)} %get-tuple-element.64.refs_1_, s32[1]{0:T(128)} %bitcast.11.refs_2_, s32[1,512]{1,0:T(1,128)} %bitcast.32, f32[1,512]{1,0:T(1,128)} %bitcast.34, s32[8,512]{1,0:T(8,128)} %reshape.80.refs_5_, ...), custom_call_target="tpu_custom_call" | custom-call | tf_op jit(solution)/shard_map/score/pallas_call | solution.py:492
  207.6 0.8 broadcast_in_dim.65
  208.7 1.4 all_to_all.12
  210.1 15.7 %all-to-all-start.1 = ((f32[128,1,1024]{2,1,0:T(1,128)}), f32[128,1,1024]{2,1,0:T(1,128)S(1)}, u32[]{:S(2)}, u32[]{:S(2)}) async-start(f32[128,1,1024]{2,1,0:T(1,128)} %all_to_all.12), calls=%async_computation.1 | async-start | bytes 1048576 | tf_op jit(solution)/shard_map/all_to_all | solution.py:561
  225.8 0.8 pad_maximum_fusion
  226.6 12.7 %all-to-all-done.1 = f32[128,1,1024]{2,1,0:T(1,128)S(1)} async-done(((f32[128,1,1024]{2,1,0:T(1,128)}), f32[128,1,1024]{2,1,0:T(1,128)S(1)}, u32[]{:S(2)}, u32[]{:S(2)}) %all-to-all-start.1) | async-done | bytes 524320 | tf_op jit(solution)/shard_map/all_to_all | solution.py:561
  239.3 0.3 reduce_max.9
  239.8 0.6 add_add_fusion
  (88 shorter events, 2.3 us)
Async XLA Ops:
  15.7 27.1 %all-to-all-start = ((s32[16,176,128]{2,1,0:T(8,128)}), s32[16,176,128]{2,1,0:T(8,128)S(1)}, u32[]{:S(2)}, u32[]{:S(2)}) async-start(s32[16,176,128]{2,1,0:T(8,128)} %broadcast_in_dim.61), calls=%async_computation | async-start | bytes 2883584 | tf_op jit(solution)/shard_map/all_to_all | solution.py:263
  42.7 1.1 copy-start
  43.8 46.7 %copy-start.1 = (bf16[1024,512]{1,0:T(8,128)(2,1)S(1)}, bf16[1024,512]{1,0:T(8,128)(2,1)}, u32[]{:S(2)}) copy-start(bf16[1024,512]{1,0:T(8,128)(2,1)} %refs_7_.1) | copy-start | bytes 3145732
  87.8 16.6 %copy-start.14 = (bf16[4,128,512]{2,1,0:T(8,128)(2,1)S(1)}, bf16[4,128,512]{2,1,0:T(8,128)(2,1)}, u32[]{:S(2)}) copy-start(bf16[4,128,512]{2,1,0:T(8,128)(2,1)} %get-tuple-element.27) | copy-start | bytes 1572868
  87.8 11.4 %collective-permute-start.4 = (bf16[4,128,512]{2,1,0:T(8,128)(2,1)}, bf16[4,128,512]{2,1,0:T(8,128)(2,1)}, u32[]{:S(2)}, u32[]{:S(2)}) collective-permute-start(bf16[4,128,512]{2,1,0:T(8,128)(2,1)} %get-tuple-element.33), channel_id=1, source_target_pairs={{0,96},{8,104},{16,112},{24,120},{32,0},{40,8},{48,16},{56,24},{64... | collective-permute-start | bytes 1572872 | tf_op jit(solution)/shard_map/ppermute | solution.py:327
  90.5 13.8 %collective-permute-start = (bf16[4,128,512]{2,1,0:T(8,128)(2,1)}, bf16[4,128,512]{2,1,0:T(8,128)(2,1)S(1)}, u32[]{:S(2)}, u32[]{:S(2)}) collective-permute-start(bf16[4,128,512]{2,1,0:T(8,128)(2,1)} %get-tuple-element.28), channel_id=1, source_target_pairs={{0,32},{8,40},{16,48},{24,56},{32,64},{40,72},{48,80},{56,88},{64,... | collective-permute-start | bytes 1572872 | tf_op jit(solution)/shard_map/ppermute | solution.py:327
  90.5 38.7 %collective-permute-start.10 = (bf16[1024,512]{1,0:T(8,128)(2,1)S(1)}, bf16[1024,512]{1,0:T(8,128)(2,1)S(1)}, u32[]{:S(2)}, u32[]{:S(2)}) collective-permute-start(bf16[1024,512]{1,0:T(8,128)(2,1)S(1)} %copy-done.1), channel_id=1, source_target_pairs={{0,2},{1,3},{2,4},{3,5},{4,6},{5,7},{6,0},{7,1},{8,10},{9,11},{10,... | collective-permute-start | bytes 3145736 | tf_op jit(solution)/shard_map/ppermute | solution.py:370
  92.2 12.0 %copy-start.24 = (bf16[4,128,512]{2,1,0:T(8,128)(2,1)S(1)}, bf16[4,128,512]{2,1,0:T(8,128)(2,1)}, u32[]{:S(2)}) copy-start(bf16[4,128,512]{2,1,0:T(8,128)(2,1)} %get-tuple-element.37) | copy-start | bytes 1572868
  92.2 22.4 %collective-permute-start.3 = (bf16[4,128,512]{2,1,0:T(8,128)(2,1)}, bf16[4,128,512]{2,1,0:T(8,128)(2,1)S(1)}, u32[]{:S(2)}, u32[]{:S(2)}) collective-permute-start(bf16[4,128,512]{2,1,0:T(8,128)(2,1)} %get-tuple-element.31), channel_id=1, source_target_pairs={{0,32},{8,40},{16,48},{24,56},{32,64},{40,72},{48,80},{56,88},{64,... | collective-permute-start | bytes 1572872 | tf_op jit(solution)/shard_map/ppermute | solution.py:327
  92.3 33.4 %collective-permute-start.2 = (bf16[4,128,512]{2,1,0:T(8,128)(2,1)}, bf16[4,128,512]{2,1,0:T(8,128)(2,1)S(1)}, u32[]{:S(2)}, u32[]{:S(2)}) collective-permute-start(bf16[4,128,512]{2,1,0:T(8,128)(2,1)} %get-tuple-element.29), channel_id=1, source_target_pairs={{0,96},{8,104},{16,112},{24,120},{32,0},{40,8},{48,16},{56,24},{64... | collective-permute-start | bytes 1572872 | tf_op jit(solution)/shard_map/ppermute | solution.py:327
  99.2 10.9 %collective-permute-start.21 = (bf16[4,128,512]{2,1,0:T(8,128)(2,1)}, bf16[4,128,512]{2,1,0:T(8,128)(2,1)S(1)}, u32[]{:S(2)}, u32[]{:S(2)}) collective-permute-start(bf16[4,128,512]{2,1,0:T(8,128)(2,1)} %get-tuple-element.42), channel_id=1, source_target_pairs={{0,24},{8,0},{16,8},{24,16},{32,56},{40,32},{48,40},{56,48},{64,88... | collective-permute-start | bytes 1572872 | tf_op jit(solution)/shard_map/ppermute | solution.py:327
  102.9 11.4 %copy-start.13 = (bf16[4,128,512]{2,1,0:T(8,128)(2,1)S(1)}, bf16[4,128,512]{2,1,0:T(8,128)(2,1)}, u32[]{:S(2)}) copy-start(bf16[4,128,512]{2,1,0:T(8,128)(2,1)} %get-tuple-element.41) | copy-start | bytes 1572868
  104.3 10.2 %collective-permute-start.17 = (bf16[4,128,512]{2,1,0:T(8,128)(2,1)S(1)}, bf16[4,128,512]{2,1,0:T(8,128)(2,1)S(1)}, u32[]{:S(2)}, u32[]{:S(2)}) collective-permute-start(bf16[4,128,512]{2,1,0:T(8,128)(2,1)S(1)} %copy-done.24), channel_id=1, source_target_pairs={{0,8},{8,16},{16,24},{24,0},{32,40},{40,48},{48,56},{56,32},{64,72... | collective-permute-start | bytes 1572872 | tf_op jit(solution)/shard_map/ppermute | solution.py:327
  104.4 10.2 %copy-start.12 = (bf16[4,128,512]{2,1,0:T(8,128)(2,1)S(1)}, bf16[4,128,512]{2,1,0:T(8,128)(2,1)}, u32[]{:S(2)}) copy-start(bf16[4,128,512]{2,1,0:T(8,128)(2,1)} %get-tuple-element.36) | copy-start | bytes 1572868
  110.1 10.7 %collective-permute-start.5 = (bf16[4,128,512]{2,1,0:T(8,128)(2,1)S(1)}, bf16[4,128,512]{2,1,0:T(8,128)(2,1)S(1)}, u32[]{:S(2)}, u32[]{:S(2)}) collective-permute-start(bf16[4,128,512]{2,1,0:T(8,128)(2,1)S(1)} %add_convert_fusion.2), channel_id=1, source_target_pairs={{0,96},{8,104},{16,112},{24,120},{32,0},{40,8},{48,16},{56,24},{64... | collective-permute-start | bytes 1572872 | tf_op jit(solution)/shard_map/ppermute | solution.py:327
  114.3 1.0 copy-start.23
  114.3 6.5 %copy-start.22 = (bf16[4,128,512]{2,1,0:T(8,128)(2,1)S(1)}, bf16[4,128,512]{2,1,0:T(8,128)(2,1)}, u32[]{:S(2)}) copy-start(bf16[4,128,512]{2,1,0:T(8,128)(2,1)} %get-tuple-element.38) | copy-start | bytes 1572868
  114.3 10.1 %copy-start.18 = (bf16[4,128,512]{2,1,0:T(8,128)(2,1)S(1)}, bf16[4,128,512]{2,1,0:T(8,128)(2,1)}, u32[]{:S(2)}) copy-start(bf16[4,128,512]{2,1,0:T(8,128)(2,1)} %get-tuple-element.30) | copy-start | bytes 1572868
  114.5 11.5 %collective-permute-start.1 = (bf16[4,128,512]{2,1,0:T(8,128)(2,1)S(1)}, bf16[4,128,512]{2,1,0:T(8,128)(2,1)S(1)}, u32[]{:S(2)}, u32[]{:S(2)}) collective-permute-start(bf16[4,128,512]{2,1,0:T(8,128)(2,1)S(1)} %add_convert_fusion.3), channel_id=1, source_target_pairs={{0,32},{8,40},{16,48},{24,56},{32,64},{40,72},{48,80},{56,88},{64,... | collective-permute-start | bytes 1572872 | tf_op jit(solution)/shard_map/ppermute | solution.py:327
  115.3 18.1 %collective-permute-start.20 = (bf16[4,128,512]{2,1,0:T(8,128)(2,1)S(1)}, bf16[4,128,512]{2,1,0:T(8,128)(2,1)S(1)}, u32[]{:S(2)}, u32[]{:S(2)}) collective-permute-start(bf16[4,128,512]{2,1,0:T(8,128)(2,1)S(1)} %copy-done.23), channel_id=1, source_target_pairs={{0,8},{8,16},{16,24},{24,0},{32,40},{40,48},{48,56},{56,32},{64,72... | collective-permute-start | bytes 1572872 | tf_op jit(solution)/shard_map/ppermute | solution.py:327
  120.8 22.1 %collective-permute-start.19 = (bf16[4,128,512]{2,1,0:T(8,128)(2,1)S(1)}, bf16[4,128,512]{2,1,0:T(8,128)(2,1)S(1)}, u32[]{:S(2)}, u32[]{:S(2)}) collective-permute-start(bf16[4,128,512]{2,1,0:T(8,128)(2,1)S(1)} %copy-done.22), channel_id=1, source_target_pairs={{0,24},{8,0},{16,8},{24,16},{32,56},{40,32},{48,40},{56,48},{64,88... | collective-permute-start | bytes 1572872 | tf_op jit(solution)/shard_map/ppermute | solution.py:327
  124.4 2.7 %copy-start.17 = (bf16[4,128,512]{2,1,0:T(8,128)(2,1)S(1)}, bf16[4,128,512]{2,1,0:T(8,128)(2,1)}, u32[]{:S(2)}) copy-start(bf16[4,128,512]{2,1,0:T(8,128)(2,1)} %get-tuple-element.26) | copy-start | bytes 1572868
  125.7 2.7 %copy-start.9 = (bf16[4,128,512]{2,1,0:T(8,128)(2,1)}, bf16[4,128,512]{2,1,0:T(8,128)(2,1)S(1)}, u32[]{:S(2)}) copy-start(bf16[4,128,512]{2,1,0:T(8,128)(2,1)S(1)} %get-tuple-element.48) | copy-start | bytes 1572868
  125.7 16.0 %collective-permute-start.22 = (bf16[4,128,512]{2,1,0:T(8,128)(2,1)S(1)}, bf16[4,128,512]{2,1,0:T(8,128)(2,1)S(1)}, u32[]{:S(2)}, u32[]{:S(2)}) collective-permute-start(bf16[4,128,512]{2,1,0:T(8,128)(2,1)S(1)} %add_convert_fusion), channel_id=1, source_target_pairs={{0,24},{8,0},{16,8},{24,16},{32,56},{40,32},{48,40},{56,48},{64,88... | collective-permute-start | bytes 1572872 | tf_op jit(solution)/shard_map/ppermute | solution.py:327
  126.0 20.4 %collective-permute-start.18 = (bf16[4,128,512]{2,1,0:T(8,128)(2,1)S(1)}, bf16[4,128,512]{2,1,0:T(8,128)(2,1)S(1)}, u32[]{:S(2)}, u32[]{:S(2)}) collective-permute-start(bf16[4,128,512]{2,1,0:T(8,128)(2,1)S(1)} %add_convert_fusion.1), channel_id=1, source_target_pairs={{0,8},{8,16},{16,24},{24,0},{32,40},{40,48},{48,56},{56,32},{64,72... | collective-permute-start | bytes 1572872 | tf_op jit(solution)/shard_map/ppermute | solution.py:327
  128.4 14.5 %copy-start.8 = (bf16[4,128,512]{2,1,0:T(8,128)(2,1)}, bf16[4,128,512]{2,1,0:T(8,128)(2,1)S(1)}, u32[]{:S(2)}) copy-start(bf16[4,128,512]{2,1,0:T(8,128)(2,1)S(1)} %get-tuple-element.46) | copy-start | bytes 1572868
  128.4 13.3 %copy-start.16 = (bf16[4,128,512]{2,1,0:T(8,128)(2,1)S(1)}, bf16[4,128,512]{2,1,0:T(8,128)(2,1)}, u32[]{:S(2)}) copy-start(bf16[4,128,512]{2,1,0:T(8,128)(2,1)} %get-tuple-element.39) | copy-start | bytes 1572868
  129.2 33.4 %copy-start.2 = (bf16[1024,512]{1,0:T(8,128)(2,1)}, bf16[1024,512]{1,0:T(8,128)(2,1)S(1)}, u32[]{:S(2)}) copy-start(bf16[1024,512]{1,0:T(8,128)(2,1)S(1)} %collective-permute-done.10.refs_7_.refs_8_) | copy-start | bytes 3145732
  129.2 26.1 %collective-permute-start.12 = (bf16[1024,512]{1,0:T(8,128)(2,1)S(1)}, bf16[1024,512]{1,0:T(8,128)(2,1)S(1)}, u32[]{:S(2)}, u32[]{:S(2)}) collective-permute-start(bf16[1024,512]{1,0:T(8,128)(2,1)S(1)} %copy-done.1), channel_id=1, source_target_pairs={{0,6},{1,7},{2,0},{3,1},{4,2},{5,3},{6,4},{7,5},{8,14},{9,15},{10,... | collective-permute-start | bytes 3145736 | tf_op jit(solution)/shard_map/ppermute | solution.py:370
  133.4 29.1 %collective-permute-start.11 = (bf16[1024,512]{1,0:T(8,128)(2,1)S(1)}, bf16[1024,512]{1,0:T(8,128)(2,1)}, u32[]{:S(2)}, u32[]{:S(2)}) collective-permute-start(bf16[1024,512]{1,0:T(8,128)(2,1)S(1)} %collective-permute-done.10.refs_7_.refs_8_), channel_id=1, source_target_pairs={{0,2},{1,3},{2,4},{3,5},{4,6},{5,7},{6,0},{7,1},{8,10},{9,11},{10,... | collective-permute-start | bytes 3145736 | tf_op jit(solution)/shard_map/ppermute | solution.py:370
  141.6 21.0 %collective-permute-start.6 = (bf16[2,128,512]{2,1,0:T(8,128)(2,1)}, bf16[2,128,512]{2,1,0:T(8,128)(2,1)}, u32[]{:S(2)}, u32[]{:S(2)}) collective-permute-start(bf16[2,128,512]{2,1,0:T(8,128)(2,1)} %pad_maximum_fusion.1), channel_id=1, source_target_pairs={{0,8},{8,16},{16,24},{24,0},{32,40},{40,48},{48,56},{56,32},{64,72... | collective-permute-start | bytes 786440 | tf_op jit(solution)/shard_map/ppermute | solution.py:327
  141.6 4.7 %copy-start.15 = (bf16[4,128,512]{2,1,0:T(8,128)(2,1)S(1)}, bf16[4,128,512]{2,1,0:T(8,128)(2,1)}, u32[]{:S(2)}) copy-start(bf16[4,128,512]{2,1,0:T(8,128)(2,1)} %get-tuple-element.35) | copy-start | bytes 1572868
  142.9 4.7 %copy-start.11 = (bf16[4,128,512]{2,1,0:T(8,128)(2,1)}, bf16[4,128,512]{2,1,0:T(8,128)(2,1)S(1)}, u32[]{:S(2)}) copy-start(bf16[4,128,512]{2,1,0:T(8,128)(2,1)S(1)} %get-tuple-element.52) | copy-start | bytes 1572868
  142.9 7.3 %collective-permute-start.8 = (bf16[2,128,512]{2,1,0:T(8,128)(2,1)S(1)}, bf16[2,128,512]{2,1,0:T(8,128)(2,1)S(1)}, u32[]{:S(2)}, u32[]{:S(2)}) collective-permute-start(bf16[2,128,512]{2,1,0:T(8,128)(2,1)S(1)} %pad_maximum_fusion.2), channel_id=1, source_target_pairs={{0,24},{8,0},{16,8},{24,16},{32,56},{40,32},{48,40},{56,48},{64,88... | collective-permute-start | bytes 786440 | tf_op jit(solution)/shard_map/ppermute | solution.py:327
  147.6 0.9 copy-start.10
  147.6 6.1 %copy-start.21 = (s32[4096]{0:T(1024)S(1)}, s32[4096]{0:T(1024)}, u32[]{:S(2)}) copy-start(s32[4096]{0:T(1024)} %param.18) | copy-start | bytes 49156
  149.2 13.8 %collective-permute-start.23 = (bf16[2,128,512]{2,1,0:T(8,128)(2,1)}, bf16[2,128,512]{2,1,0:T(8,128)(2,1)}, u32[]{:S(2)}, u32[]{:S(2)}) collective-permute-start(bf16[2,128,512]{2,1,0:T(8,128)(2,1)} %pad_maximum_fusion.3), channel_id=1, source_target_pairs={{0,32},{8,40},{16,48},{24,56},{32,64},{40,72},{48,80},{56,88},{64,... | collective-permute-start | bytes 786440 | tf_op jit(solution)/shard_map/ppermute | solution.py:327
  150.2 14.2 %collective-permute-start.25 = (bf16[2,128,512]{2,1,0:T(8,128)(2,1)}, bf16[2,128,512]{2,1,0:T(8,128)(2,1)}, u32[]{:S(2)}, u32[]{:S(2)}) collective-permute-start(bf16[2,128,512]{2,1,0:T(8,128)(2,1)} %pad_maximum_fusion.4), channel_id=1, source_target_pairs={{0,96},{8,104},{16,112},{24,120},{32,0},{40,8},{48,16},{56,24},{64... | collective-permute-start | bytes 786440 | tf_op jit(solution)/shard_map/ppermute | solution.py:327
  155.3 24.2 %copy-start.3 = (bf16[1024,512]{1,0:T(8,128)(2,1)}, bf16[1024,512]{1,0:T(8,128)(2,1)S(1)}, u32[]{:S(2)}) copy-start(bf16[1024,512]{1,0:T(8,128)(2,1)S(1)} %collective-permute-done.12.refs_9_.refs_10_) | copy-start | bytes 3145732
  155.3 29.6 %collective-permute-start.13 = (bf16[1024,512]{1,0:T(8,128)(2,1)S(1)}, bf16[1024,512]{1,0:T(8,128)(2,1)S(1)}, u32[]{:S(2)}, u32[]{:S(2)}) collective-permute-start(bf16[1024,512]{1,0:T(8,128)(2,1)S(1)} %copy-done.1), channel_id=1, source_target_pairs={{0,1},{1,0},{2,3},{3,2},{4,5},{5,4},{6,7},{7,6},{8,9},{9,8},{10,11... | collective-permute-start | bytes 3145736 | tf_op jit(solution)/shard_map/ppermute | solution.py:370
  162.5 22.4 %collective-permute-start.14 = (bf16[1024,512]{1,0:T(8,128)(2,1)S(1)}, bf16[1024,512]{1,0:T(8,128)(2,1)S(1)}, u32[]{:S(2)}, u32[]{:S(2)}) collective-permute-start(bf16[1024,512]{1,0:T(8,128)(2,1)S(1)} %collective-permute-done.10.refs_7_.refs_8_), channel_id=1, source_target_pairs={{0,1},{1,0},{2,3},{3,2},{4,5},{5,4},{6,7},{7,6},{8,9},{9,8},{10,11... | collective-permute-start | bytes 3145736 | tf_op jit(solution)/shard_map/ppermute | solution.py:370
  162.6 22.3 %collective-permute-start.16 = (bf16[1024,512]{1,0:T(8,128)(2,1)S(1)}, bf16[1024,512]{1,0:T(8,128)(2,1)S(1)}, u32[]{:S(2)}, u32[]{:S(2)}) collective-permute-start(bf16[1024,512]{1,0:T(8,128)(2,1)S(1)} %collective-permute-done.12.refs_9_.refs_10_), channel_id=1, source_target_pairs={{0,1},{1,0},{2,3},{3,2},{4,5},{5,4},{6,7},{7,6},{8,9},{9,8},{10,11... | collective-permute-start | bytes 3145736 | tf_op jit(solution)/shard_map/ppermute | solution.py:370
  163.1 22.8 %collective-permute-start.15 = (bf16[1024,512]{1,0:T(8,128)(2,1)}, bf16[1024,512]{1,0:T(8,128)(2,1)S(1)}, u32[]{:S(2)}, u32[]{:S(2)}) collective-permute-start(bf16[1024,512]{1,0:T(8,128)(2,1)} %collective-permute-done.11.refs_8_.refs_9_), channel_id=1, source_target_pairs={{0,1},{1,0},{2,3},{3,2},{4,5},{5,4},{6,7},{7,6},{8,9},{9,8},{10,11... | collective-permute-start | bytes 3145736 | tf_op jit(solution)/shard_map/ppermute | solution.py:370
  164.4 4.5 %collective-permute-start.9 = (bf16[1,128,512]{2,1,0:T(8,128)(2,1)S(1)}, bf16[1,128,512]{2,1,0:T(8,128)(2,1)S(1)}, u32[]{:S(2)}, u32[]{:S(2)}) collective-permute-start(bf16[1,128,512]{2,1,0:T(8,128)(2,1)S(1)} %add_convert_fusion.6), channel_id=1, source_target_pairs={{0,24},{8,0},{16,8},{24,16},{32,56},{40,32},{48,40},{56,48},{64,88... | collective-permute-start | bytes 393224 | tf_op jit(solution)/shard_map/ppermute | solution.py:327
  168.9 3.8 %collective-permute-start.26 = (bf16[1,128,512]{2,1,0:T(8,128)(2,1)S(1)}, bf16[1,128,512]{2,1,0:T(8,128)(2,1)S(1)}, u32[]{:S(2)}, u32[]{:S(2)}) collective-permute-start(bf16[1,128,512]{2,1,0:T(8,128)(2,1)S(1)} %add_convert_fusion.4), channel_id=1, source_target_pairs={{0,96},{8,104},{16,112},{24,120},{32,0},{40,8},{48,16},{56,24},{64... | collective-permute-start | bytes 393224 | tf_op jit(solution)/shard_map/ppermute | solution.py:327
  172.7 5.1 %collective-permute-start.7 = (bf16[1,128,512]{2,1,0:T(8,128)(2,1)S(1)}, bf16[1,128,512]{2,1,0:T(8,128)(2,1)S(1)}, u32[]{:S(2)}, u32[]{:S(2)}) collective-permute-start(bf16[1,128,512]{2,1,0:T(8,128)(2,1)S(1)} %get-tuple-element.63), channel_id=1, source_target_pairs={{0,8},{8,16},{16,24},{24,0},{32,40},{40,48},{48,56},{56,32},{64,72... | collective-permute-start | bytes 393224 | tf_op jit(solution)/shard_map/ppermute | solution.py:327
  177.8 5.3 %collective-permute-start.24 = (bf16[1,128,512]{2,1,0:T(8,128)(2,1)S(1)}, bf16[1,128,512]{2,1,0:T(8,128)(2,1)S(1)}, u32[]{:S(2)}, u32[]{:S(2)}) collective-permute-start(bf16[1,128,512]{2,1,0:T(8,128)(2,1)S(1)} %get-tuple-element.65), channel_id=1, source_target_pairs={{0,32},{8,40},{16,48},{24,56},{32,64},{40,72},{48,80},{56,88},{64,... | collective-permute-start | bytes 393224 | tf_op jit(solution)/shard_map/ppermute | solution.py:327
  184.9 1.0 copy-start.4
  184.9 1.3 copy-start.5
  185.9 1.0 copy-start.6
  186.2 1.0 copy-start.7
  207.6 18.1 %copy-start.19 = (bf16[256,512]{1,0:T(8,128)(2,1)S(1)}, bf16[256,512]{1,0:T(8,128)(2,1)}, u32[]{:S(2)}) copy-start(bf16[256,512]{1,0:T(8,128)(2,1)} %get-tuple-element.34) | copy-start | bytes 786436
  207.6 18.1 %copy-start.20 = (bf16[256,512]{1,0:T(8,128)(2,1)S(1)}, bf16[256,512]{1,0:T(8,128)(2,1)}, u32[]{:S(2)}) copy-start(bf16[256,512]{1,0:T(8,128)(2,1)} %get-tuple-element.44) | copy-start | bytes 786436
  210.1 29.2 %all-to-all-start.1 = ((f32[128,1,1024]{2,1,0:T(1,128)}), f32[128,1,1024]{2,1,0:T(1,128)S(1)}, u32[]{:S(2)}, u32[]{:S(2)}) async-start(f32[128,1,1024]{2,1,0:T(1,128)} %all_to_all.12), calls=%async_computation.1 | async-start | bytes 1048576 | tf_op jit(solution)/shard_map/all_to_all | solution.py:561

commit v3 on v1

--- a/solution.py
+++ b/solution.py
@@ -13,17 +13,18 @@
 CHUNK = 128
 STRIDE = 132
 BLOCK = 10
+USUAL = 8
 STAGE = 1024
 DEEP = 4
 LINES = 176
 COUNTS = 165
 SIDE = 4
-SCORED = 256
+SCORED = 512
 LOG2E = 1.4426950408889634
 MESSAGES = 2 * SIDE
 
 
-def compose_kernel(slots_ref, self_ref, count_ref, fetch_ref, keys_ref):
+def compose_kernel(slots_ref, self_ref, count_ref, fetch_ref, keys_ref, ends_ref):
     neighbours, negatives = slots_ref.shape
     parts, per_part = fetch_ref.shape
     per_line = per_part // LANES
@@ -65,10 +66,40 @@
     own = own | ((tile_of(count_ref) - 20) << 14) | (1 << 13)
     keys_ref[neighbours * negatives // LANES :, :] = own[: negatives // LANES]
 
+    keys = keys_ref[...]
+    at = lax.broadcasted_iota(jnp.int32, (1, LANES), 1)
+    ends = jnp.zeros((1, LANES), jnp.int32)
+    for p in range(parts):
+        below = jnp.sum((keys < min((p + 1 - 8) << 28, DEAD)).astype(jnp.int32), axis=0, keepdims=True)
+        ends = jnp.where(at == p, jnp.sum(below, axis=1, keepdims=True), ends)
+    ends_ref[...] = ends
+
+
+def pack_kernel(keys_ref, ends_ref, count_ref, out_ref):
+    entries = keys_ref.shape[0]
+    negatives = count_ref.shape[1]
+    keys = keys_ref[...]
+    lines = (((keys >> 19) & (negatives - 1)) << 16) | (keys & 16383)
+    count = [count_ref[:, q * LANES : (q + 1) * LANES] for q in range(negatives // LANES)]
+    for p in range(out_ref.shape[0]):
+        out_ref[p, :entries, :] = lines
+        out_ref[p, entries : entries + 1, :] = ends_ref[...]
+        for q, line in enumerate(count):
+            out_ref[p, COUNTS + q : COUNTS + q + 1, :] = line
+        out_ref[p, COUNTS + len(count) :, :] = jnp.zeros((LINES - COUNTS - len(count), LANES), jnp.int32)
+
+
+def packed_lists(keys, ends, neighbour_count, devices):
+    return pl.pallas_call(
+        pack_kernel,
+        out_shape=jax.ShapeDtypeStruct((devices, LINES, LANES), jnp.int32),
+        name="pack",
+    )(keys, ends, neighbour_count[None, :])
+
 
 def owner_kernel(part_ref, ends_ref, lists_ref, message_hbm, self_hbm, *refs):
     outs = refs[: 2 * MESSAGES]
-    table, stage, pick, rows, acc, raw, weights, offsets, places, ready, sems, place_sem, out_sems = refs[2 * MESSAGES :]
+    table, stage, pick, rows, acc, raw, aligned, weights, offsets, places, ready, sems, place_sem, out_sems = refs[2 * MESSAGES :]
     items = message_hbm.shape[0]
     width = message_hbm.shape[1]
     tiles = width // LANES
@@ -90,12 +121,17 @@
     def place_copy():
         return pltpu.make_async_copy(offsets, places, place_sem)
 
-    def place(r, base):
-        for c in range(BLOCK):
+    def place(r, first):
+        base = first >> 7
+        skip = first & (LANES - 1)
+        for c in range(BLOCK + 1):
             raw[c : c + 1, :] = lists_ref[r, pl.ds(base + c, 1), :]
+        ahead = lax.broadcasted_iota(jnp.int32, (16, LANES), 1) < LANES - skip
+        turn = (LANES - skip) & (LANES - 1)
+        aligned[...] = jnp.where(ahead, pltpu.roll(raw[0:16, :], turn, 1), pltpu.roll(raw[1:17, :], turn, 1))
         for half in range(2):
             at = slice(8 * half, 8 * half + 8)
-            lines = raw[at, :]
+            lines = aligned[at, :]
             offsets[at, :] = (lines & 16383) * tiles
             v = (lines >> 16) & (negatives - 1)
             count = jnp.zeros_like(v)
@@ -126,7 +162,7 @@
         for c in range(DEEP):
             stage_copy(c).start()
         raw[...] = jnp.zeros_like(raw)
-        place(asker(0), range_of(asker(0))[0] >> 7)
+        place(asker(0), range_of(asker(0))[0])
         rows[...] = jnp.zeros_like(rows)
         for c in range(2 * per_table):
             stage_copy(c).wait()
@@ -149,39 +185,35 @@
 
     a = asker(step)
     start, end = range_of(a)
-    row_first = start >> 7
-    row_last = (end + 127) >> 7
-
-    def picked(r, line, weight):
+
+    def picked(c, left, line, weight):
         v = lax.broadcasted_iota(jnp.int32, (negatives, LANES), 0)
-        at = r * LANES + lax.broadcasted_iota(jnp.int32, (1, LANES), 1)
-        who = jnp.where((at >= start) & (at < end), line >> 16, -1)
+        at = c * LANES + lax.broadcasted_iota(jnp.int32, (1, LANES), 1)
+        who = jnp.where(at < left, line >> 16, -1)
         return jnp.where(v == who, weight, 0.0).astype(jnp.bfloat16)
 
-    def gather(base):
+    def gather(left):
         place_copy().wait()
         for c in range(BLOCK):
-            r = base + c
-
-            @pl.when(r < row_last)
-            def _(c=c, r=r):
-                pick[:, c * LANES : (c + 1) * LANES] = picked(r, raw[c : c + 1, :], weights[c : c + 1, :])
+
+            @pl.when(c * LANES < left)
+            def _(c=c):
+                pick[:, c * LANES : (c + 1) * LANES] = picked(c, left, aligned[c : c + 1, :], weights[c : c + 1, :])
                 for e in range(CHUNK):
                     at = pl.multiple_of(places[c, e], tiles)
                     rows[c, pl.ds(e, tiles, stride=STRIDE), :] = table[pl.ds(at, tiles), :]
 
-            @pl.when(r >= row_last)
+            @pl.when(c * LANES >= left)
             def _(c=c):
                 pick[:, c * LANES : (c + 1) * LANES] = jnp.zeros((negatives, LANES), jnp.bfloat16)
 
-    def gather_more(base):
+    def gather_more(left):
         place_copy().wait()
 
         def chunk(c, _):
             cols = pl.ds(pl.multiple_of(c * LANES, LANES), LANES)
-            live = base + c < row_last
             one = pl.ds(c, 1)
-            pick[:, cols] = jnp.where(live, picked(base + c, raw[one, :], weights[one, :]), 0).astype(jnp.bfloat16)
+            pick[:, cols] = picked(c, left, aligned[one, :], weights[one, :])
 
             def entry(e, _):
                 at = pl.multiple_of(places[c, e], tiles)
@@ -192,43 +224,51 @@
 
         lax.fori_loop(0, BLOCK, chunk, 0)
 
-    def summed():
+    def summed(low, high):
         gathered = jnp.concatenate(
             [
                 jnp.concatenate(
                     [rows[c, j * STRIDE : j * STRIDE + CHUNK, :].astype(jnp.bfloat16) for j in range(tiles)],
                     axis=1,
                 )
-                for c in range(BLOCK)
+                for c in range(low, high)
             ],
             axis=0,
         )
-        return jnp.dot(pick[...], gathered, preferred_element_type=jnp.float32)
-
-    gather(row_first)
-    blocks = (row_last - row_first + BLOCK - 1) // BLOCK
-
-    @pl.when((blocks <= 1) & (step + 1 < devices))
-    def _():
-        following = asker(step + 1)
-        place(following, range_of(following)[0] >> 7)
-
-    acc[...] = summed()
-
-    @pl.when(blocks > 1)
-    def _():
-        def more(i, _):
-            place(a, row_first + i * BLOCK)
-            gather_more(row_first + i * BLOCK)
-            acc[...] += summed()
-            return 0
-
-        lax.fori_loop(1, blocks, more, 0)
-
+        return jnp.dot(
+            pick[:, low * LANES : high * LANES], gathered, preferred_element_type=jnp.float32
+        )
+
+    many = end - start
+    block = BLOCK * LANES
+    gather(many)
+
+    def place_next():
         @pl.when(step + 1 < devices)
         def _():
             following = asker(step + 1)
-            place(following, range_of(following)[0] >> 7)
+            place(following, range_of(following)[0])
+
+    @pl.when(many <= block)
+    def _():
+        place_next()
+
+    acc[...] = summed(0, USUAL)
+
+    @pl.when(many > USUAL * LANES)
+    def _():
+        acc[...] += summed(USUAL, BLOCK)
+
+    @pl.when(many > block)
+    def _():
+        def more(i, _):
+            place(a, start + i * block)
+            gather_more(many - i * block)
+            acc[...] += summed(0, BLOCK)
+            return 0
+
+        lax.fori_loop(1, (many + block - 1) // block, more, 0)
+        place_next()
 
     slot = step % 2
 
@@ -255,11 +295,6 @@
     def _():
         wait_out(slot)
         wait_out(1 - slot)
-
-
-def from_everyone(x, axis):
-    devices = lax.axis_size(axis)
-    return lax.all_to_all(jnp.broadcast_to(x[None], (devices, *x.shape)), axis, 0, 0, tiled=True)
 
 
 def composed_keys(neighbour_slots, self_slot, neighbour_count, fetch_rows):
@@ -267,7 +302,10 @@
     folded = negatives // LANES
     return pl.pallas_call(
         compose_kernel,
-        out_shape=jax.ShapeDtypeStruct(((neighbours + 1) * folded, LANES), jnp.int32),
+        out_shape=[
+            jax.ShapeDtypeStruct(((neighbours + 1) * folded, LANES), jnp.int32),
+            jax.ShapeDtypeStruct((1, LANES), jnp.int32),
+        ],
         name="compose",
     )(
         neighbour_slots.T,
@@ -300,6 +338,7 @@
             pltpu.VMEM((negatives, BLOCK * CHUNK), jnp.bfloat16),
             pltpu.VMEM((BLOCK, tiles * STRIDE, LANES), jnp.float32),
             pltpu.VMEM((negatives, width), jnp.float32),
+            pltpu.VMEM((24, LANES), jnp.int32),
             pltpu.VMEM((16, LANES), jnp.int32),
             pltpu.VMEM((16, LANES), jnp.float32),
             pltpu.VMEM((16, LANES), jnp.int32),
@@ -406,9 +445,9 @@
 
 def score_kernel(*refs):
     sums = refs[:4]
-    count_ref, bias_ref, log_ref = refs[4:7]
-    queries = refs[7 : 7 + 2 * SIDE]
-    embed_ref, lse_ref, held, even, odd, logs, sems = refs[7 + 2 * SIDE :]
+    count_ref, bias_ref, log_ref, place_ref = refs[4:8]
+    queries = refs[8 : 8 + 2 * SIDE]
+    embed_ref, lse_ref, held, even, odd, logs, sems = refs[8 + 2 * SIDE :]
     f32 = jnp.float32
     rows = queries[0].shape[0]
     blocks = len(queries) * rows // SCORED
@@ -424,7 +463,8 @@
     def columns(row):
         return jnp.broadcast_to(row, (LANES, negatives)).T
 
-    logs[...] = columns(jnp.log(log_ref[...].astype(f32)) * LOG2E)
+    own = log_ref[pl.ds(place_ref[0], 1), :]
+    logs[...] = columns(jnp.log(own.astype(f32)) * LOG2E)
     counts = columns(count_ref[...].astype(f32))
     quarter = negatives // 4
     for q in range(4):
@@ -467,14 +507,16 @@
     lax.fori_loop(0, blocks // 2, pair, 0)
 
 
-def scored(sums, count, bias, own_count, queries):
+def scored(sums, count, bias, counts_all, place, queries):
     negatives = count.shape[0]
     rows, width = queries[0].shape
     total = rows * len(queries)
     in_vmem = pl.BlockSpec(memory_space=pltpu.VMEM)
     return pl.pallas_call(
         score_kernel,
-        in_specs=[in_vmem] * 7 + [pl.BlockSpec(memory_space=pl.ANY)] * len(queries),
+        in_specs=[in_vmem] * 7
+        + [pl.BlockSpec(memory_space=pltpu.SMEM)]
+        + [pl.BlockSpec(memory_space=pl.ANY)] * len(queries),
         out_specs=[in_vmem] * 2,
         out_shape=[
             jax.ShapeDtypeStruct((negatives, width), jnp.bfloat16),
@@ -488,7 +530,7 @@
             pltpu.SemaphoreType.DMA((len(queries),)),
         ],
         name="score",
-    )(*sums, count[None, :], bias[None, :], own_count[None, :], *queries)
+    )(*sums, count[None, :], bias[None, :], counts_all, place, *queries)
 
 
 def per_device(
@@ -510,25 +552,23 @@
     groups = lax.axis_size("qry")
     query_blocks = all_queries(queries)
 
-    keys = composed_keys(neighbour_slots, self_slot, neighbour_count, fetch_rows).reshape(-1)
-    bounds = jnp.array([min((p + 1 - 8) << 28, DEAD) for p in range(parts)], jnp.int32)
-    ends = jnp.sum((keys[None, :] < bounds[:, None]).astype(jnp.int32), axis=1)
-    ordered = lax.sort(keys, is_stable=False)
-    ordered = (((ordered >> 19) & (negatives - 1)) << 16) | (ordered & 16383)
-    tail = jnp.zeros((LINES * LANES - keys.size - LANES - negatives,), jnp.int32)
-    lines = jnp.concatenate([ordered, jnp.pad(ends, (0, LANES - parts)), neighbour_count, tail])
-    lists = from_everyone(lines.reshape(LINES, LANES), "neg")
+    keys, ends = composed_keys(neighbour_slots, self_slot, neighbour_count, fetch_rows)
+    ordered = lax.sort(keys.reshape(-1), is_stable=False).reshape(keys.shape)
+    lists = packed_lists(ordered, ends, neighbour_count, parts)
+    lists = lax.all_to_all(lists, "neg", split_axis=0, concat_axis=0, tiled=True)
 
     message_part, self_part = tables(items_table, message_weight, message_bias, neighbour_weight, self_weight)
 
-    own_count = lax.dynamic_slice(negative_count, (lax.axis_index("qry") * negatives,), (negatives,))
     place = lax.axis_index("neg")
     part = jnp.stack([place // SIDE, place % SIDE]).astype(jnp.int32)
-    outs = owner_sums(part, lists[:, keys.size // LANES, :parts], lists, message_part, self_part, negatives)
+    outs = owner_sums(part, lists[:, keys.shape[0], :parts], lists, message_part, self_part, negatives)
     sums = [q[0] for q in scattered_sums(outs)]
 
-    negative_embed, part_lse = scored(sums, neighbour_count, output_bias, own_count, query_blocks)
     here = lax.axis_index("qry")
+    counts_all = negative_count.reshape(groups, negatives)
+    negative_embed, part_lse = scored(
+        sums, neighbour_count, output_bias, counts_all, here.reshape(1), query_blocks
+    )
     z, core = here // 2, here % 2
     group = jnp.arange(groups)
     source = ((z - group // 2) % SIDE) + SIDE * ((group % 2) ^ core)

time: 231 us -> 229 us (level)
  waiting for transfers between devices: 40.5 us -> 34.7 us
  starting transfers between devices: 49.3 us -> 54.8 us
  other arithmetic: 27 us -> 29.9 us
  local copies, waits for them, and re-layouts: 6.69 us -> 4.1 us
    ppermute x20, starting transfers between devices: 28.6 us -> 38.7 us  [moved(): return lax.ppermute(x, 'neg', [(i, place(i)) for i in range(SIDE * SIDE)])]
    ppermute x20, waiting for transfers between devices: 38.9 us -> 33 us  [moved(): return lax.ppermute(x, 'neg', [(i, place(i)) for i in range(SIDE * SIDE)])]
    ppermute x7, starting transfers between devices: 13.1 us -> 8.49 us  [turned(): return lax.ppermute(x, 'qry', [(i, place(i)) for i in range(2 * SIDE)])]
    pallas_call x1, Pallas kernels: 14 us -> 11 us  [scored(): pl.pallas_call(score_kernel, in_specs=[in_vmem] * 7 + [pl.BlockSpec(memor...]
    pallas_call x1 -> x2, Pallas kernels: 2.57 us -> 4.76 us  [the longest x1 2.57 us: composed_keys(): pl.pallas_call(compose_kernel, out_shape=[jax.ShapeDtypeStruct(((neighbou...]
  transfers between devices with their start and end apart: 28 -> 28, of which waited for: 11 -> 10; matrix products, arithmetic and copies ran while one was open for 7% -> 9% of each run, Pallas kernels for 7% -> 8%
where the time goes in v3:
time: 229 us; the launch traced here: 228 us
  Pallas kernels  75.9 us (33%)
  starting transfers between devices  54.8 us (24%)
  waiting for transfers between devices  34.7 us (15%)
  other arithmetic  29.9 us (13%)
  blocking collectives  27.6 us (12%)
  local copies, waits for them, and re-layouts  4.1 us (2%)
    pallas_call x1, Pallas kernels, owner_sums(): pl.pallas_call(owner_kernel, grid=(devices,), in_specs=[pl.BlockSpec(memo...  42.9 us
    ppermute x20, starting transfers between devices, moved(): return lax.ppermute(x, 'neg', [(i, place(i)) for i in range(SIDE * SIDE)])  38.7 us
    ppermute x20, waiting for transfers between devices, moved(): return lax.ppermute(x, 'neg', [(i, place(i)) for i in range(SIDE * SIDE)])  33 us
    all_to_all x1, blocking collectives, per_device(): lax.all_to_all(shared.reshape(parts * groups, -1), ('neg', 'qry'), split_...  27.6 us
    pallas_call x1, Pallas kernels, tables(): pl.pallas_call(table_kernel, grid=(items // STAGE,), in_specs=[block, wei...  17.2 us
    pallas_call x1, Pallas kernels, scored(): pl.pallas_call(score_kernel, in_specs=[in_vmem] * 7 + [pl.BlockSpec(memor...  11 us
    sort x1, other arithmetic, per_device(): ordered = lax.sort(keys.reshape(-1), is_stable=False).reshape(keys.shape)  9.88 us
    ppermute x7, starting transfers between devices, turned(): return lax.ppermute(x, 'qry', [(i, place(i)) for i in range(2 * SIDE)])  8.49 us
  transfers between devices with their start and end apart: 28, of which 10 were waited for; matrix products, arithmetic and copies ran while one was open for 9% of the time, Pallas kernels for 8%

profile of v3, /device:TPU:1, one launch (start us, length us, event | category | flops | bytes accessed | tf_op | source)
XLA Modules:
  0.0 227.9 jit_solution(1684626275259725220)
XLA Ops:
  0.6 2.6 %compose.1 = (s32[164,128]{1,0:T(8,128)}, s32[1,128]{1,0:T(1,128)}) custom-call(s32[40,512]{1,0:T(8,128)} %bitcast.27, s32[1,512]{1,0:T(1,128)} %bitcast.32, s32[1,512]{1,0:T(1,128)} %bitcast.29, s32[16,640]{1,0:T(8,128)} %fetch_ref.1), custom_call_target="tpu_custom_call" | custom-call | tf_op jit(solution)/shard_map/compose/pallas_call | solution.py:303
  3.2 9.9 %sort.7 = s32[20992]{0:T(1024)} sort(s32[20992]{0:T(1024)} %bitcast.26), dimensions={0}, to_apply=%region_0.0 | sort | flops 314880 | bytes 167936 | tf_op jit(solution)/shard_map/sort | solution.py:556
  13.1 2.2 pack.1
  15.3 7.6 %all-to-all-start = ((s32[16,176,128]{2,1,0:T(8,128)}), s32[16,176,128]{2,1,0:T(8,128)S(1)}, u32[]{:S(2)}, u32[]{:S(2)}) async-start(s32[16,176,128]{2,1,0:T(8,128)} %pack.1), calls=%async_computation | async-start | bytes 2883584 | tf_op jit(solution)/shard_map/all_to_all | solution.py:558
  22.9 17.2 %tables.1 = (bf16[8192,512]{1,0:T(8,128)(2,1)}, bf16[8192,512]{1,0:T(8,128)(2,1)}) custom-call(bf16[8192,512]{1,0:T(8,128)(2,1)} %items_ref.1, bf16[512,512]{1,0:T(8,128)(2,1)} %message_ref.1, f32[1,512]{1,0:T(1,128)} %bitcast.34, bf16[512,512]{1,0:T(8,128)(2,1)} %neighbour_ref.1, bf16[512,512]{1,0:T(8,128)(2,1)} %self_ref.1), custom_call_target="tpu_custom_call" | custom-call | tf_op jit(solution)/shard_map/tables/pallas_call | solution.py:435
  40.1 0.6 pad_add_fusion.part_ref
  40.7 1.6 all-to-all-done.lists_ref
  42.3 0.6 slice.100
  43.0 0.5 copy-done
  43.5 42.9 %owner.1 = (bf16[4,128,512]{2,1,0:T(8,128)(2,1)}, bf16[4,128,512]{2,1,0:T(8,128)(2,1)}, bf16[4,128,512]{2,1,0:T(8,128)(2,1)}, bf16[4,128,512]{2,1,0:T(8,128)(2,1...) custom-call(s32[2]{0:T(128)} %pad_add_fusion.part_ref, ...), custom_call_target="tpu_custom_call" | custom-call | tf_op jit(solution)/shard_map/owner/pallas_call | solution.py:323
  86.4 1.1 collective-permute-start.14
  87.6 0.4 collective-permute-start.10
  88.0 1.6 collective-permute-start.20
  89.6 0.6 collective-permute-start.13
  90.3 2.2 collective-permute-start.12
  92.5 4.4 %collective-permute-done.14 = bf16[4,128,512]{2,1,0:T(8,128)(2,1)S(1)} collective-permute-done((bf16[4,128,512]{2,1,0:T(8,128)(2,1)}, bf16[4,128,512]{2,1,0:T(8,128)(2,1)S(1)}, u32[]{:S(2)}, u32[]{:S(2)}) %collective-permute-start.14) | collective-permute-done | bytes 524320 | tf_op jit(solution)/shard_map/ppermute | solution.py:365
  96.9 3.3 %collective-permute-start.4 = (bf16[4,128,512]{2,1,0:T(8,128)(2,1)}, bf16[4,128,512]{2,1,0:T(8,128)(2,1)S(1)}, u32[]{:S(2)}, u32[]{:S(2)}) collective-permute-start(bf16[4,128,512]{2,1,0:T(8,128)(2,1)} %get-tuple-element.35), channel_id=1, source_target_pairs={{0,96},{8,104},{16,112},{24,120},{32,0},{40,8},{48,16},{56,24},{64... | collective-permute-start | bytes 1572872 | tf_op jit(solution)/shard_map/ppermute | solution.py:365
  100.2 1.2 add_convert_fusion
  101.4 1.0 collective-permute-start
  102.4 1.2 add_convert_fusion.1
  103.5 3.6 %collective-permute-done.4 = bf16[4,128,512]{2,1,0:T(8,128)(2,1)S(1)} collective-permute-done((bf16[4,128,512]{2,1,0:T(8,128)(2,1)}, bf16[4,128,512]{2,1,0:T(8,128)(2,1)S(1)}, u32[]{:S(2)}, u32[]{:S(2)}) %collective-permute-start.4) | collective-permute-done | bytes 524320 | tf_op jit(solution)/shard_map/ppermute | solution.py:365
  107.1 4.4 %collective-permute-start.15 = (bf16[4,128,512]{2,1,0:T(8,128)(2,1)S(1)}, bf16[4,128,512]{2,1,0:T(8,128)(2,1)S(1)}, u32[]{:S(2)}, u32[]{:S(2)}) collective-permute-start(bf16[4,128,512]{2,1,0:T(8,128)(2,1)S(1)} %add_convert_fusion), channel_id=1, source_target_pairs={{0,24},{8,0},{16,8},{24,16},{32,56},{40,32},{48,40},{56,48},{64,88... | collective-permute-start | bytes 1572872 | tf_op jit(solution)/shard_map/ppermute | solution.py:365
  111.5 1.2 add_convert_fusion.2
  112.7 0.4 collective-permute-start.11
  113.1 1.2 add_convert_fusion.3
  114.3 0.6 collective-permute-start.3
  115.0 3.3 %collective-permute-done.15 = bf16[4,128,512]{2,1,0:T(8,128)(2,1)S(1)} collective-permute-done((bf16[4,128,512]{2,1,0:T(8,128)(2,1)S(1)}, bf16[4,128,512]{2,1,0:T(8,128)(2,1)S(1)}, u32[]{:S(2)}, u32[]{:S(2)}) %collective-permute-start.15) | collective-permute-done | bytes 524320 | tf_op jit(solution)/shard_map/ppermute | solution.py:365
  118.3 3.5 %collective-permute-start.2 = (bf16[4,128,512]{2,1,0:T(8,128)(2,1)}, bf16[4,128,512]{2,1,0:T(8,128)(2,1)S(1)}, u32[]{:S(2)}, u32[]{:S(2)}) collective-permute-start(bf16[4,128,512]{2,1,0:T(8,128)(2,1)} %get-tuple-element.31), channel_id=1, source_target_pairs={{0,96},{8,104},{16,112},{24,120},{32,0},{40,8},{48,16},{56,24},{64... | collective-permute-start | bytes 1572872 | tf_op jit(solution)/shard_map/ppermute | solution.py:365
  121.8 1.3 fusion.16
  123.2 3.1 %collective-permute-done.11 = bf16[4,128,512]{2,1,0:T(8,128)(2,1)S(1)} collective-permute-done((bf16[4,128,512]{2,1,0:T(8,128)(2,1)S(1)}, bf16[4,128,512]{2,1,0:T(8,128)(2,1)S(1)}, u32[]{:S(2)}, u32[]{:S(2)}) %collective-permute-start.11) | collective-permute-done | bytes 524320 | tf_op jit(solution)/shard_map/ppermute | solution.py:365
  126.6 0.9 pad_maximum_fusion.2
  127.5 0.6 collective-permute-start.22
  128.1 0.9 collective-permute-start.21
  129.1 10.2 %collective-permute-done.5 = bf16[4,128,512]{2,1,0:T(8,128)(2,1)S(1)} collective-permute-done((bf16[4,128,512]{2,1,0:T(8,128)(2,1)S(1)}, bf16[4,128,512]{2,1,0:T(8,128)(2,1)S(1)}, u32[]{:S(2)}, u32[]{:S(2)}) %collective-permute-start.5) | collective-permute-done | bytes 524320 | tf_op jit(solution)/shard_map/ppermute | solution.py:365
  139.3 0.8 collective-permute-start.16
  140.1 1.2 fusion.18
  141.3 2.6 %collective-permute-start.18 = (bf16[2,128,512]{2,1,0:T(8,128)(2,1)S(1)}, bf16[2,128,512]{2,1,0:T(8,128)(2,1)S(1)}, u32[]{:S(2)}, u32[]{:S(2)}) collective-permute-start(bf16[2,128,512]{2,1,0:T(8,128)(2,1)S(1)} %pad_maximum_fusion.3), channel_id=1, source_target_pairs={{0,96},{8,104},{16,112},{24,120},{32,0},{40,8},{48,16},{56,24},{64... | collective-permute-start | bytes 786440 | tf_op jit(solution)/shard_map/ppermute | solution.py:365
  144.2 0.8 copy-done.3
  145.1 0.7 pad_maximum_fusion
  145.8 11.2 %collective-permute-start.6 = (bf16[2,128,512]{2,1,0:T(8,128)(2,1)}, bf16[2,128,512]{2,1,0:T(8,128)(2,1)}, u32[]{:S(2)}, u32[]{:S(2)}) collective-permute-start(bf16[2,128,512]{2,1,0:T(8,128)(2,1)} %pad_maximum_fusion), channel_id=1, source_target_pairs={{0,8},{8,16},{16,24},{24,0},{32,40},{40,48},{48,56},{56,32},{64,72... | collective-permute-start | bytes 786440 | tf_op jit(solution)/shard_map/ppermute | solution.py:365
  157.0 0.7 pad_maximum_fusion.1
  157.8 0.6 reshape.80.refs_6_
  158.5 0.9 add_convert_fusion.4
  159.4 4.4 %collective-permute-start.23 = (bf16[1024,512]{1,0:T(8,128)(2,1)}, bf16[1024,512]{1,0:T(8,128)(2,1)}, u32[]{:S(2)}, u32[]{:S(2)}) collective-permute-start(bf16[1024,512]{1,0:T(8,128)(2,1)} %refs_8_.1), channel_id=1, source_target_pairs={{0,1},{1,0},{2,3},{3,2},{4,5},{5,4},{6,7},{7,6},{8,9},{9,8},{10,11... | collective-permute-start | bytes 3145736 | tf_op jit(solution)/shard_map/ppermute | solution.py:408
  163.9 0.4 collective-permute-start.26
  164.4 0.4 collective-permute-start.25
  164.7 3.1 %collective-permute-start.19 = (bf16[1,128,512]{2,1,0:T(8,128)(2,1)S(1)}, bf16[1,128,512]{2,1,0:T(8,128)(2,1)S(1)}, u32[]{:S(2)}, u32[]{:S(2)}) collective-permute-start(bf16[1,128,512]{2,1,0:T(8,128)(2,1)S(1)} %add_convert_fusion.4), channel_id=1, source_target_pairs={{0,96},{8,104},{16,112},{24,120},{32,0},{40,8},{48,16},{56,24},{64... | collective-permute-start | bytes 393224 | tf_op jit(solution)/shard_map/ppermute | solution.py:365
  167.9 1.0 add_convert_fusion.6
  168.9 0.9 collective-permute-done.19
  169.8 2.2 collective-permute-start.9
  172.0 1.8 fusion.3
  174.0 0.3 collective-permute-start.17
  174.3 1.9 fusion.7
  176.2 3.2 %collective-permute-done.17 = bf16[1,128,512]{2,1,0:T(8,128)(2,1)S(1)} collective-permute-done((bf16[1,128,512]{2,1,0:T(8,128)(2,1)S(1)}, bf16[1,128,512]{2,1,0:T(8,128)(2,1)S(1)}, u32[]{:S(2)}, u32[]{:S(2)}) %collective-permute-start.17) | collective-permute-done | bytes 131104 | tf_op jit(solution)/shard_map/ppermute | solution.py:365
  179.4 0.7 collective-permute-start.7
  180.1 0.7 fusion.5.refs_2_
  180.9 4.1 %collective-permute-done.7 = bf16[1,128,512]{2,1,0:T(8,128)(2,1)S(1)} collective-permute-done((bf16[1,128,512]{2,1,0:T(8,128)(2,1)S(1)}, bf16[1,128,512]{2,1,0:T(8,128)(2,1)S(1)}, u32[]{:S(2)}, u32[]{:S(2)}) %collective-permute-start.7) | collective-permute-done | bytes 131104 | tf_op jit(solution)/shard_map/ppermute | solution.py:365
  185.0 1.7 fusion.9.refs_0_
  186.6 11.0 %score.1 = (bf16[512,512]{1,0:T(8,128)(2,1)}, f32[16,512]{1,0:T(8,128)}) custom-call(f32[128,512]{1,0:T(8,128)} %fusion.9.refs_0_, f32[128,512]{1,0:T(8,128)} %get-tuple-element.64.refs_1_, f32[128,512]{1,0:T(8,128)} %fusion.5.refs_2_, f32[128,512]{1,0:T(8,128)} %get-tuple-element.62.refs_3_, s32[1,512]{1,0:T(1,128)} %bitcast.31, f32[1,512]{1,0:T(1,128)} %bitcast.33, ...), custom_call_target="tpu_custom_call" | custom-call | tf_op jit(solution)/shard_map/score/pallas_call | solution.py:515
  197.7 0.8 broadcast_in_dim.51
  198.7 0.6 all_to_all.12
  199.3 27.6 %all_to_all.17 = f32[128,1,1024]{2,1,0:T(1,128)S(1)} all-to-all(f32[128,1,1024]{2,1,0:T(1,128)S(1)} %all_to_all.12), channel_id=1, replica_groups=mesh['neg'=16,'qry'=8] {'neg','qry'}, dimensions={0} | all-to-all | bytes 1048576 | tf_op jit(solution)/shard_map/all_to_all | solution.py:579
  226.9 0.3 reduce_max.9
  227.3 0.6 add_add_fusion
  (49 shorter events, 1.4 us)
Async XLA Ops:
  15.3 27.1 %all-to-all-start = ((s32[16,176,128]{2,1,0:T(8,128)}), s32[16,176,128]{2,1,0:T(8,128)S(1)}, u32[]{:S(2)}, u32[]{:S(2)}) async-start(s32[16,176,128]{2,1,0:T(8,128)} %pack.1), calls=%async_computation | async-start | bytes 2883584 | tf_op jit(solution)/shard_map/all_to_all | solution.py:558
  42.3 1.2 copy-start
  86.4 39.9 %copy-start.7 = (bf16[4,128,512]{2,1,0:T(8,128)(2,1)S(1)}, bf16[4,128,512]{2,1,0:T(8,128)(2,1)}, u32[]{:S(2)}) copy-start(bf16[4,128,512]{2,1,0:T(8,128)(2,1)} %get-tuple-element.36) | copy-start | bytes 1572868
  86.4 53.7 %copy-start.6 = (bf16[4,128,512]{2,1,0:T(8,128)(2,1)S(1)}, bf16[4,128,512]{2,1,0:T(8,128)(2,1)}, u32[]{:S(2)}) copy-start(bf16[4,128,512]{2,1,0:T(8,128)(2,1)} %get-tuple-element.32) | copy-start | bytes 1572868
  86.4 10.4 %collective-permute-start.14 = (bf16[4,128,512]{2,1,0:T(8,128)(2,1)}, bf16[4,128,512]{2,1,0:T(8,128)(2,1)S(1)}, u32[]{:S(2)}, u32[]{:S(2)}) collective-permute-start(bf16[4,128,512]{2,1,0:T(8,128)(2,1)} %get-tuple-element.43), channel_id=1, source_target_pairs={{0,24},{8,0},{16,8},{24,16},{32,56},{40,32},{48,40},{56,48},{64,88... | collective-permute-start | bytes 1572872 | tf_op jit(solution)/shard_map/ppermute | solution.py:365
  87.6 13.8 %collective-permute-start.10 = (bf16[4,128,512]{2,1,0:T(8,128)(2,1)}, bf16[4,128,512]{2,1,0:T(8,128)(2,1)S(1)}, u32[]{:S(2)}, u32[]{:S(2)}) collective-permute-start(bf16[4,128,512]{2,1,0:T(8,128)(2,1)} %get-tuple-element.38), channel_id=1, source_target_pairs={{0,8},{8,16},{16,24},{24,0},{32,40},{40,48},{48,56},{56,32},{64,72... | collective-permute-start | bytes 1572872 | tf_op jit(solution)/shard_map/ppermute | solution.py:365
  88.0 39.5 %collective-permute-start.20 = (bf16[1024,512]{1,0:T(8,128)(2,1)}, bf16[1024,512]{1,0:T(8,128)(2,1)}, u32[]{:S(2)}, u32[]{:S(2)}) collective-permute-start(bf16[1024,512]{1,0:T(8,128)(2,1)} %refs_8_.1), channel_id=1, source_target_pairs={{0,2},{1,3},{2,4},{3,5},{4,6},{5,7},{6,0},{7,1},{8,10},{9,11},{10,... | collective-permute-start | bytes 3145736 | tf_op jit(solution)/shard_map/ppermute | solution.py:408
  89.6 24.7 %collective-permute-start.13 = (bf16[4,128,512]{2,1,0:T(8,128)(2,1)}, bf16[4,128,512]{2,1,0:T(8,128)(2,1)S(1)}, u32[]{:S(2)}, u32[]{:S(2)}) collective-permute-start(bf16[4,128,512]{2,1,0:T(8,128)(2,1)} %get-tuple-element.41), channel_id=1, source_target_pairs={{0,8},{8,16},{16,24},{24,0},{32,40},{40,48},{48,56},{56,32},{64,72... | collective-permute-start | bytes 1572872 | tf_op jit(solution)/shard_map/ppermute | solution.py:365
  90.3 32.8 %collective-permute-start.12 = (bf16[4,128,512]{2,1,0:T(8,128)(2,1)}, bf16[4,128,512]{2,1,0:T(8,128)(2,1)S(1)}, u32[]{:S(2)}, u32[]{:S(2)}) collective-permute-start(bf16[4,128,512]{2,1,0:T(8,128)(2,1)} %get-tuple-element.39), channel_id=1, source_target_pairs={{0,24},{8,0},{16,8},{24,16},{32,56},{40,32},{48,40},{56,48},{64,88... | collective-permute-start | bytes 1572872 | tf_op jit(solution)/shard_map/ppermute | solution.py:365
  96.9 10.2 %collective-permute-start.4 = (bf16[4,128,512]{2,1,0:T(8,128)(2,1)}, bf16[4,128,512]{2,1,0:T(8,128)(2,1)S(1)}, u32[]{:S(2)}, u32[]{:S(2)}) collective-permute-start(bf16[4,128,512]{2,1,0:T(8,128)(2,1)} %get-tuple-element.35), channel_id=1, source_target_pairs={{0,96},{8,104},{16,112},{24,120},{32,0},{40,8},{48,16},{56,24},{64... | collective-permute-start | bytes 1572872 | tf_op jit(solution)/shard_map/ppermute | solution.py:365
  101.4 42.6 %copy-start.5 = (bf16[4,128,512]{2,1,0:T(8,128)(2,1)S(1)}, bf16[4,128,512]{2,1,0:T(8,128)(2,1)}, u32[]{:S(2)}) copy-start(bf16[4,128,512]{2,1,0:T(8,128)(2,1)} %get-tuple-element.28) | copy-start | bytes 1572868
  101.4 11.3 %collective-permute-start = (bf16[4,128,512]{2,1,0:T(8,128)(2,1)}, bf16[4,128,512]{2,1,0:T(8,128)(2,1)S(1)}, u32[]{:S(2)}, u32[]{:S(2)}) collective-permute-start(bf16[4,128,512]{2,1,0:T(8,128)(2,1)} %get-tuple-element.30), channel_id=1, source_target_pairs={{0,32},{8,40},{16,48},{24,56},{32,64},{40,72},{48,80},{56,88},{64,... | collective-permute-start | bytes 1572872 | tf_op jit(solution)/shard_map/ppermute | solution.py:365
  107.1 11.2 %collective-permute-start.15 = (bf16[4,128,512]{2,1,0:T(8,128)(2,1)S(1)}, bf16[4,128,512]{2,1,0:T(8,128)(2,1)S(1)}, u32[]{:S(2)}, u32[]{:S(2)}) collective-permute-start(bf16[4,128,512]{2,1,0:T(8,128)(2,1)S(1)} %add_convert_fusion), channel_id=1, source_target_pairs={{0,24},{8,0},{16,8},{24,16},{32,56},{40,32},{48,40},{56,48},{64,88... | collective-permute-start | bytes 1572872 | tf_op jit(solution)/shard_map/ppermute | solution.py:365
  112.7 13.6 %collective-permute-start.11 = (bf16[4,128,512]{2,1,0:T(8,128)(2,1)S(1)}, bf16[4,128,512]{2,1,0:T(8,128)(2,1)S(1)}, u32[]{:S(2)}, u32[]{:S(2)}) collective-permute-start(bf16[4,128,512]{2,1,0:T(8,128)(2,1)S(1)} %add_convert_fusion.1), channel_id=1, source_target_pairs={{0,8},{8,16},{16,24},{24,0},{32,40},{40,48},{48,56},{56,32},{64,72... | collective-permute-start | bytes 1572872 | tf_op jit(solution)/shard_map/ppermute | solution.py:365
  114.3 13.8 %collective-permute-start.3 = (bf16[4,128,512]{2,1,0:T(8,128)(2,1)}, bf16[4,128,512]{2,1,0:T(8,128)(2,1)S(1)}, u32[]{:S(2)}, u32[]{:S(2)}) collective-permute-start(bf16[4,128,512]{2,1,0:T(8,128)(2,1)} %get-tuple-element.33), channel_id=1, source_target_pairs={{0,32},{8,40},{16,48},{24,56},{32,64},{40,72},{48,80},{56,88},{64,... | collective-permute-start | bytes 1572872 | tf_op jit(solution)/shard_map/ppermute | solution.py:365
  118.3 23.0 %collective-permute-start.2 = (bf16[4,128,512]{2,1,0:T(8,128)(2,1)}, bf16[4,128,512]{2,1,0:T(8,128)(2,1)S(1)}, u32[]{:S(2)}, u32[]{:S(2)}) collective-permute-start(bf16[4,128,512]{2,1,0:T(8,128)(2,1)} %get-tuple-element.31), channel_id=1, source_target_pairs={{0,96},{8,104},{16,112},{24,120},{32,0},{40,8},{48,16},{56,24},{64... | collective-permute-start | bytes 1572872 | tf_op jit(solution)/shard_map/ppermute | solution.py:365
  121.8 36.0 %copy-start.8 = (s32[4096]{0:T(1024)S(1)}, s32[4096]{0:T(1024)}, u32[]{:S(2)}) copy-start(s32[4096]{0:T(1024)} %param.17) | copy-start | bytes 49156
  123.1 20.8 %copy-start.2 = (bf16[4,128,512]{2,1,0:T(8,128)(2,1)}, bf16[4,128,512]{2,1,0:T(8,128)(2,1)S(1)}, u32[]{:S(2)}) copy-start(bf16[4,128,512]{2,1,0:T(8,128)(2,1)S(1)} %get-tuple-element.48) | copy-start | bytes 1572868
  123.1 16.1 %collective-permute-start.5 = (bf16[4,128,512]{2,1,0:T(8,128)(2,1)S(1)}, bf16[4,128,512]{2,1,0:T(8,128)(2,1)S(1)}, u32[]{:S(2)}, u32[]{:S(2)}) collective-permute-start(bf16[4,128,512]{2,1,0:T(8,128)(2,1)S(1)} %add_convert_fusion.2), channel_id=1, source_target_pairs={{0,96},{8,104},{16,112},{24,120},{32,0},{40,8},{48,16},{56,24},{64... | collective-permute-start | bytes 1572872 | tf_op jit(solution)/shard_map/ppermute | solution.py:365
  126.3 17.7 %collective-permute-start.1 = (bf16[4,128,512]{2,1,0:T(8,128)(2,1)S(1)}, bf16[4,128,512]{2,1,0:T(8,128)(2,1)S(1)}, u32[]{:S(2)}, u32[]{:S(2)}) collective-permute-start(bf16[4,128,512]{2,1,0:T(8,128)(2,1)S(1)} %add_convert_fusion.3), channel_id=1, source_target_pairs={{0,32},{8,40},{16,48},{24,56},{32,64},{40,72},{48,80},{56,88},{64,... | collective-permute-start | bytes 1572872 | tf_op jit(solution)/shard_map/ppermute | solution.py:365
  126.5 17.4 %copy-start.1 = (bf16[4,128,512]{2,1,0:T(8,128)(2,1)}, bf16[4,128,512]{2,1,0:T(8,128)(2,1)S(1)}, u32[]{:S(2)}) copy-start(bf16[4,128,512]{2,1,0:T(8,128)(2,1)S(1)} %get-tuple-element.46) | copy-start | bytes 1572868
  127.5 31.9 %collective-permute-start.22 = (bf16[1024,512]{1,0:T(8,128)(2,1)}, bf16[1024,512]{1,0:T(8,128)(2,1)}, u32[]{:S(2)}, u32[]{:S(2)}) collective-permute-start(bf16[1024,512]{1,0:T(8,128)(2,1)} %refs_8_.1), channel_id=1, source_target_pairs={{0,6},{1,7},{2,0},{3,1},{4,2},{5,3},{6,4},{7,5},{8,14},{9,15},{10,... | collective-permute-start | bytes 3145736 | tf_op jit(solution)/shard_map/ppermute | solution.py:408
  128.1 35.7 %collective-permute-start.21 = (bf16[1024,512]{1,0:T(8,128)(2,1)}, bf16[1024,512]{1,0:T(8,128)(2,1)}, u32[]{:S(2)}, u32[]{:S(2)}) collective-permute-start(bf16[1024,512]{1,0:T(8,128)(2,1)} %collective-permute-done.20.refs_9_), channel_id=1, source_target_pairs={{0,2},{1,3},{2,4},{3,5},{4,6},{5,7},{6,0},{7,1},{8,10},{9,11},{10,... | collective-permute-start | bytes 3145736 | tf_op jit(solution)/shard_map/ppermute | solution.py:408
  139.3 24.7 %collective-permute-start.16 = (bf16[2,128,512]{2,1,0:T(8,128)(2,1)}, bf16[2,128,512]{2,1,0:T(8,128)(2,1)}, u32[]{:S(2)}, u32[]{:S(2)}) collective-permute-start(bf16[2,128,512]{2,1,0:T(8,128)(2,1)} %pad_maximum_fusion.2), channel_id=1, source_target_pairs={{0,32},{8,40},{16,48},{24,56},{32,64},{40,72},{48,80},{56,88},{64,... | collective-permute-start | bytes 786440 | tf_op jit(solution)/shard_map/ppermute | solution.py:365
  141.3 3.7 %copy-start.4 = (bf16[4,128,512]{2,1,0:T(8,128)(2,1)}, bf16[4,128,512]{2,1,0:T(8,128)(2,1)S(1)}, u32[]{:S(2)}) copy-start(bf16[4,128,512]{2,1,0:T(8,128)(2,1)S(1)} %get-tuple-element.52) | copy-start | bytes 1572868
  141.3 16.4 %collective-permute-start.18 = (bf16[2,128,512]{2,1,0:T(8,128)(2,1)S(1)}, bf16[2,128,512]{2,1,0:T(8,128)(2,1)S(1)}, u32[]{:S(2)}, u32[]{:S(2)}) collective-permute-start(bf16[2,128,512]{2,1,0:T(8,128)(2,1)S(1)} %pad_maximum_fusion.3), channel_id=1, source_target_pairs={{0,96},{8,104},{16,112},{24,120},{32,0},{40,8},{48,16},{56,24},{64... | collective-permute-start | bytes 786440 | tf_op jit(solution)/shard_map/ppermute | solution.py:365
  144.2 0.8 copy-start.3
  145.8 18.6 %collective-permute-start.6 = (bf16[2,128,512]{2,1,0:T(8,128)(2,1)}, bf16[2,128,512]{2,1,0:T(8,128)(2,1)}, u32[]{:S(2)}, u32[]{:S(2)}) collective-permute-start(bf16[2,128,512]{2,1,0:T(8,128)(2,1)} %pad_maximum_fusion), channel_id=1, source_target_pairs={{0,8},{8,16},{16,24},{24,0},{32,40},{40,48},{48,56},{56,32},{64,72... | collective-permute-start | bytes 786440 | tf_op jit(solution)/shard_map/ppermute | solution.py:365
  157.7 7.0 %collective-permute-start.8 = (bf16[2,128,512]{2,1,0:T(8,128)(2,1)}, bf16[2,128,512]{2,1,0:T(8,128)(2,1)}, u32[]{:S(2)}, u32[]{:S(2)}) collective-permute-start(bf16[2,128,512]{2,1,0:T(8,128)(2,1)} %pad_maximum_fusion.1), channel_id=1, source_target_pairs={{0,24},{8,0},{16,8},{24,16},{32,56},{40,32},{48,40},{56,48},{64,88... | collective-permute-start | bytes 786440 | tf_op jit(solution)/shard_map/ppermute | solution.py:365
  159.4 27.2 %collective-permute-start.23 = (bf16[1024,512]{1,0:T(8,128)(2,1)}, bf16[1024,512]{1,0:T(8,128)(2,1)}, u32[]{:S(2)}, u32[]{:S(2)}) collective-permute-start(bf16[1024,512]{1,0:T(8,128)(2,1)} %refs_8_.1), channel_id=1, source_target_pairs={{0,1},{1,0},{2,3},{3,2},{4,5},{5,4},{6,7},{7,6},{8,9},{9,8},{10,11... | collective-permute-start | bytes 3145736 | tf_op jit(solution)/shard_map/ppermute | solution.py:408
  163.8 22.8 %collective-permute-start.24 = (bf16[1024,512]{1,0:T(8,128)(2,1)}, bf16[1024,512]{1,0:T(8,128)(2,1)}, u32[]{:S(2)}, u32[]{:S(2)}) collective-permute-start(bf16[1024,512]{1,0:T(8,128)(2,1)} %collective-permute-done.20.refs_9_), channel_id=1, source_target_pairs={{0,1},{1,0},{2,3},{3,2},{4,5},{5,4},{6,7},{7,6},{8,9},{9,8},{10,11... | collective-permute-start | bytes 3145736 | tf_op jit(solution)/shard_map/ppermute | solution.py:408
  163.9 22.7 %collective-permute-start.26 = (bf16[1024,512]{1,0:T(8,128)(2,1)}, bf16[1024,512]{1,0:T(8,128)(2,1)}, u32[]{:S(2)}, u32[]{:S(2)}) collective-permute-start(bf16[1024,512]{1,0:T(8,128)(2,1)} %collective-permute-done.22.refs_11_), channel_id=1, source_target_pairs={{0,1},{1,0},{2,3},{3,2},{4,5},{5,4},{6,7},{7,6},{8,9},{9,8},{10,11... | collective-permute-start | bytes 3145736 | tf_op jit(solution)/shard_map/ppermute | solution.py:408
  164.4 22.3 %collective-permute-start.25 = (bf16[1024,512]{1,0:T(8,128)(2,1)}, bf16[1024,512]{1,0:T(8,128)(2,1)}, u32[]{:S(2)}, u32[]{:S(2)}) collective-permute-start(bf16[1024,512]{1,0:T(8,128)(2,1)} %collective-permute-done.21.refs_10_), channel_id=1, source_target_pairs={{0,1},{1,0},{2,3},{3,2},{4,5},{5,4},{6,7},{7,6},{8,9},{9,8},{10,11... | collective-permute-start | bytes 3145736 | tf_op jit(solution)/shard_map/ppermute | solution.py:408
  164.7 5.1 %collective-permute-start.19 = (bf16[1,128,512]{2,1,0:T(8,128)(2,1)S(1)}, bf16[1,128,512]{2,1,0:T(8,128)(2,1)S(1)}, u32[]{:S(2)}, u32[]{:S(2)}) collective-permute-start(bf16[1,128,512]{2,1,0:T(8,128)(2,1)S(1)} %add_convert_fusion.4), channel_id=1, source_target_pairs={{0,96},{8,104},{16,112},{24,120},{32,0},{40,8},{48,16},{56,24},{64... | collective-permute-start | bytes 393224 | tf_op jit(solution)/shard_map/ppermute | solution.py:365
  169.8 4.1 %collective-permute-start.9 = (bf16[1,128,512]{2,1,0:T(8,128)(2,1)S(1)}, bf16[1,128,512]{2,1,0:T(8,128)(2,1)S(1)}, u32[]{:S(2)}, u32[]{:S(2)}) collective-permute-start(bf16[1,128,512]{2,1,0:T(8,128)(2,1)S(1)} %add_convert_fusion.6), channel_id=1, source_target_pairs={{0,24},{8,0},{16,8},{24,16},{32,56},{40,32},{48,40},{56,48},{64,88... | collective-permute-start | bytes 393224 | tf_op jit(solution)/shard_map/ppermute | solution.py:365
  174.0 5.4 %collective-permute-start.17 = (bf16[1,128,512]{2,1,0:T(8,128)(2,1)S(1)}, bf16[1,128,512]{2,1,0:T(8,128)(2,1)S(1)}, u32[]{:S(2)}, u32[]{:S(2)}) collective-permute-start(bf16[1,128,512]{2,1,0:T(8,128)(2,1)S(1)} %get-tuple-element.63), channel_id=1, source_target_pairs={{0,32},{8,40},{16,48},{24,56},{32,64},{40,72},{48,80},{56,88},{64,... | collective-permute-start | bytes 393224 | tf_op jit(solution)/shard_map/ppermute | solution.py:365
  179.4 5.5 %collective-permute-start.7 = (bf16[1,128,512]{2,1,0:T(8,128)(2,1)S(1)}, bf16[1,128,512]{2,1,0:T(8,128)(2,1)S(1)}, u32[]{:S(2)}, u32[]{:S(2)}) collective-permute-start(bf16[1,128,512]{2,1,0:T(8,128)(2,1)S(1)} %get-tuple-element.65), channel_id=1, source_target_pairs={{0,8},{8,16},{16,24},{24,0},{32,40},{40,48},{48,56},{56,32},{64,72... | collective-permute-start | bytes 393224 | tf_op jit(solution)/shard_map/ppermute | solution.py:365

commit v4 on v3

--- a/solution.py
+++ b/solution.py
@@ -15,11 +15,11 @@
 BLOCK = 10
 USUAL = 8
 STAGE = 1024
-DEEP = 4
+DEEP = 8
 LINES = 176
 COUNTS = 165
 SIDE = 4
-SCORED = 512
+SCORED = 1024
 LOG2E = 1.4426950408889634
 MESSAGES = 2 * SIDE
 
@@ -463,7 +463,7 @@
     def columns(row):
         return jnp.broadcast_to(row, (LANES, negatives)).T
 
-    own = log_ref[pl.ds(place_ref[0], 1), :]
+    own = log_ref[:, pl.ds(pl.multiple_of(place_ref[0] * negatives, negatives), negatives)]
     logs[...] = columns(jnp.log(own.astype(f32)) * LOG2E)
     counts = columns(count_ref[...].astype(f32))
     quarter = negatives // 4
@@ -486,13 +486,19 @@
             peak = jnp.max(scores, axis=0, keepdims=True)
             total = jnp.sum(jnp.exp2(scores - peak), axis=0, keepdims=True)
             found.append((peak + jnp.log2(total)) * (1.0 / LOG2E))
-        lse_ref[pl.ds(i, 1), :] = jnp.concatenate(found, axis=1)
+        found = jnp.concatenate(found, axis=1)
+        z, core = place_ref[0] >> 1, place_ref[0] & 1
+        group = ((z - (i & (SIDE - 1))) & (SIDE - 1)) * 2 + (core ^ (i // SIDE))
+        for a in range(lse_ref.shape[0] // len(queries)):
+            lse_ref[a * len(queries) + group] = found
 
     copy(0, queries[0]).wait()
     even[...] = products(0)
 
     def pair(i, _):
         following = jnp.minimum(2 * i + 2, blocks - 1)
+        if per_query == 1:
+            copy(2 * i + 1, queries[0]).wait()
 
         @pl.when((following % per_query == 0) & (2 * i + 2 < blocks))
         def _():
@@ -507,7 +513,7 @@
     lax.fori_loop(0, blocks // 2, pair, 0)
 
 
-def scored(sums, count, bias, counts_all, place, queries):
+def scored(sums, count, bias, counts_all, place, queries, parts):
     negatives = count.shape[0]
     rows, width = queries[0].shape
     total = rows * len(queries)
@@ -520,7 +526,7 @@
         out_specs=[in_vmem] * 2,
         out_shape=[
             jax.ShapeDtypeStruct((negatives, width), jnp.bfloat16),
-            jax.ShapeDtypeStruct((total // SCORED, SCORED), jnp.float32),
+            jax.ShapeDtypeStruct((parts * len(queries), 1, rows), jnp.float32),
         ],
         scratch_shapes=[
             pltpu.VMEM((total, width), jnp.bfloat16),
@@ -565,20 +571,11 @@
     sums = [q[0] for q in scattered_sums(outs)]
 
     here = lax.axis_index("qry")
-    counts_all = negative_count.reshape(groups, negatives)
-    negative_embed, part_lse = scored(
-        sums, neighbour_count, output_bias, counts_all, here.reshape(1), query_blocks
+    negative_embed, shared = scored(
+        sums, neighbour_count, output_bias, negative_count[None, :], here.reshape(1), query_blocks, parts
     )
-    z, core = here // 2, here % 2
-    group = jnp.arange(groups)
-    source = ((z - group // 2) % SIDE) + SIDE * ((group % 2) ^ core)
-    picked = source[:, None] == group[None, :]
-    blocks = part_lse.reshape(groups, -1)
-    blocks = jnp.sum(jnp.where(picked[:, :, None], blocks[None], 0.0), axis=1)
-    shared = jnp.broadcast_to(blocks[None], (parts, groups, queries.shape[0]))
-    parts_lse = lax.all_to_all(
-        shared.reshape(parts * groups, -1), ("neg", "qry"), split_axis=0, concat_axis=0, tiled=True
-    )
+    parts_lse = lax.all_to_all(shared, ("neg", "qry"), split_axis=0, concat_axis=0, tiled=True)
+    parts_lse = parts_lse.reshape(parts * groups, -1)
     top = jnp.max(parts_lse, axis=0)
     query_lse = top + jnp.log(jnp.sum(jnp.exp(parts_lse - top[None, :]), axis=0))
     return (negative_embed, query_lse - math.log(negatives * parts * groups))

time: 229 us -> 226 us (0.987)
  transfers between devices with their start and end apart: 28 -> 28, of which waited for: 10 -> 10; matrix products, arithmetic and copies ran while one was open for 9% -> 8% of each run, Pallas kernels for 8% -> 8%
where the time goes in v4:
time: 226 us; the launch traced here: 225 us
  Pallas kernels  74.3 us (33%)
  starting transfers between devices  55.4 us (25%)
  waiting for transfers between devices  34.4 us (15%)
  other arithmetic  29.6 us (13%)
  blocking collectives  28.3 us (13%)
    pallas_call x1, Pallas kernels, owner_sums(): pl.pallas_call(owner_kernel, grid=(devices,), in_specs=[pl.BlockSpec(memo...  41.9 us
    ppermute x20, starting transfers between devices, moved(): return lax.ppermute(x, 'neg', [(i, place(i)) for i in range(SIDE * SIDE)])  38.7 us
    ppermute x20, waiting for transfers between devices, moved(): return lax.ppermute(x, 'neg', [(i, place(i)) for i in range(SIDE * SIDE)])  32.8 us
    all_to_all x1, blocking collectives, per_device(): lax.all_to_all(shared, ('neg', 'qry'), split_axis=0, concat_axis=0, tiled...  28.3 us
    pallas_call x1, Pallas kernels, tables(): pl.pallas_call(table_kernel, grid=(items // STAGE,), in_specs=[block, wei...  17.2 us
    pallas_call x1, Pallas kernels, scored(): pl.pallas_call(score_kernel, in_specs=[in_vmem] * 7 + [pl.BlockSpec(memor...  10.4 us
    sort x1, other arithmetic, per_device(): ordered = lax.sort(keys.reshape(-1), is_stable=False).reshape(keys.shape)  9.88 us
    ppermute x7, starting transfers between devices, turned(): return lax.ppermute(x, 'qry', [(i, place(i)) for i in range(2 * SIDE)])  9.1 us
  transfers between devices with their start and end apart: 28, of which 10 were waited for; matrix products, arithmetic and copies ran while one was open for 8% of the time, Pallas kernels for 8%

profile of v4, /device:TPU:1, one launch (start us, length us, event | category | flops | bytes accessed | tf_op | source)
XLA Modules:
  0.0 225.0 jit_solution(17945591825717303118)
XLA Ops:
  0.6 2.6 %compose.1 = (s32[164,128]{1,0:T(8,128)}, s32[1,128]{1,0:T(1,128)}) custom-call(s32[40,512]{1,0:T(8,128)} %bitcast.28, s32[1,512]{1,0:T(1,128)} %bitcast.34, s32[1,512]{1,0:T(1,128)} %bitcast.30, s32[16,640]{1,0:T(8,128)} %fetch_ref.1), custom_call_target="tpu_custom_call" | custom-call | tf_op jit(solution)/shard_map/compose/pallas_call | solution.py:303
  3.2 9.9 %sort.7 = s32[20992]{0:T(1024)} sort(s32[20992]{0:T(1024)} %bitcast.27), dimensions={0}, to_apply=%region_0.0 | sort | flops 314880 | bytes 167936 | tf_op jit(solution)/shard_map/sort | solution.py:562
  13.1 2.2 pack.1
  15.3 7.6 %all-to-all-start = ((s32[16,176,128]{2,1,0:T(8,128)}), s32[16,176,128]{2,1,0:T(8,128)S(1)}, u32[]{:S(2)}, u32[]{:S(2)}) async-start(s32[16,176,128]{2,1,0:T(8,128)} %pack.1), calls=%async_computation | async-start | bytes 2883584 | tf_op jit(solution)/shard_map/all_to_all | solution.py:564
  22.9 17.2 %tables.1 = (bf16[8192,512]{1,0:T(8,128)(2,1)}, bf16[8192,512]{1,0:T(8,128)(2,1)}) custom-call(bf16[8192,512]{1,0:T(8,128)(2,1)} %items_ref.1, bf16[512,512]{1,0:T(8,128)(2,1)} %message_ref.1, f32[1,512]{1,0:T(1,128)} %bitcast.36, bf16[512,512]{1,0:T(8,128)(2,1)} %neighbour_ref.1, bf16[512,512]{1,0:T(8,128)(2,1)} %self_ref.1), custom_call_target="tpu_custom_call" | custom-call | tf_op jit(solution)/shard_map/tables/pallas_call | solution.py:435
  40.1 0.6 pad_add_fusion.part_ref
  40.7 1.6 all-to-all-done.lists_ref
  42.3 0.6 slice.100
  43.0 0.5 copy-done
  43.5 41.9 %owner.1 = (bf16[4,128,512]{2,1,0:T(8,128)(2,1)}, bf16[4,128,512]{2,1,0:T(8,128)(2,1)}, bf16[4,128,512]{2,1,0:T(8,128)(2,1)}, bf16[4,128,512]{2,1,0:T(8,128)(2,1...) custom-call(s32[2]{0:T(128)} %pad_add_fusion.part_ref, ...), custom_call_target="tpu_custom_call" | custom-call | tf_op jit(solution)/shard_map/owner/pallas_call | solution.py:323
  85.4 1.1 collective-permute-start.14
  86.6 0.4 collective-permute-start.10
  87.0 1.6 collective-permute-start.20
  88.6 0.6 collective-permute-start.13
  89.2 2.1 collective-permute-start.12
  91.3 4.6 %collective-permute-done.14 = bf16[4,128,512]{2,1,0:T(8,128)(2,1)S(1)} collective-permute-done((bf16[4,128,512]{2,1,0:T(8,128)(2,1)}, bf16[4,128,512]{2,1,0:T(8,128)(2,1)S(1)}, u32[]{:S(2)}, u32[]{:S(2)}) %collective-permute-start.14) | collective-permute-done | bytes 524320 | tf_op jit(solution)/shard_map/ppermute | solution.py:365
  95.9 3.3 %collective-permute-start.4 = (bf16[4,128,512]{2,1,0:T(8,128)(2,1)}, bf16[4,128,512]{2,1,0:T(8,128)(2,1)S(1)}, u32[]{:S(2)}, u32[]{:S(2)}) collective-permute-start(bf16[4,128,512]{2,1,0:T(8,128)(2,1)} %get-tuple-element.35), channel_id=1, source_target_pairs={{0,96},{8,104},{16,112},{24,120},{32,0},{40,8},{48,16},{56,24},{64... | collective-permute-start | bytes 1572872 | tf_op jit(solution)/shard_map/ppermute | solution.py:365
  99.2 1.2 add_convert_fusion
  100.4 1.0 collective-permute-start
  101.4 1.2 add_convert_fusion.1
  102.5 3.6 %collective-permute-done.4 = bf16[4,128,512]{2,1,0:T(8,128)(2,1)S(1)} collective-permute-done((bf16[4,128,512]{2,1,0:T(8,128)(2,1)}, bf16[4,128,512]{2,1,0:T(8,128)(2,1)S(1)}, u32[]{:S(2)}, u32[]{:S(2)}) %collective-permute-start.4) | collective-permute-done | bytes 524320 | tf_op jit(solution)/shard_map/ppermute | solution.py:365
  106.1 4.4 %collective-permute-start.15 = (bf16[4,128,512]{2,1,0:T(8,128)(2,1)S(1)}, bf16[4,128,512]{2,1,0:T(8,128)(2,1)S(1)}, u32[]{:S(2)}, u32[]{:S(2)}) collective-permute-start(bf16[4,128,512]{2,1,0:T(8,128)(2,1)S(1)} %add_convert_fusion), channel_id=1, source_target_pairs={{0,24},{8,0},{16,8},{24,16},{32,56},{40,32},{48,40},{56,48},{64,88... | collective-permute-start | bytes 1572872 | tf_op jit(solution)/shard_map/ppermute | solution.py:365
  110.5 1.2 add_convert_fusion.2
  111.7 0.4 collective-permute-start.11
  112.1 1.2 add_convert_fusion.3
  113.3 0.6 collective-permute-start.3
  114.0 3.3 %collective-permute-done.15 = bf16[4,128,512]{2,1,0:T(8,128)(2,1)S(1)} collective-permute-done((bf16[4,128,512]{2,1,0:T(8,128)(2,1)S(1)}, bf16[4,128,512]{2,1,0:T(8,128)(2,1)S(1)}, u32[]{:S(2)}, u32[]{:S(2)}) %collective-permute-start.15) | collective-permute-done | bytes 524320 | tf_op jit(solution)/shard_map/ppermute | solution.py:365
  117.3 3.5 %collective-permute-start.2 = (bf16[4,128,512]{2,1,0:T(8,128)(2,1)}, bf16[4,128,512]{2,1,0:T(8,128)(2,1)S(1)}, u32[]{:S(2)}, u32[]{:S(2)}) collective-permute-start(bf16[4,128,512]{2,1,0:T(8,128)(2,1)} %get-tuple-element.31), channel_id=1, source_target_pairs={{0,96},{8,104},{16,112},{24,120},{32,0},{40,8},{48,16},{56,24},{64... | collective-permute-start | bytes 1572872 | tf_op jit(solution)/shard_map/ppermute | solution.py:365
  120.8 1.3 fusion.11
  122.2 3.1 %collective-permute-done.11 = bf16[4,128,512]{2,1,0:T(8,128)(2,1)S(1)} collective-permute-done((bf16[4,128,512]{2,1,0:T(8,128)(2,1)S(1)}, bf16[4,128,512]{2,1,0:T(8,128)(2,1)S(1)}, u32[]{:S(2)}, u32[]{:S(2)}) %collective-permute-start.11) | collective-permute-done | bytes 524320 | tf_op jit(solution)/shard_map/ppermute | solution.py:365
  125.2 0.2 fusion.10
  125.5 0.8 pad_maximum_fusion.2
  126.4 0.6 collective-permute-start.22
  127.0 0.9 collective-permute-start.21
  127.9 10.4 %collective-permute-done.5 = bf16[4,128,512]{2,1,0:T(8,128)(2,1)S(1)} collective-permute-done((bf16[4,128,512]{2,1,0:T(8,128)(2,1)S(1)}, bf16[4,128,512]{2,1,0:T(8,128)(2,1)S(1)}, u32[]{:S(2)}, u32[]{:S(2)}) %collective-permute-start.5) | collective-permute-done | bytes 524320 | tf_op jit(solution)/shard_map/ppermute | solution.py:365
  138.2 0.9 collective-permute-start.16
  139.1 1.3 fusion.13
  140.4 2.6 %collective-permute-start.18 = (bf16[2,128,512]{2,1,0:T(8,128)(2,1)S(1)}, bf16[2,128,512]{2,1,0:T(8,128)(2,1)S(1)}, u32[]{:S(2)}, u32[]{:S(2)}) collective-permute-start(bf16[2,128,512]{2,1,0:T(8,128)(2,1)S(1)} %pad_maximum_fusion.3), channel_id=1, source_target_pairs={{0,96},{8,104},{16,112},{24,120},{32,0},{40,8},{48,16},{56,24},{64... | collective-permute-start | bytes 786440 | tf_op jit(solution)/shard_map/ppermute | solution.py:365
  143.0 0.2 fusion.12
  143.3 0.8 copy-done.3
  144.1 0.7 pad_maximum_fusion
  144.8 11.2 %collective-permute-start.6 = (bf16[2,128,512]{2,1,0:T(8,128)(2,1)}, bf16[2,128,512]{2,1,0:T(8,128)(2,1)}, u32[]{:S(2)}, u32[]{:S(2)}) collective-permute-start(bf16[2,128,512]{2,1,0:T(8,128)(2,1)} %pad_maximum_fusion), channel_id=1, source_target_pairs={{0,8},{8,16},{16,24},{24,0},{32,40},{40,48},{48,56},{56,32},{64,72... | collective-permute-start | bytes 786440 | tf_op jit(solution)/shard_map/ppermute | solution.py:365
  156.1 0.7 pad_maximum_fusion.1
  156.9 0.9 add_convert_fusion.4
  157.8 4.4 %collective-permute-start.23 = (bf16[1024,512]{1,0:T(8,128)(2,1)}, bf16[1024,512]{1,0:T(8,128)(2,1)}, u32[]{:S(2)}, u32[]{:S(2)}) collective-permute-start(bf16[1024,512]{1,0:T(8,128)(2,1)} %refs_8_.1), channel_id=1, source_target_pairs={{0,1},{1,0},{2,3},{3,2},{4,5},{5,4},{6,7},{7,6},{8,9},{9,8},{10,11... | collective-permute-start | bytes 3145736 | tf_op jit(solution)/shard_map/ppermute | solution.py:408
  162.4 0.4 collective-permute-start.26
  162.8 1.1 collective-permute-start.25
  163.8 2.5 %collective-permute-start.19 = (bf16[1,128,512]{2,1,0:T(8,128)(2,1)S(1)}, bf16[1,128,512]{2,1,0:T(8,128)(2,1)S(1)}, u32[]{:S(2)}, u32[]{:S(2)}) collective-permute-start(bf16[1,128,512]{2,1,0:T(8,128)(2,1)S(1)} %add_convert_fusion.4), channel_id=1, source_target_pairs={{0,96},{8,104},{16,112},{24,120},{32,0},{40,8},{48,16},{56,24},{64... | collective-permute-start | bytes 393224 | tf_op jit(solution)/shard_map/ppermute | solution.py:365
  166.3 1.0 add_convert_fusion.6
  167.3 0.9 collective-permute-done.19
  168.2 2.2 collective-permute-start.9
  170.4 1.8 fusion.3
  172.2 0.1 collective-permute-done.9
  172.4 0.3 collective-permute-start.17
  172.7 1.9 fusion.7
  174.7 3.2 %collective-permute-done.17 = bf16[1,128,512]{2,1,0:T(8,128)(2,1)S(1)} collective-permute-done((bf16[1,128,512]{2,1,0:T(8,128)(2,1)S(1)}, bf16[1,128,512]{2,1,0:T(8,128)(2,1)S(1)}, u32[]{:S(2)}, u32[]{:S(2)}) %collective-permute-start.17) | collective-permute-done | bytes 131104 | tf_op jit(solution)/shard_map/ppermute | solution.py:365
  177.8 1.4 collective-permute-start.7
  179.2 0.7 fusion.5.refs_2_
  180.0 3.6 %collective-permute-done.7 = bf16[1,128,512]{2,1,0:T(8,128)(2,1)S(1)} collective-permute-done((bf16[1,128,512]{2,1,0:T(8,128)(2,1)S(1)}, bf16[1,128,512]{2,1,0:T(8,128)(2,1)S(1)}, u32[]{:S(2)}, u32[]{:S(2)}) %collective-permute-start.7) | collective-permute-done | bytes 131104 | tf_op jit(solution)/shard_map/ppermute | solution.py:365
  183.6 1.7 fusion.9.refs_0_
  185.2 10.4 %score.1 = (bf16[512,512]{1,0:T(8,128)(2,1)}, f32[128,1,1024]{2,1,0:T(1,128)}) custom-call(f32[128,512]{1,0:T(8,128)} %fusion.9.refs_0_, f32[128,512]{1,0:T(8,128)} %get-tuple-element.64.refs_1_, f32[128,512]{1,0:T(8,128)} %fusion.5.refs_2_, f32[128,512]{1,0:T(8,128)} %get-tuple-element.62.refs_3_, s32[1,512]{1,0:T(1,128)} %bitcast.32, f32[1,512]{1,0:T(1,128)} %bitcast.35, ...), custom_call_target="tpu_custom_call" | custom-call | tf_op jit(solution)/shard_map/score/pallas_call | solution.py:521
  195.6 28.3 %all_to_all.10 = f32[128,1,1024]{2,1,0:T(1,128)S(1)} all-to-all(f32[128,1,1024]{2,1,0:T(1,128)} %get-tuple-element.45), channel_id=1, replica_groups=mesh['neg'=16,'qry'=8] {'neg','qry'}, dimensions={0} | all-to-all | bytes 1048576 | tf_op jit(solution)/shard_map/all_to_all | solution.py:577
  223.9 0.3 reduce_max.9
  224.4 0.6 add_add_fusion
  (40 shorter events, 0.5 us)
Async XLA Ops:
  15.3 27.1 %all-to-all-start = ((s32[16,176,128]{2,1,0:T(8,128)}), s32[16,176,128]{2,1,0:T(8,128)S(1)}, u32[]{:S(2)}, u32[]{:S(2)}) async-start(s32[16,176,128]{2,1,0:T(8,128)} %pack.1), calls=%async_computation | async-start | bytes 2883584 | tf_op jit(solution)/shard_map/all_to_all | solution.py:564
  42.3 1.2 copy-start
  85.4 39.8 %copy-start.7 = (bf16[4,128,512]{2,1,0:T(8,128)(2,1)S(1)}, bf16[4,128,512]{2,1,0:T(8,128)(2,1)}, u32[]{:S(2)}) copy-start(bf16[4,128,512]{2,1,0:T(8,128)(2,1)} %get-tuple-element.36) | copy-start | bytes 1572868
  85.4 53.6 %copy-start.6 = (bf16[4,128,512]{2,1,0:T(8,128)(2,1)S(1)}, bf16[4,128,512]{2,1,0:T(8,128)(2,1)}, u32[]{:S(2)}) copy-start(bf16[4,128,512]{2,1,0:T(8,128)(2,1)} %get-tuple-element.32) | copy-start | bytes 1572868
  85.4 10.4 %collective-permute-start.14 = (bf16[4,128,512]{2,1,0:T(8,128)(2,1)}, bf16[4,128,512]{2,1,0:T(8,128)(2,1)S(1)}, u32[]{:S(2)}, u32[]{:S(2)}) collective-permute-start(bf16[4,128,512]{2,1,0:T(8,128)(2,1)} %get-tuple-element.43), channel_id=1, source_target_pairs={{0,24},{8,0},{16,8},{24,16},{32,56},{40,32},{48,40},{56,48},{64,88... | collective-permute-start | bytes 1572872 | tf_op jit(solution)/shard_map/ppermute | solution.py:365
  86.6 13.8 %collective-permute-start.10 = (bf16[4,128,512]{2,1,0:T(8,128)(2,1)}, bf16[4,128,512]{2,1,0:T(8,128)(2,1)S(1)}, u32[]{:S(2)}, u32[]{:S(2)}) collective-permute-start(bf16[4,128,512]{2,1,0:T(8,128)(2,1)} %get-tuple-element.38), channel_id=1, source_target_pairs={{0,8},{8,16},{16,24},{24,0},{32,40},{40,48},{48,56},{56,32},{64,72... | collective-permute-start | bytes 1572872 | tf_op jit(solution)/shard_map/ppermute | solution.py:365
  87.0 39.4 %collective-permute-start.20 = (bf16[1024,512]{1,0:T(8,128)(2,1)}, bf16[1024,512]{1,0:T(8,128)(2,1)}, u32[]{:S(2)}, u32[]{:S(2)}) collective-permute-start(bf16[1024,512]{1,0:T(8,128)(2,1)} %refs_8_.1), channel_id=1, source_target_pairs={{0,2},{1,3},{2,4},{3,5},{4,6},{5,7},{6,0},{7,1},{8,10},{9,11},{10,... | collective-permute-start | bytes 3145736 | tf_op jit(solution)/shard_map/ppermute | solution.py:408
  88.6 24.7 %collective-permute-start.13 = (bf16[4,128,512]{2,1,0:T(8,128)(2,1)}, bf16[4,128,512]{2,1,0:T(8,128)(2,1)S(1)}, u32[]{:S(2)}, u32[]{:S(2)}) collective-permute-start(bf16[4,128,512]{2,1,0:T(8,128)(2,1)} %get-tuple-element.41), channel_id=1, source_target_pairs={{0,8},{8,16},{16,24},{24,0},{32,40},{40,48},{48,56},{56,32},{64,72... | collective-permute-start | bytes 1572872 | tf_op jit(solution)/shard_map/ppermute | solution.py:365
  89.2 32.9 %collective-permute-start.12 = (bf16[4,128,512]{2,1,0:T(8,128)(2,1)}, bf16[4,128,512]{2,1,0:T(8,128)(2,1)S(1)}, u32[]{:S(2)}, u32[]{:S(2)}) collective-permute-start(bf16[4,128,512]{2,1,0:T(8,128)(2,1)} %get-tuple-element.39), channel_id=1, source_target_pairs={{0,24},{8,0},{16,8},{24,16},{32,56},{40,32},{48,40},{56,48},{64,88... | collective-permute-start | bytes 1572872 | tf_op jit(solution)/shard_map/ppermute | solution.py:365
  95.9 10.2 %collective-permute-start.4 = (bf16[4,128,512]{2,1,0:T(8,128)(2,1)}, bf16[4,128,512]{2,1,0:T(8,128)(2,1)S(1)}, u32[]{:S(2)}, u32[]{:S(2)}) collective-permute-start(bf16[4,128,512]{2,1,0:T(8,128)(2,1)} %get-tuple-element.35), channel_id=1, source_target_pairs={{0,96},{8,104},{16,112},{24,120},{32,0},{40,8},{48,16},{56,24},{64... | collective-permute-start | bytes 1572872 | tf_op jit(solution)/shard_map/ppermute | solution.py:365
  100.4 42.7 %copy-start.5 = (bf16[4,128,512]{2,1,0:T(8,128)(2,1)S(1)}, bf16[4,128,512]{2,1,0:T(8,128)(2,1)}, u32[]{:S(2)}) copy-start(bf16[4,128,512]{2,1,0:T(8,128)(2,1)} %get-tuple-element.28) | copy-start | bytes 1572868
  100.4 11.3 %collective-permute-start = (bf16[4,128,512]{2,1,0:T(8,128)(2,1)}, bf16[4,128,512]{2,1,0:T(8,128)(2,1)S(1)}, u32[]{:S(2)}, u32[]{:S(2)}) collective-permute-start(bf16[4,128,512]{2,1,0:T(8,128)(2,1)} %get-tuple-element.30), channel_id=1, source_target_pairs={{0,32},{8,40},{16,48},{24,56},{32,64},{40,72},{48,80},{56,88},{64,... | collective-permute-start | bytes 1572872 | tf_op jit(solution)/shard_map/ppermute | solution.py:365
  106.1 11.2 %collective-permute-start.15 = (bf16[4,128,512]{2,1,0:T(8,128)(2,1)S(1)}, bf16[4,128,512]{2,1,0:T(8,128)(2,1)S(1)}, u32[]{:S(2)}, u32[]{:S(2)}) collective-permute-start(bf16[4,128,512]{2,1,0:T(8,128)(2,1)S(1)} %add_convert_fusion), channel_id=1, source_target_pairs={{0,24},{8,0},{16,8},{24,16},{32,56},{40,32},{48,40},{56,48},{64,88... | collective-permute-start | bytes 1572872 | tf_op jit(solution)/shard_map/ppermute | solution.py:365
  111.7 13.5 %collective-permute-start.11 = (bf16[4,128,512]{2,1,0:T(8,128)(2,1)S(1)}, bf16[4,128,512]{2,1,0:T(8,128)(2,1)S(1)}, u32[]{:S(2)}, u32[]{:S(2)}) collective-permute-start(bf16[4,128,512]{2,1,0:T(8,128)(2,1)S(1)} %add_convert_fusion.1), channel_id=1, source_target_pairs={{0,8},{8,16},{16,24},{24,0},{32,40},{40,48},{48,56},{56,32},{64,72... | collective-permute-start | bytes 1572872 | tf_op jit(solution)/shard_map/ppermute | solution.py:365
  113.3 13.7 %collective-permute-start.3 = (bf16[4,128,512]{2,1,0:T(8,128)(2,1)}, bf16[4,128,512]{2,1,0:T(8,128)(2,1)S(1)}, u32[]{:S(2)}, u32[]{:S(2)}) collective-permute-start(bf16[4,128,512]{2,1,0:T(8,128)(2,1)} %get-tuple-element.33), channel_id=1, source_target_pairs={{0,32},{8,40},{16,48},{24,56},{32,64},{40,72},{48,80},{56,88},{64,... | collective-permute-start | bytes 1572872 | tf_op jit(solution)/shard_map/ppermute | solution.py:365
  117.3 23.1 %collective-permute-start.2 = (bf16[4,128,512]{2,1,0:T(8,128)(2,1)}, bf16[4,128,512]{2,1,0:T(8,128)(2,1)S(1)}, u32[]{:S(2)}, u32[]{:S(2)}) collective-permute-start(bf16[4,128,512]{2,1,0:T(8,128)(2,1)} %get-tuple-element.31), channel_id=1, source_target_pairs={{0,96},{8,104},{16,112},{24,120},{32,0},{40,8},{48,16},{56,24},{64... | collective-permute-start | bytes 1572872 | tf_op jit(solution)/shard_map/ppermute | solution.py:365
  122.1 21.0 %copy-start.2 = (bf16[4,128,512]{2,1,0:T(8,128)(2,1)}, bf16[4,128,512]{2,1,0:T(8,128)(2,1)S(1)}, u32[]{:S(2)}) copy-start(bf16[4,128,512]{2,1,0:T(8,128)(2,1)S(1)} %get-tuple-element.48) | copy-start | bytes 1572868
  122.1 16.2 %collective-permute-start.5 = (bf16[4,128,512]{2,1,0:T(8,128)(2,1)S(1)}, bf16[4,128,512]{2,1,0:T(8,128)(2,1)S(1)}, u32[]{:S(2)}, u32[]{:S(2)}) collective-permute-start(bf16[4,128,512]{2,1,0:T(8,128)(2,1)S(1)} %add_convert_fusion.2), channel_id=1, source_target_pairs={{0,96},{8,104},{16,112},{24,120},{32,0},{40,8},{48,16},{56,24},{64... | collective-permute-start | bytes 1572872 | tf_op jit(solution)/shard_map/ppermute | solution.py:365
  125.2 17.8 %collective-permute-start.1 = (bf16[4,128,512]{2,1,0:T(8,128)(2,1)S(1)}, bf16[4,128,512]{2,1,0:T(8,128)(2,1)S(1)}, u32[]{:S(2)}, u32[]{:S(2)}) collective-permute-start(bf16[4,128,512]{2,1,0:T(8,128)(2,1)S(1)} %add_convert_fusion.3), channel_id=1, source_target_pairs={{0,32},{8,40},{16,48},{24,56},{32,64},{40,72},{48,80},{56,88},{64,... | collective-permute-start | bytes 1572872 | tf_op jit(solution)/shard_map/ppermute | solution.py:365
  125.5 17.5 %copy-start.1 = (bf16[4,128,512]{2,1,0:T(8,128)(2,1)}, bf16[4,128,512]{2,1,0:T(8,128)(2,1)S(1)}, u32[]{:S(2)}) copy-start(bf16[4,128,512]{2,1,0:T(8,128)(2,1)S(1)} %get-tuple-element.46) | copy-start | bytes 1572868
  126.4 31.4 %collective-permute-start.22 = (bf16[1024,512]{1,0:T(8,128)(2,1)}, bf16[1024,512]{1,0:T(8,128)(2,1)}, u32[]{:S(2)}, u32[]{:S(2)}) collective-permute-start(bf16[1024,512]{1,0:T(8,128)(2,1)} %refs_8_.1), channel_id=1, source_target_pairs={{0,6},{1,7},{2,0},{3,1},{4,2},{5,3},{6,4},{7,5},{8,14},{9,15},{10,... | collective-permute-start | bytes 3145736 | tf_op jit(solution)/shard_map/ppermute | solution.py:408
  127.0 35.3 %collective-permute-start.21 = (bf16[1024,512]{1,0:T(8,128)(2,1)}, bf16[1024,512]{1,0:T(8,128)(2,1)}, u32[]{:S(2)}, u32[]{:S(2)}) collective-permute-start(bf16[1024,512]{1,0:T(8,128)(2,1)} %collective-permute-done.20.refs_9_), channel_id=1, source_target_pairs={{0,2},{1,3},{2,4},{3,5},{4,6},{5,7},{6,0},{7,1},{8,10},{9,11},{10,... | collective-permute-start | bytes 3145736 | tf_op jit(solution)/shard_map/ppermute | solution.py:408
  138.2 24.1 %collective-permute-start.16 = (bf16[2,128,512]{2,1,0:T(8,128)(2,1)}, bf16[2,128,512]{2,1,0:T(8,128)(2,1)}, u32[]{:S(2)}, u32[]{:S(2)}) collective-permute-start(bf16[2,128,512]{2,1,0:T(8,128)(2,1)} %pad_maximum_fusion.2), channel_id=1, source_target_pairs={{0,32},{8,40},{16,48},{24,56},{32,64},{40,72},{48,80},{56,88},{64,... | collective-permute-start | bytes 786440 | tf_op jit(solution)/shard_map/ppermute | solution.py:365
  140.3 3.8 %copy-start.4 = (bf16[4,128,512]{2,1,0:T(8,128)(2,1)}, bf16[4,128,512]{2,1,0:T(8,128)(2,1)S(1)}, u32[]{:S(2)}) copy-start(bf16[4,128,512]{2,1,0:T(8,128)(2,1)S(1)} %get-tuple-element.52) | copy-start | bytes 1572868
  140.4 16.4 %collective-permute-start.18 = (bf16[2,128,512]{2,1,0:T(8,128)(2,1)S(1)}, bf16[2,128,512]{2,1,0:T(8,128)(2,1)S(1)}, u32[]{:S(2)}, u32[]{:S(2)}) collective-permute-start(bf16[2,128,512]{2,1,0:T(8,128)(2,1)S(1)} %pad_maximum_fusion.3), channel_id=1, source_target_pairs={{0,96},{8,104},{16,112},{24,120},{32,0},{40,8},{48,16},{56,24},{64... | collective-permute-start | bytes 786440 | tf_op jit(solution)/shard_map/ppermute | solution.py:365
  143.3 0.8 copy-start.3
  144.8 17.9 %collective-permute-start.6 = (bf16[2,128,512]{2,1,0:T(8,128)(2,1)}, bf16[2,128,512]{2,1,0:T(8,128)(2,1)}, u32[]{:S(2)}, u32[]{:S(2)}) collective-permute-start(bf16[2,128,512]{2,1,0:T(8,128)(2,1)} %pad_maximum_fusion), channel_id=1, source_target_pairs={{0,8},{8,16},{16,24},{24,0},{32,40},{40,48},{48,56},{56,32},{64,72... | collective-permute-start | bytes 786440 | tf_op jit(solution)/shard_map/ppermute | solution.py:365
  156.8 7.0 %collective-permute-start.8 = (bf16[2,128,512]{2,1,0:T(8,128)(2,1)}, bf16[2,128,512]{2,1,0:T(8,128)(2,1)}, u32[]{:S(2)}, u32[]{:S(2)}) collective-permute-start(bf16[2,128,512]{2,1,0:T(8,128)(2,1)} %pad_maximum_fusion.1), channel_id=1, source_target_pairs={{0,24},{8,0},{16,8},{24,16},{32,56},{40,32},{48,40},{56,48},{64,88... | collective-permute-start | bytes 786440 | tf_op jit(solution)/shard_map/ppermute | solution.py:365
  157.8 27.4 %collective-permute-start.23 = (bf16[1024,512]{1,0:T(8,128)(2,1)}, bf16[1024,512]{1,0:T(8,128)(2,1)}, u32[]{:S(2)}, u32[]{:S(2)}) collective-permute-start(bf16[1024,512]{1,0:T(8,128)(2,1)} %refs_8_.1), channel_id=1, source_target_pairs={{0,1},{1,0},{2,3},{3,2},{4,5},{5,4},{6,7},{7,6},{8,9},{9,8},{10,11... | collective-permute-start | bytes 3145736 | tf_op jit(solution)/shard_map/ppermute | solution.py:408
  162.3 23.0 %collective-permute-start.24 = (bf16[1024,512]{1,0:T(8,128)(2,1)}, bf16[1024,512]{1,0:T(8,128)(2,1)}, u32[]{:S(2)}, u32[]{:S(2)}) collective-permute-start(bf16[1024,512]{1,0:T(8,128)(2,1)} %collective-permute-done.20.refs_9_), channel_id=1, source_target_pairs={{0,1},{1,0},{2,3},{3,2},{4,5},{5,4},{6,7},{7,6},{8,9},{9,8},{10,11... | collective-permute-start | bytes 3145736 | tf_op jit(solution)/shard_map/ppermute | solution.py:408
  162.4 22.9 %collective-permute-start.26 = (bf16[1024,512]{1,0:T(8,128)(2,1)}, bf16[1024,512]{1,0:T(8,128)(2,1)}, u32[]{:S(2)}, u32[]{:S(2)}) collective-permute-start(bf16[1024,512]{1,0:T(8,128)(2,1)} %collective-permute-done.22.refs_11_), channel_id=1, source_target_pairs={{0,1},{1,0},{2,3},{3,2},{4,5},{5,4},{6,7},{7,6},{8,9},{9,8},{10,11... | collective-permute-start | bytes 3145736 | tf_op jit(solution)/shard_map/ppermute | solution.py:408
  162.8 22.5 %collective-permute-start.25 = (bf16[1024,512]{1,0:T(8,128)(2,1)}, bf16[1024,512]{1,0:T(8,128)(2,1)}, u32[]{:S(2)}, u32[]{:S(2)}) collective-permute-start(bf16[1024,512]{1,0:T(8,128)(2,1)} %collective-permute-done.21.refs_10_), channel_id=1, source_target_pairs={{0,1},{1,0},{2,3},{3,2},{4,5},{5,4},{6,7},{7,6},{8,9},{9,8},{10,11... | collective-permute-start | bytes 3145736 | tf_op jit(solution)/shard_map/ppermute | solution.py:408
  163.8 4.4 %collective-permute-start.19 = (bf16[1,128,512]{2,1,0:T(8,128)(2,1)S(1)}, bf16[1,128,512]{2,1,0:T(8,128)(2,1)S(1)}, u32[]{:S(2)}, u32[]{:S(2)}) collective-permute-start(bf16[1,128,512]{2,1,0:T(8,128)(2,1)S(1)} %add_convert_fusion.4), channel_id=1, source_target_pairs={{0,96},{8,104},{16,112},{24,120},{32,0},{40,8},{48,16},{56,24},{64... | collective-permute-start | bytes 393224 | tf_op jit(solution)/shard_map/ppermute | solution.py:365
  168.2 4.1 %collective-permute-start.9 = (bf16[1,128,512]{2,1,0:T(8,128)(2,1)S(1)}, bf16[1,128,512]{2,1,0:T(8,128)(2,1)S(1)}, u32[]{:S(2)}, u32[]{:S(2)}) collective-permute-start(bf16[1,128,512]{2,1,0:T(8,128)(2,1)S(1)} %add_convert_fusion.6), channel_id=1, source_target_pairs={{0,24},{8,0},{16,8},{24,16},{32,56},{40,32},{48,40},{56,48},{64,88... | collective-permute-start | bytes 393224 | tf_op jit(solution)/shard_map/ppermute | solution.py:365
  172.4 5.4 %collective-permute-start.17 = (bf16[1,128,512]{2,1,0:T(8,128)(2,1)S(1)}, bf16[1,128,512]{2,1,0:T(8,128)(2,1)S(1)}, u32[]{:S(2)}, u32[]{:S(2)}) collective-permute-start(bf16[1,128,512]{2,1,0:T(8,128)(2,1)S(1)} %get-tuple-element.63), channel_id=1, source_target_pairs={{0,32},{8,40},{16,48},{24,56},{32,64},{40,72},{48,80},{56,88},{64,... | collective-permute-start | bytes 393224 | tf_op jit(solution)/shard_map/ppermute | solution.py:365
  177.8 5.7 %collective-permute-start.7 = (bf16[1,128,512]{2,1,0:T(8,128)(2,1)S(1)}, bf16[1,128,512]{2,1,0:T(8,128)(2,1)S(1)}, u32[]{:S(2)}, u32[]{:S(2)}) collective-permute-start(bf16[1,128,512]{2,1,0:T(8,128)(2,1)S(1)} %get-tuple-element.65), channel_id=1, source_target_pairs={{0,8},{8,16},{16,24},{24,0},{32,40},{40,48},{48,56},{56,32},{64,72... | collective-permute-start | bytes 393224 | tf_op jit(solution)/shard_map/ppermute | solution.py:365
